TPU v7x, 32 devices: a whole 2x2x4 slice. The times are simulated.
32 devices in a mesh: rep: 4 (over z), seq: 8 (over y, x, core).
Axes of the slice: x: 2, y: 2, z: 4, core: 2. Of those that a mesh axis runs over, the one named last changes fastest.
Arguments:
- frames_in: bfloat16 [4, 8, 4, 128, 1152], P('rep', 'seq'), may hold values from -6 to 6
- conditioning: float32 [4, 1152], P('rep'), may hold values from -6 to 6
- mod_first: bfloat16 [1152, 6912], P('seq'), may hold values from -0.1875 to 0.1875
- qkv_first: bfloat16 [1152, 3456], P('seq'), may hold values from -0.1875 to 0.1875
- out_first: bfloat16 [1152, 1152], P('seq'), may hold values from -0.75 to 0.75
- up_first: bfloat16 [1152, 4608], P('seq'), may hold values from -0.1875 to 0.1875
- down_first: bfloat16 [4608, 1152], P('seq'), may hold values from -0.09375 to 0.09375
- mod_second: bfloat16 [1152, 6912], P('seq'), may hold values from -0.1875 to 0.1875
- qkv_second: bfloat16 [1152, 3456], P('seq'), may hold values from -0.1875 to 0.1875
- out_second: bfloat16 [1152, 1152], P('seq'), may hold values from -0.375 to 0.375
- up_second: bfloat16 [1152, 4608], P('seq'), may hold values from -0.1875 to 0.1875
- down_second: bfloat16 [4608, 1152], P('seq'), may hold values from -0.09375 to 0.09375
- cotangent: float32 [4, 8, 4, 128, 1152], P('rep', 'seq'), may hold values from -6 to 6
Outputs:
- block_out: float32 [4, 8, 4, 128, 1152], P('rep', 'seq')
- input_grad: float32 [4, 8, 4, 128, 1152], P('rep', 'seq')
- conditioning_grad: float32 [4, 1152], P('rep', 'seq')
- mod_first_grad: float32 [1152, 6912], P('seq')
- qkv_first_grad: float32 [1152, 3456], P('seq')
- out_first_grad: float32 [1152, 1152], P('seq')
- up_first_grad: float32 [1152, 4608], P('seq')
- first_down_gradient: float32 [4608, 1152], P('seq')
- mod_second_grad: float32 [1152, 6912], P('seq')
- qkv_second_grad: float32 [1152, 3456], P('seq')
- out_second_grad: float32 [1152, 1152], P('seq')
- up_second_grad: float32 [1152, 4608], P('seq')
- down_second_grad: float32 [4608, 1152], P('seq')
All inputs are finite; a program needn't handle non-finite values.
Results may differ from a plain program's by a relative error of at most 0.02175.
Values may be sent and summed in bfloat16 or wider, within the bound.
A program may use at most 384 MiB of HBM per device.

v0:
```python
import jax
import jax.numpy as jnp
from jax import lax
from jax.sharding import PartitionSpec as P

HEADS = 16
HEAD_WIDTH = 72


norm_epsilon = 1e-06


def from_partner(block, axis, apart):
    count = lax.axis_size(axis)
    route = []
    for low in range(count):
        high = low | 1 << apart
        if high != low and high < count:
            route += [(low, high), (high, low)]
    return lax.ppermute(block, axis, route)


def shortened(x):
    return jax.tree.map(lambda a: a.astype(jnp.bfloat16) if a.dtype == jnp.float32 else a, x)


def layer_mod(stream, shift_part, scale_part):
    row_mean = jnp.mean(stream, axis=-1, keepdims=True)
    centred = stream - row_mean
    row_var = jnp.mean(centred * centred, axis=-1, keepdims=True)
    return centred * lax.rsqrt(row_var + norm_epsilon) * (1.0 + scale_part) + shift_part


def gelu_tanh(pre_value):
    return jax.nn.gelu(pre_value, approximate=True)


def project(left_operand, right_operand):
    return jnp.einsum(
        "csld,de->csle", left_operand, right_operand, preferred_element_type=jnp.float32
    )


def project_back(incoming, right_operand):
    return jnp.einsum("csle,de->csld", incoming, right_operand, preferred_element_type=jnp.float32)


def mod_parts(modulation):
    return [segment[:, None, None, :] for segment in jnp.split(modulation, 6, axis=-1)]


def modulations(conditioning, mod_one, mod_two):
    row_count = mod_one.shape[0]
    row_start = lax.axis_index("seq") * row_count
    silu_local = lax.dynamic_slice_in_dim(
        jax.nn.silu(conditioning), row_start, row_count, 1
    ).astype(jnp.bfloat16)
    part_one = jnp.dot(silu_local, mod_one, preferred_element_type=jnp.float32)
    part_two = jnp.dot(silu_local, mod_two, preferred_element_type=jnp.float32)
    summed = lax.psum((part_one, part_two), "seq")
    return (summed[0], summed[1], silu_local, row_start)


def gather_layer(qkv_w, out_w, up_w, down_w):
    return (
        lax.all_gather(qkv_w, "seq", axis=0, tiled=True),
        lax.all_gather(out_w, "seq", axis=0, tiled=True),
        lax.all_gather(up_w, "seq", axis=0, tiled=True),
        lax.all_gather(down_w, "seq", axis=0, tiled=True),
    )


def gather_layer_again(qkv_w, out_w, up_w, down_w):
    return (
        lax.all_gather(qkv_w, "seq", axis=0, tiled=True),
        lax.all_gather(out_w, "seq", axis=0, tiled=True),
        lax.all_gather(up_w, "seq", axis=0, tiled=True),
        lax.all_gather(down_w, "seq", axis=0, tiled=True),
    )


def partner_values(stacked):
    return from_partner(stacked, "seq", 0)


def partner_grads(stacked):
    return from_partner(stacked.astype(jnp.bfloat16), "seq", 0).astype(stacked.dtype)


def to_places(stream):
    clip_count, frame_dev, half_places, features = stream.shape
    devices = lax.axis_size("seq")
    place_part = half_places // devices
    exchanged = lax.all_to_all(
        stream.reshape(1, clip_count, frame_dev, devices, place_part, features).astype(
            jnp.bfloat16
        ),
        "seq",
        split_axis=3,
        concat_axis=0,
        tiled=True,
    ).astype(jnp.float32)
    exchanged = exchanged.reshape(devices // 2, 2, clip_count, frame_dev, place_part, features)
    exchanged = jnp.transpose(exchanged, (2, 1, 4, 0, 3, 5))
    return exchanged.reshape(clip_count, 2 * place_part, devices // 2 * frame_dev, features)


def to_frames(stream, frame_dev):
    clip_count, place_count, frame_total, features = stream.shape
    devices = lax.axis_size("seq")
    place_part = place_count // 2
    arranged = stream.reshape(clip_count, 2, place_part, devices // 2, frame_dev, features)
    arranged = jnp.transpose(arranged, (3, 1, 0, 4, 2, 5)).reshape(
        devices, clip_count, frame_dev, 1, place_part, features
    )
    exchanged = lax.all_to_all(
        shortened(arranged), "seq", split_axis=0, concat_axis=3, tiled=True
    ).astype(arranged.dtype)
    return exchanged.reshape(clip_count, frame_dev, devices * place_part, features)


def forward_layer(stream, modulation, weights, spatial):
    qkv_w, out_w, up_w, down_w = weights
    shift_attn, scale_attn, gate_attn, shift_mlp, scale_mlp, gate_mlp = mod_parts(modulation)
    clip_count, seq_count, seq_len, features = stream.shape
    normed = layer_mod(stream, shift_attn, scale_attn).astype(jnp.bfloat16)
    projected = project(normed, qkv_w).astype(jnp.bfloat16)
    queries, keys_all, values_all = jnp.split(projected, 3, axis=-1)
    if spatial:
        remote = partner_values(jnp.stack([keys_all, values_all]))
        keys_all = jnp.concatenate([keys_all, remote[0]], axis=2)
        values_all = jnp.concatenate([values_all, remote[1]], axis=2)
    key_len = keys_all.shape[2]
    queries = queries.reshape(clip_count, seq_count, seq_len, HEADS, HEAD_WIDTH)
    keys_all = keys_all.reshape(clip_count, seq_count, key_len, HEADS, HEAD_WIDTH)
    values_all = values_all.reshape(clip_count, seq_count, key_len, HEADS, HEAD_WIDTH)
    scores = jnp.einsum(
        "cslhe,csmhe->cshlm", queries, keys_all, preferred_element_type=jnp.float32
    ) * HEAD_WIDTH ** (-0.5)
    peak_score = jnp.max(scores, axis=-1, keepdims=True)
    scaled_exp = jnp.exp(scores - peak_score)
    attention = scaled_exp / jnp.sum(scaled_exp, axis=-1, keepdims=True)
    attention_low = attention.astype(jnp.bfloat16)
    attended = jnp.einsum(
        "cshlm,csmhe->cslhe", attention_low, values_all, preferred_element_type=jnp.float32
    )
    attended = attended.astype(jnp.bfloat16).reshape(clip_count, seq_count, seq_len, features)
    branch = project(attended, out_w)
    middle = stream + gate_attn * branch
    normed_mid = layer_mod(middle, shift_mlp, scale_mlp).astype(jnp.bfloat16)
    hidden_pre = project(normed_mid, up_w)
    hidden = gelu_tanh(hidden_pre).astype(jnp.bfloat16)
    mlp_out = project(hidden, down_w)
    result = middle + gate_mlp * mlp_out
    kept_state = (
        normed,
        queries,
        keys_all,
        values_all,
        attention,
        attention_low,
        attended,
        branch,
        middle,
        normed_mid,
        hidden_pre,
        hidden,
        mlp_out,
    )
    return (result, kept_state)


def backward_layer(result_grad, stream, modulation, weights, kept_state, spatial):
    qkv_w, out_w, up_w, down_w = weights
    (
        normed,
        queries,
        keys_all,
        values_all,
        attention,
        attention_low,
        attended,
        branch,
        middle,
        normed_mid,
        hidden_pre,
        hidden,
        mlp_out,
    ) = kept_state
    shift_attn, scale_attn, gate_attn, shift_mlp, scale_mlp, gate_mlp = mod_parts(modulation)
    clip_count, seq_count, seq_len, features = stream.shape
    gate_mlp_grad = jnp.sum(result_grad * mlp_out, axis=(1, 2))
    mlp_grad = (gate_mlp * result_grad).astype(jnp.bfloat16)
    hidden_grad = project_back(mlp_grad, down_w)
    pre_grad = jax.vjp(gelu_tanh, hidden_pre)[1](hidden_grad)[0].astype(jnp.bfloat16)
    normed_mid_grad = project_back(pre_grad, up_w)
    middle_ln_grad, shift_mlp_grad, scale_mlp_grad = jax.vjp(
        layer_mod, middle, shift_mlp, scale_mlp
    )[1](normed_mid_grad)
    middle_grad = result_grad + middle_ln_grad
    gate_attn_grad = jnp.sum(middle_grad * branch, axis=(1, 2))
    branch_grad = (gate_attn * middle_grad).astype(jnp.bfloat16)
    attended_grad = project_back(branch_grad, out_w).astype(jnp.bfloat16)
    attended_grad = attended_grad.reshape(clip_count, seq_count, seq_len, HEADS, HEAD_WIDTH)
    attention_grad = jnp.einsum(
        "cslhe,csmhe->cshlm", attended_grad, values_all, preferred_element_type=jnp.float32
    )
    scores_grad = attention * (
        attention_grad - jnp.sum(attention_grad * attention, axis=-1, keepdims=True)
    )
    scores_grad = scores_grad.astype(jnp.bfloat16)
    inv_root = HEAD_WIDTH ** (-0.5)
    queries_grad = (
        jnp.einsum("cshlm,csmhe->cslhe", scores_grad, keys_all, preferred_element_type=jnp.float32)
        * inv_root
    )
    keys_grad = (
        jnp.einsum("cshlm,cslhe->csmhe", scores_grad, queries, preferred_element_type=jnp.float32)
        * inv_root
    )
    values_grad = jnp.einsum(
        "cshlm,cslhe->csmhe", attention_low, attended_grad, preferred_element_type=jnp.float32
    )
    if spatial:
        returned = partner_grads(
            jnp.stack([keys_grad[:, :, seq_len:], values_grad[:, :, seq_len:]])
        )
        keys_grad = keys_grad[:, :, :seq_len] + returned[0]
        values_grad = values_grad[:, :, :seq_len] + returned[1]
    qkv_grad = jnp.concatenate(
        [
            component.reshape(clip_count, seq_count, seq_len, features)
            for component in (queries_grad, keys_grad, values_grad)
        ],
        axis=-1,
    )
    qkv_grad = qkv_grad.astype(jnp.bfloat16)
    normed_grad = project_back(qkv_grad, qkv_w)
    stream_ln_grad, attention_shift_gradient, scale_attn_grad = jax.vjp(
        layer_mod, stream, shift_attn, scale_attn
    )[1](normed_grad)
    stream_grad = middle_grad + stream_ln_grad
    mod_grad = jnp.concatenate(
        [
            attention_shift_gradient.reshape(clip_count, features),
            scale_attn_grad.reshape(clip_count, features),
            gate_attn_grad,
            shift_mlp_grad.reshape(clip_count, features),
            scale_mlp_grad.reshape(clip_count, features),
            gate_mlp_grad,
        ],
        axis=-1,
    )
    grad_pairs = (
        (normed, qkv_grad),
        (attended, branch_grad),
        (normed_mid, pre_grad),
        (hidden, mlp_grad),
    )
    return (stream_grad, mod_grad, grad_pairs)


def spread_rows_out(left_operand, right_operand):
    left_flat = left_operand.reshape(-1, left_operand.shape[-1])
    right_flat = right_operand.reshape(-1, right_operand.shape[-1])
    return lax.psum_scatter(
        jnp.einsum("nd,ne->de", left_flat, right_flat, preferred_element_type=jnp.float32).astype(
            jnp.bfloat16
        ),
        "seq",
        scatter_dimension=0,
        tiled=True,
    ).astype(jnp.float32)


def layer_grads(grad_pairs):
    return tuple(
        (spread_rows_out(grad_pairs[index][0], grad_pairs[index][1]) for index in range(4))
    )


def per_device(
    frames_in,
    conditioning,
    mod_first,
    qkv_first,
    out_first,
    up_first,
    down_first,
    mod_second,
    qkv_second,
    out_second,
    up_second,
    down_second,
    cotangent,
):
    clip_count = frames_in.shape[0]
    frame_dev = frames_in.shape[2]
    half_places = frames_in.shape[3]
    features = frames_in.shape[4]
    start_stream = frames_in.reshape(clip_count, frame_dev, half_places, features).astype(
        jnp.float32
    )
    mod_one, mod_two, silu_local, row_start = modulations(conditioning, mod_first, mod_second)
    weights_one = gather_layer(qkv_first, out_first, up_first, down_first)
    spatial_out, unused_one = forward_layer(start_stream, mod_one, weights_one, True)
    weights_two = gather_layer(qkv_second, out_second, up_second, down_second)
    temporal_out, unused_two = forward_layer(to_places(spatial_out), mod_two, weights_two, False)
    block_out = to_frames(temporal_out, frame_dev)
    mod_one, mod_two, silu_local, row_start = modulations(conditioning, mod_first, mod_second)
    again_one = gather_layer_again(qkv_first, out_first, up_first, down_first)
    spatial_again, state_one = forward_layer(start_stream, mod_one, again_one, True)
    again_two = gather_layer_again(qkv_second, out_second, up_second, down_second)
    placed_again = to_places(spatial_again)
    unused_three, state_two = forward_layer(placed_again, mod_two, again_two, False)
    cotangent_sites = to_places(cotangent.reshape(clip_count, frame_dev, half_places, features))
    placed_grad, mod_grad_two, pairs_two = backward_layer(
        cotangent_sites, placed_again, mod_two, again_two, state_two, False
    )
    row_attn = qkv_first.shape[0]
    grads_two = layer_grads(pairs_two)
    spatial_grad = to_frames(placed_grad, frame_dev)
    stream_grad, mod_grad_one, pairs_one = backward_layer(
        spatial_grad, start_stream, mod_one, again_one, state_one, True
    )
    grads_one = layer_grads(pairs_one)
    mod_totals = (
        lax.psum(mod_grad_one.astype(jnp.bfloat16), "seq").astype(jnp.float32),
        lax.psum(mod_grad_two.astype(jnp.bfloat16), "seq").astype(jnp.float32),
    )
    low_one = mod_totals[0].astype(jnp.bfloat16)
    low_two = mod_totals[1].astype(jnp.bfloat16)
    mod_weight_one = jnp.einsum(
        "cd,ce->de", silu_local, low_one, preferred_element_type=jnp.float32
    )
    mod_weight_two = jnp.einsum(
        "cd,ce->de", silu_local, low_two, preferred_element_type=jnp.float32
    )
    silu_grad = jnp.einsum("ce,de->cd", low_one, mod_first, preferred_element_type=jnp.float32)
    silu_grad = silu_grad + jnp.einsum(
        "ce,de->cd", low_two, mod_second, preferred_element_type=jnp.float32
    )
    condition_local = lax.dynamic_slice_in_dim(conditioning, row_start, row_attn, 1)
    condition_grad = jax.vjp(jax.nn.silu, condition_local)[1](silu_grad)[0]
    summed = (
        lax.psum(mod_weight_one.astype(jnp.bfloat16), "rep").astype(jnp.float32),
        lax.psum(grads_one[0].astype(jnp.bfloat16), "rep").astype(jnp.float32),
        lax.psum(grads_one[1].astype(jnp.bfloat16), "rep").astype(jnp.float32),
        lax.psum(grads_one[2].astype(jnp.bfloat16), "rep").astype(jnp.float32),
        lax.psum(grads_one[3].astype(jnp.bfloat16), "rep").astype(jnp.float32),
        lax.psum(mod_weight_two.astype(jnp.bfloat16), "rep").astype(jnp.float32),
        lax.psum(grads_two[0].astype(jnp.bfloat16), "rep").astype(jnp.float32),
        lax.psum(grads_two[1].astype(jnp.bfloat16), "rep").astype(jnp.float32),
        lax.psum(grads_two[2].astype(jnp.bfloat16), "rep").astype(jnp.float32),
        lax.psum(grads_two[3].astype(jnp.bfloat16), "rep").astype(jnp.float32),
    )
    out_shape = (clip_count, 1, frame_dev, half_places, features)
    return (
        block_out.reshape(out_shape),
        stream_grad.reshape(out_shape),
        condition_grad,
        summed[0],
        summed[1],
        summed[2],
        summed[3],
        summed[4],
        summed[5],
        summed[6],
        summed[7],
        summed[8],
        summed[9],
    )


def solution(mesh):
    return jax.shard_map(
        per_device,
        mesh=mesh,
        in_specs=(
            P("rep", "seq", None, None, None),
            P("rep", None),
            P("seq", None),
            P("seq", None),
            P("seq", None),
            P("seq", None),
            P("seq", None),
            P("seq", None),
            P("seq", None),
            P("seq", None),
            P("seq", None),
            P("seq", None),
            P("rep", "seq", None, None, None),
        ),
        out_specs=(
            P("rep", "seq", None, None, None),
            P("rep", "seq", None, None, None),
            P("rep", "seq"),
            P("seq", None),
            P("seq", None),
            P("seq", None),
            P("seq", None),
            P("seq", None),
            P("seq", None),
            P("seq", None),
            P("seq", None),
            P("seq", None),
            P("seq", None),
        ),
        check_vma=False,
    )
```

profile of v0, /device:TPU:0, one launch (start us, length us, event | category | flops | bytes accessed | tf_op | source)
XLA Modules:
  0.0 1630.0 jit_solution(10004412810075176240)
XLA Ops:
  17.6 26.8 %all-reduce = (f32[1,6912]{1,0:T(1,128)S(1)}, f32[1,6912]{1,0:T(1,128)S(1)}) all-reduce(f32[1,6912]{1,0:T(1,128)S(1)} %fusion.149, f32[1,6912]{1,0:T(1,128)S(1)} %fusion.147), channel_id=1, replica_groups=mesh['rep'=4,'seq'=8] {'seq'}, use_global_device_ids=true, to_apply=%region_0.1 | all-reduce | flops 13824 | bytes 110592 | tf_op jit(solution)/shard_map/psum | solution.py:60
  44.6 21.0 %all-gather.9.cloned.1.call-done = bf16[1152,3456]{1,0:T(8,128)(2,1)} async-done(((bf16[144,3456]{1,0:T(8,128)(2,1)}), bf16[1152,3456]{1,0:T(8,128)(2,1)}) %all-gather.9.cloned.1.call-update) | async-done | bytes 7962640 | tf_op jit(solution)/shard_map/all_gather | solution.py:66
  65.6 8.8 fusion.60
  80.2 4.8 all-to-all-start.2
  103.4 4.9 fusion.178
  109.3 22.1 %fusion.119 = bf16[4,16,72,128]{3,2,1,0:T(8,128)(2,1)} fusion(bf16[1,4,128,16,72]{2,4,3,1,0:T(8,128)(2,1)} %bitcast.356, bf16[1,4,128,16,72]{2,4,3,1,0:T(8,128)(2,1)} %bitcast.354, f32[4,16,128]{2,1,0:T(8,128)S(1)} %get-tuple-element.81, f32[4,16,128,256]{3,2,1,0:T(8,128)} %copy-done.5), kind=kOutput, calls=%fused_computation.180 | convolution fusion | flops 317792512 | bytes 11960320 | tf_op jit(solution)/shard_map/cshlm,csmhe->cslhe/dot_general | solution.py:144
  131.3 5.5 fusion.173
  138.7 36.6 %all-gather.13.cloned.1.call-done = bf16[1152,4608]{1,0:T(8,128)(2,1)} async-done(((bf16[144,4608]{1,0:T(8,128)(2,1)}), bf16[1152,4608]{1,0:T(8,128)(2,1)}) %all-gather.13.cloned.1.call-update) | async-done | bytes 10616848 | tf_op jit(solution)/shard_map/all_gather | solution.py:68
  175.2 12.4 fusion.22
  187.7 53.2 %all-gather.15.cloned.1.call-done = bf16[4608,1152]{1,0:T(8,128)(2,1)} async-done(((bf16[576,1152]{1,0:T(8,128)(2,1)}), bf16[4608,1152]{1,0:T(8,128)(2,1)}) %all-gather.15.cloned.1.call-update) | async-done | bytes 10616848 | tf_op jit(solution)/shard_map/all_gather | solution.py:69
  240.8 13.8 add_convert_fusion.4
  268.3 9.0 all-to-all-done
  291.1 9.5 all-gather.17.cloned.1.call-done
  300.6 9.0 fusion.57
  311.3 5.7 reshape.1276
  317.0 5.8 reshape.1277
  322.7 4.8 reshape.1275
  331.1 16.3 %fusion.179 = (f32[32,16,16]{2,1,0:T(8,128)S(1)}, f32[32,16,16,16]{2,3,1,0:T(8,128)S(1)}) fusion(f32[32,16,16,16]{2,3,1,0:T(8,128)S(1)} %fusion.109), kind=kOutput, calls=%fused_computation.279 | output fusion | flops 524303 | bytes 1081344 | tf_op jit(solution)/shard_map/sub | solution.py:141
  355.1 6.6 fusion.172
  364.0 34.0 %all-gather.21.cloned.1.call-done = bf16[1152,4608]{1,0:T(8,128)(2,1)} async-done(((bf16[144,4608]{1,0:T(8,128)(2,1)}), bf16[1152,4608]{1,0:T(8,128)(2,1)}) %all-gather.21.cloned.1.call-update) | async-done | bytes 10616848 | tf_op jit(solution)/shard_map/all_gather | solution.py:68
  398.1 13.2 fusion.14
  411.2 52.5 %all-gather.23.cloned.1.call-done = bf16[4608,1152]{1,0:T(8,128)(2,1)} async-done(((bf16[576,1152]{1,0:T(8,128)(2,1)}), bf16[4608,1152]{1,0:T(8,128)(2,1)}) %all-gather.23.cloned.1.call-update) | async-done | bytes 10616848 | tf_op jit(solution)/shard_map/all_gather | solution.py:69
  463.8 15.9 fusion.37
  479.8 13.5 multiply_reduce_fusion.13
  497.6 18.1 %multiply_reduce_fusion.4 = (bf16[1152]{0:T(1024)(128)(2,1)}, bf16[32,16,1152]{2,1,0:T(8,128)(2,1)}, bf16[1152]{0:T(1024)(128)(2,1)}, f32[32,16,1152]{2,1,0:T(8,128)S(1)}) fusion(f32[32,16,1152]{2,1,0:T(8,128)} %reshape.1279, f32[32,16,1152]{2,1,0:T(8,128)} %get-tuple-element.59, f32[1152]{0:T(1024)S(1)} %get-tuple-element.25, ...), kind=kOutput, calls=%fused_computation.133 | convolution fusion | flops 5465896960 | bytes 33052160 | tf_op jit(solution)/shard_map/csld,de->csle/dot_general | solution.py:39
  563.3 10.9 multiply_reduce_fusion.12
  597.5 4.9 convolution_convert_fusion
  606.7 17.4 %fusion.30 = bf16[4,128,4608]{2,1,0:T(8,128)(2,1)} fusion(f32[4,128,4608]{2,1,0:T(8,128)} %fusion.22, bf16[4608,1152]{1,0:T(8,128)(2,1)} %all-gather.15.cloned.1.call-done, f32[4,128,1152]{2,1,0:T(8,128)S(1)} %bitcast.337, f32[1152]{0:T(1024)S(1)} %copy-done.64), kind=kOutput, calls=%fused_computation.40 | convolution fusion | flops 5484183552 | bytes 27136512 | tf_op jit(solution)/shard_map/csle,de->csld/dot_general | solution.py:45
  624.2 11.9 multiply_reduce_fusion.11
  646.5 10.6 fusion.7
  657.2 4.7 convolution_convert_fusion.2
  664.5 22.2 %convolution_bitcast_fusion.6 = f32[1,4,256,16,72]{2,4,3,1,0:T(8,128)} fusion(bf16[4,128,16,72]{1,3,2,0:T(8,128)(2,1)} %bitcast.360, f32[4,16,128]{2,1,0:T(8,128)S(1)} %copy-done.54, f32[4,16,128,256]{3,2,1,0:T(8,128)} %copy-done.5), kind=kOutput, calls=%fused_computation.161 | convolution fusion | flops 312484096 | bytes 14319616 | tf_op jit(solution)/shard_map/cshlm,cslhe->csmhe/dot_general | solution.py:221
  686.7 7.5 multiply_reduce_fusion
  710.5 5.3 fusion.92
  721.2 9.8 fusion.6
  732.3 12.9 fusion.3
  746.0 11.1 fusion.2
  758.6 12.1 fusion.5
  771.5 11.5 fusion.4
  784.3 10.9 fusion.85
  798.0 23.5 %all-reduce.1 = (bf16[6912]{0:T(1024)(128)(2,1)S(1)}, bf16[6912]{0:T(1024)(128)(2,1)S(1)}) all-reduce(bf16[6912]{0:T(1024)(128)(2,1)S(1)} %reduce.79, bf16[6912]{0:T(1024)(128)(2,1)S(1)} %reduce.80), channel_id=1, replica_groups=mesh['rep'=4,'seq'=8] {'seq'}, use_global_device_ids=true, to_apply=%region_30.31 | all-reduce | flops 13824 | bytes 55296 | tf_op jit(solution)/shard_map/psum | solution.py:328
  824.0 20.3 %reduce-scatter.9.cloned.1.call-done = bf16[144,3456]{1,0:T(8,128)(2,1)} async-done(((bf16[1152,3456]{1,0:T(8,128)(2,1)}), bf16[144,3456]{1,0:T(8,128)(2,1)}) %reduce-scatter.9.cloned.1.call-update) | async-done | bytes 995344 | tf_op jit(solution)/shard_map/reduce_scatter | solution.py:266
  844.3 85.7 %reduce-scatter.23.cloned.1.call-done = bf16[576,1152]{1,0:T(8,128)(2,1)} async-done(((bf16[4608,1152]{1,0:T(8,128)(2,1)}), bf16[576,1152]{1,0:T(8,128)(2,1)}) %reduce-scatter.23.cloned.1.call-update) | async-done | bytes 1327120 | tf_op jit(solution)/shard_map/reduce_scatter | solution.py:266
  930.0 85.6 %reduce-scatter.21.cloned.1.call-done = bf16[144,4608]{1,0:T(8,128)(2,1)} async-done(((bf16[1152,4608]{1,0:T(8,128)(2,1)}), bf16[144,4608]{1,0:T(8,128)(2,1)}) %reduce-scatter.21.cloned.1.call-update) | async-done | bytes 1327120 | tf_op jit(solution)/shard_map/reduce_scatter | solution.py:266
  1015.6 85.6 %reduce-scatter.15.cloned.1.call-done = bf16[576,1152]{1,0:T(8,128)(2,1)} async-done(((bf16[4608,1152]{1,0:T(8,128)(2,1)}), bf16[576,1152]{1,0:T(8,128)(2,1)}) %reduce-scatter.15.cloned.1.call-update) | async-done | bytes 1327120 | tf_op jit(solution)/shard_map/reduce_scatter | solution.py:266
  1101.2 85.6 %reduce-scatter.13.cloned.1.call-done = bf16[144,4608]{1,0:T(8,128)(2,1)} async-done(((bf16[1152,4608]{1,0:T(8,128)(2,1)}), bf16[144,4608]{1,0:T(8,128)(2,1)}) %reduce-scatter.13.cloned.1.call-update) | async-done | bytes 1327120 | tf_op jit(solution)/shard_map/reduce_scatter | solution.py:266
  1191.5 19.3 %all_to_all.16 = bf16[8,1,4,1,16,1152]{5,4,2,3,1,0:T(8,128)(2,1)S(1)} all-to-all(bf16[8,1,4,1,16,1152]{5,4,2,3,1,0:T(8,128)(2,1)S(1)} %bitcast.348), channel_id=1, replica_groups=mesh['rep'=4,'seq'=8] {'seq'}, dimensions={0} | all-to-all | bytes 2359296 | tf_op jit(solution)/shard_map/all_to_all | solution.py:116
  1217.4 386.7 %all-reduce.5.cloned.1.call-done = (bf16[144,6912]{1,0:T(8,128)(2,1)}, bf16[144,3456]{1,0:T(8,128)(2,1)}, bf16[144,1152]{1,0:T(8,128)(2,1)}, bf16[144,4608]{1,0:...) async-done(((bf16[144,6912]{1,0:T(8,128)(2,1)}, ...) | async-done | bytes 11943952 | tf_op jit(solution)/shard_map/psum | solution.py:346
  (419 shorter events, 234.6 us)
Async XLA Ops:
  7.2 58.4 %all-gather.9.cloned.1.call-start = ((), (), s32[]{:S(2)}) async-start(), calls=%async_computation.12 | async-start | bytes 8957952 | tf_op jit(solution)/shard_map/all_gather | solution.py:66
  7.9 123.4 %all-gather.11.cloned.1.call-start = ((), (), s32[]{:S(2)}) async-start(), calls=%async_computation.13 | async-start | bytes 2985984 | tf_op jit(solution)/shard_map/all_gather | solution.py:67
  8.7 166.6 %all-gather.13.cloned.1.call-start = ((), (), s32[]{:S(2)}) async-start(), calls=%async_computation.14 | async-start | bytes 11943936 | tf_op jit(solution)/shard_map/all_gather | solution.py:68
  9.4 231.4 %all-gather.15.cloned.1.call-start = ((), (), s32[]{:S(2)}) async-start(), calls=%async_computation.15 | async-start | bytes 11943936 | tf_op jit(solution)/shard_map/all_gather | solution.py:69
  10.0 290.6 %all-gather.17.cloned.1.call-start = ((), (), s32[]{:S(2)}) async-start(), calls=%async_computation.16 | async-start | bytes 8957952 | tf_op jit(solution)/shard_map/all_gather | solution.py:66
  10.6 344.5 %all-gather.19.cloned.1.call-start = ((), (), s32[]{:S(2)}) async-start(), calls=%async_computation.17 | async-start | bytes 2985984 | tf_op jit(solution)/shard_map/all_gather | solution.py:67
  11.2 386.9 %all-gather.21.cloned.1.call-start = ((), (), s32[]{:S(2)}) async-start(), calls=%async_computation.18 | async-start | bytes 11943936 | tf_op jit(solution)/shard_map/all_gather | solution.py:68
  11.9 451.9 %all-gather.23.cloned.1.call-start = ((), (), s32[]{:S(2)}) async-start(), calls=%async_computation.19 | async-start | bytes 11943936 | tf_op jit(solution)/shard_map/all_gather | solution.py:69
  12.9 52.7 %copy-start.70 = (f32[4,128]{1,0:T(4,128)}, f32[4,128]{1,0:T(4,128)S(1)}, u32[]{:S(2)}) copy-start(f32[4,128]{1,0:T(4,128)S(1)} %broadcast_multiply_fusion.3) | copy-start | bytes 6148
  13.4 61.0 %copy-start.80 = (f32[4,128]{1,0:T(4,128)}, f32[4,128]{1,0:T(4,128)S(1)}, u32[]{:S(2)}) copy-start(f32[4,128]{1,0:T(4,128)S(1)} %fusion.143) | copy-start | bytes 6148
  44.5 29.9 %copy-start.58 = (f32[1152]{0:T(1024)}, f32[1152]{0:T(1024)S(1)}, u32[]{:S(2)}) copy-start(f32[1152]{0:T(1024)S(1)} %get-tuple-element.35) | copy-start | bytes 13828
  44.5 29.9 %copy-start.96 = (f32[1152]{0:T(1024)}, f32[1152]{0:T(1024)S(1)}, u32[]{:S(2)}) copy-start(f32[1152]{0:T(1024)S(1)} %get-tuple-element.34) | copy-start | bytes 13828
  44.6 86.8 %copy-start.49 = (f32[1152]{0:T(1024)}, f32[1152]{0:T(1024)S(1)}, u32[]{:S(2)}) copy-start(f32[1152]{0:T(1024)S(1)} %get-tuple-element.36) | copy-start | bytes 13828
  44.6 130.7 %copy-start.55 = (f32[1152]{0:T(1024)}, f32[1152]{0:T(1024)S(1)}, u32[]{:S(2)}) copy-start(f32[1152]{0:T(1024)S(1)} %get-tuple-element.33) | copy-start | bytes 13828
  44.6 130.7 %copy-start.94 = (f32[1152]{0:T(1024)}, f32[1152]{0:T(1024)S(1)}, u32[]{:S(2)}) copy-start(f32[1152]{0:T(1024)S(1)} %get-tuple-element.32) | copy-start | bytes 13828
  44.6 196.2 %copy-start.63 = (f32[1152]{0:T(1024)}, f32[1152]{0:T(1024)S(1)}, u32[]{:S(2)}) copy-start(f32[1152]{0:T(1024)S(1)} %get-tuple-element.31) | copy-start | bytes 13828
  78.1 14.1 collective-permute-start
  80.2 175.6 %all-to-all-start.2 = ((bf16[1,1,4,8,16,1152]{5,4,2,1,0,3:T(8,128)(2,1)}), bf16[1,1,4,8,16,1152]{5,4,2,1,0,3:T(8,128)(2,1)}, u32[]{:S(2)}, u32[]{:S(2)}) async-start(bf16[1,1,4,8,16,1152]{5,4,2,1,0,3:T(8,128)(2,1)} %copy.281), calls=%async_computation.2 | async-start | bytes 2359296 | tf_op jit(solution)/shard_map/all_to_all | solution.py:94
  109.3 22.1 %copy-start.53 = (f32[4,16,128]{2,1,0:T(8,128)}, f32[4,16,128]{2,1,0:T(8,128)S(1)}, u32[]{:S(2)}) copy-start(f32[4,16,128]{2,1,0:T(8,128)S(1)} %get-tuple-element.81) | copy-start | bytes 98308
  136.9 50.8 %copy-start.73 = (f32[4,128]{1,0:T(4,128)}, f32[4,128]{1,0:T(4,128)S(1)}, u32[]{:S(2)}) copy-start(f32[4,128]{1,0:T(4,128)S(1)} %broadcast_multiply_fusion.2) | copy-start | bytes 6148
  138.6 49.0 %copy-start.78 = (f32[4,128]{1,0:T(4,128)}, f32[4,128]{1,0:T(4,128)S(1)}, u32[]{:S(2)}) copy-start(f32[4,128]{1,0:T(4,128)S(1)} %multiply_reduce_fusion.16) | copy-start | bytes 6148
  138.7 49.0 %copy-start.83 = (f32[4,128]{1,0:T(4,128)}, f32[4,128]{1,0:T(4,128)S(1)}, u32[]{:S(2)}) copy-start(f32[4,128]{1,0:T(4,128)S(1)} %fusion.144) | copy-start | bytes 6148
  255.8 21.5 %all-to-all-start = ((bf16[1,1,4,8,16,1152]{5,4,2,1,0,3:T(8,128)(2,1)}), bf16[1,1,4,8,16,1152]{5,4,2,1,0,3:T(8,128)(2,1)S(1)}, u32[]{:S(2)}, u32[]{:S(2)}) async-start(bf16[1,1,4,8,16,1152]{5,4,2,1,0,3:T(8,128)(2,1)} %copy.260), calls=%async_computation | async-start | bytes 2359296 | tf_op jit(solution)/shard_map/all_to_all | solution.py:94
  259.4 41.2 %copy-start.100 = (f32[1152]{0:T(1024)}, f32[1152]{0:T(1024)S(1)}, u32[]{:S(2)}) copy-start(f32[1152]{0:T(1024)S(1)} %get-tuple-element.28) | copy-start | bytes 13828
  259.4 138.6 %copy-start.98 = (f32[1152]{0:T(1024)}, f32[1152]{0:T(1024)S(1)}, u32[]{:S(2)}) copy-start(f32[1152]{0:T(1024)S(1)} %get-tuple-element.26) | copy-start | bytes 13828
  259.4 238.2 %copy-start.66 = (f32[1152]{0:T(1024)}, f32[1152]{0:T(1024)S(1)}, u32[]{:S(2)}) copy-start(f32[1152]{0:T(1024)S(1)} %get-tuple-element.27) | copy-start | bytes 13828
  259.5 238.1 %copy-start.68 = (f32[1152]{0:T(1024)}, f32[1152]{0:T(1024)S(1)}, u32[]{:S(2)}) copy-start(f32[1152]{0:T(1024)S(1)} %get-tuple-element.25) | copy-start | bytes 13828
  331.1 16.4 %copy-start.33 = (bf16[32,16,16,72]{3,2,1,0:T(8,128)(2,1)S(1)}, bf16[32,16,16,72]{3,2,1,0:T(8,128)(2,1)}, u32[]{:S(2)}) copy-start(bf16[32,16,16,72]{3,2,1,0:T(8,128)(2,1)} %reshape.1275) | copy-start | bytes 3538948
  361.8 135.8 %copy-start.51 = (f32[32,16]{1,0:T(8,128)}, f32[32,16]{1,0:T(8,128)S(1)}, u32[]{:S(2)}) copy-start(f32[32,16]{1,0:T(8,128)S(1)} %copy.275) | copy-start | bytes 6148
  364.0 133.6 %copy-start.61 = (f32[32,16]{1,0:T(8,128)}, f32[32,16]{1,0:T(8,128)S(1)}, u32[]{:S(2)}) copy-start(f32[32,16]{1,0:T(8,128)S(1)} %copy.277) | copy-start | bytes 6148
  463.8 16.0 copy-start.11
  479.8 13.5 copy-start.106
  586.1 20.3 %all-to-all-start.3 = ((bf16[8,1,4,1,16,1152]{5,4,2,3,1,0:T(8,128)(2,1)}), bf16[8,1,4,1,16,1152]{5,4,2,3,1,0:T(8,128)(2,1)S(1)}, u32[]{:S(2)}, u32[]{:S(2)}) async-start(bf16[8,1,4,1,16,1152]{5,4,2,3,1,0:T(8,128)(2,1)} %bitcast.346), calls=%async_computation.3 | async-start | bytes 2359296 | tf_op jit(solution)/shard_map/all_to_all | solution.py:116
  589.7 234.3 %reduce-scatter.19.cloned.1.call-start = ((), (), s32[]{:S(2)}) async-start(), calls=%async_computation.25 | async-start | bytes 2985984 | tf_op jit(solution)/shard_map/reduce_scatter | solution.py:266
  602.4 221.5 %reduce-scatter.11.cloned.1.call-start = ((), (), s32[]{:S(2)}) async-start(), calls=%async_computation.21 | async-start | bytes 2985984 | tf_op jit(solution)/shard_map/reduce_scatter | solution.py:266
  606.4 17.7 %copy-start.20 = (bf16[8,1,4,1,16,1152]{5,4,2,3,1,0:T(8,128)(2,1)}, bf16[8,1,4,1,16,1152]{5,4,2,3,1,0:T(8,128)(2,1)S(1)}, u32[]{:S(2)}) copy-start(bf16[8,1,4,1,16,1152]{5,4,2,3,1,0:T(8,128)(2,1)S(1)} %all-to-all-done.3) | copy-start | bytes 3538948
  606.6 17.5 %copy-start.4 = (f32[4,128,1152]{2,1,0:T(8,128)S(1)}, f32[4,128,1152]{2,1,0:T(8,128)}, u32[]{:S(2)}) copy-start(f32[4,128,1152]{2,1,0:T(8,128)} %copy-done.3) | copy-start | bytes 7077892
  606.6 17.5 %copy-start.56 = (f32[1152]{0:T(1024)S(1)}, f32[1152]{0:T(1024)}, u32[]{:S(2)}) copy-start(f32[1152]{0:T(1024)} %copy-done.55) | copy-start | bytes 13828
  606.7 17.5 %copy-start.74 = (f32[4,128]{1,0:T(4,128)S(1)}, f32[4,128]{1,0:T(4,128)}, u32[]{:S(2)}) copy-start(f32[4,128]{1,0:T(4,128)} %copy-done.73) | copy-start | bytes 6148
  645.8 178.2 %reduce-scatter.17.cloned.1.call-start = ((), (), s32[]{:S(2)}) async-start(), calls=%async_computation.24 | async-start | bytes 8957952 | tf_op jit(solution)/shard_map/reduce_scatter | solution.py:266
  657.1 187.2 %reduce-scatter.9.cloned.1.call-start = ((), (), s32[]{:S(2)}) async-start(), calls=%async_computation.20 | async-start | bytes 8957952 | tf_op jit(solution)/shard_map/reduce_scatter | solution.py:266
  664.5 22.2 %copy-start.43 = (bf16[1,4,128,1152]{2,3,1,0:T(8,128)(2,1)S(1)}, bf16[1,4,128,1152]{2,3,1,0:T(8,128)(2,1)}, u32[]{:S(2)}) copy-start(bf16[1,4,128,1152]{2,3,1,0:T(8,128)(2,1)} %copy.254) | copy-start | bytes 3538948
  703.2 5.3 collective-permute-start.1
  731.0 199.0 %reduce-scatter.23.cloned.1.call-start = ((), (), s32[]{:S(2)}) async-start(), calls=%async_computation.27 | async-start | bytes 11943936 | tf_op jit(solution)/shard_map/reduce_scatter | solution.py:266
  745.3 270.4 %reduce-scatter.21.cloned.1.call-start = ((), (), s32[]{:S(2)}) async-start(), calls=%async_computation.26 | async-start | bytes 11943936 | tf_op jit(solution)/shard_map/reduce_scatter | solution.py:266
  757.2 344.0 %reduce-scatter.15.cloned.1.call-start = ((), (), s32[]{:S(2)}) async-start(), calls=%async_computation.23 | async-start | bytes 11943936 | tf_op jit(solution)/shard_map/reduce_scatter | solution.py:266
  770.8 416.0 %reduce-scatter.13.cloned.1.call-start = ((), (), s32[]{:S(2)}) async-start(), calls=%async_computation.22 | async-start | bytes 11943936 | tf_op jit(solution)/shard_map/reduce_scatter | solution.py:266
  783.0 821.1 %all-reduce.5.cloned.1.call-start = ((), (), s32[]{:S(2)}) async-start(), calls=%async_computation.28 | async-start | bytes 23887872 | tf_op jit(solution)/shard_map/psum | solution.py:346
  (83 other events, 250.4 us)
Sparse Core Ops, SparseCore 0:
  9.9 55.5 all-gather.8
  67.4 38.8 all-gather.10
  108.2 66.9 all-gather.12
  177.0 63.8 all-gather.14
  242.6 57.9 all-gather.16
  302.3 29.9 all-gather.18
  334.2 63.8 all-gather.20
  399.9 63.8 all-gather.22
  602.5 45.0 reduce-scatter.18
  652.0 43.7 reduce-scatter.10
  699.3 70.5 reduce-scatter.16
  773.7 70.5 reduce-scatter.8
  847.8 82.1 reduce-scatter.22
  933.4 82.2 reduce-scatter.20
  1019.0 82.1 reduce-scatter.14
  1104.6 82.1 reduce-scatter.12
  1191.7 412.4 all-reduce.4
where the time goes:
time: 1640 us; the launch traced here: 1630 us
  waiting for transfers between devices  974 us (59%)
  matrix products  326 us (20%)
  local copies, waits for them, and re-layouts  141 us (9%)
  other arithmetic  90 us (5%)
  blocking collectives  69.6 us (4%)
    psum x1, waiting for transfers between devices, per_device(): lax.psum(mod_weight_one.astype(jnp.bfloat16), 'rep').astype(jnp.float32)  387 us
    reduce_scatter x8, waiting for transfers between devices, spread_rows_out(): lax.psum_scatter(jnp.einsum('nd,ne->de', left_flat, right_flat, preferred...  363 us
    all_gather x2, waiting for transfers between devices, gather_layer(): lax.all_gather(down_w, 'seq', axis=0, tiled=True)  106 us
    dot_general x8, matrix products, project(): jnp.einsum('csld,de->csle', left_operand, right_operand, preferred_elemen...  87.4 us
    dot_general x8, matrix products, project_back(): jnp.einsum('csle,de->csld', incoming, right_operand, preferred_element_ty...  87.1 us
    dot_general x8, matrix products, spread_rows_out(): jnp.einsum('nd,ne->de', left_flat, right_flat, preferred_element_type=jnp...  76.2 us
    all_gather x2, waiting for transfers between devices, gather_layer(): lax.all_gather(up_w, 'seq', axis=0, tiled=True)  70.6 us
  transfers between devices with their start and end apart: 22, of which 14 were waited for; matrix products, arithmetic and copies ran while one was open for 24% of the time, Pallas kernels for 0%

commit v1 on v0

--- a/solution.py
+++ b/solution.py
@@ -260,23 +260,134 @@
     return (stream_grad, mod_grad, grad_pairs)
 
 
-def spread_rows_out(left_operand, right_operand):
-    left_flat = left_operand.reshape(-1, left_operand.shape[-1])
-    right_flat = right_operand.reshape(-1, right_operand.shape[-1])
-    return lax.psum_scatter(
-        jnp.einsum("nd,ne->de", left_flat, right_flat, preferred_element_type=jnp.float32).astype(
+def bit_count(axis):
+    return lax.axis_size(axis).bit_length() - 1
+
+
+def swap(block, axis, bit):
+    count = lax.axis_size(axis)
+    return lax.ppermute(block, axis, [(at, at ^ (1 << bit)) for at in range(count)])
+
+
+def bit_of(axis, bit):
+    return (lax.axis_index(axis) >> bit) & 1
+
+
+def pick(block, which, axis):
+    return lax.dynamic_index_in_dim(block, which, axis, keepdims=False)
+
+
+def spread_rows_out(left_turned, right_operand, flipped):
+    bits = bit_count("seq")
+    total_rows, tokens = left_turned.shape
+    rows = total_rows >> bits
+    halves = left_turned.reshape(1 << (bits - 1), 2, rows, tokens)
+    core = bit_of("seq", 0)
+
+    def product(which):
+        left = pick(halves, which, 1).reshape(-1, tokens)
+        return jnp.dot(left, right_operand, preferred_element_type=jnp.float32).astype(
             jnp.bfloat16
-        ),
-        "seq",
-        scatter_dimension=0,
-        tiled=True,
-    ).astype(jnp.float32)
+        )
+
+    arrived = swap(product(1 - core), "seq", 0)
+    held = product(core)
+    left_bits = list(range(bits - 1, 0, -1))
+    shape = [2] * (bits - 1) + [rows, right_operand.shape[1]]
+    held = held.reshape(shape)
+    arrived = arrived.reshape(shape)
+    order = list(left_bits) if flipped else left_bits[::-1]
+    for bit in order:
+        at = left_bits.index(bit)
+        mine = bit_of("seq", bit)
+        away = pick(held, 1 - mine, at).astype(jnp.float32) + pick(arrived, 1 - mine, at)
+        kept = pick(held, mine, at).astype(jnp.float32) + pick(arrived, mine, at)
+        arrived = swap(away.astype(jnp.bfloat16), "seq", bit)
+        held = kept.astype(jnp.bfloat16)
+        left_bits.remove(bit)
+    return held.astype(jnp.float32) + arrived
+
+
+def rep_sum(block, axis):
+    bits = bit_count("rep")
+    held = block.astype(jnp.bfloat16)
+    for bit in range(bits):
+        mine = bit_of("rep", bit)
+        low, high = jnp.split(held, 2, axis)
+        away = jnp.where(mine == 0, high, low)
+        kept = jnp.where(mine == 0, low, high)
+        held = (kept.astype(jnp.float32) + swap(away, "rep", bit)).astype(jnp.bfloat16)
+    for bit in reversed(range(bits)):
+        mine = bit_of("rep", bit)
+        other = swap(held, "rep", bit)
+        low = jnp.where(mine == 0, held, other)
+        high = jnp.where(mine == 0, other, held)
+        held = jnp.concatenate([low, high], axis)
+    return held.astype(jnp.float32)
+
+
+def turned(operand):
+    return operand.reshape(-1, operand.shape[-1]).T
+
+
+def flat(operand):
+    return operand.reshape(-1, operand.shape[-1])
+
+
+def cut(width, parts, of):
+    return width * parts // of // 128 * 128
+
+
+def down_grad(pair):
+    left, right = turned(pair[0]), flat(pair[1])
+    edge = cut(right.shape[1], 5, 9)
+    return jnp.concatenate(
+        [
+            rep_sum(spread_rows_out(left, right[:, :edge], False), 0),
+            rep_sum(spread_rows_out(left, right[:, edge:], True), 0),
+        ],
+        1,
+    )
+
+
+def up_grad(pair):
+    left, right = turned(pair[0]), flat(pair[1])
+    edge = cut(right.shape[1], 4, 9)
+    return jnp.concatenate(
+        [
+            rep_sum(spread_rows_out(left, right[:, :edge], False), 1),
+            rep_sum(spread_rows_out(left, right[:, edge:], True), 1),
+        ],
+        1,
+    )
+
+
+def attention_grads(qkv_pair, out_pair):
+    left, right = turned(qkv_pair[0]), flat(qkv_pair[1])
+    width = right.shape[1]
+    edge = cut(width, 16, 27)
+    first = rep_sum(spread_rows_out(left, right[:, :edge], False), 1)
+    second = spread_rows_out(left, right[:, edge:], True)
+    third = spread_rows_out(turned(out_pair[0]), flat(out_pair[1]), True)
+    joined = rep_sum(jnp.concatenate([second, third], 1), 1)
+    return (
+        jnp.concatenate([first, joined[:, : width - edge]], 1),
+        joined[:, width - edge :],
+    )
 
 
 def layer_grads(grad_pairs):
-    return tuple(
-        (spread_rows_out(grad_pairs[index][0], grad_pairs[index][1]) for index in range(4))
-    )
+    qkv_pair, out_pair, up_pair, down_pair = grad_pairs
+    down = down_grad(down_pair)
+    up = up_grad(up_pair)
+    qkv, out = attention_grads(qkv_pair, out_pair)
+    return (qkv, out, up, down)
+
+
+def seq_sum(block):
+    for bit in range(bit_count("seq")):
+        block = block + swap(block, "seq", bit)
+    return block
 
 
 def per_device(
@@ -324,17 +435,15 @@
         spatial_grad, start_stream, mod_one, again_one, state_one, True
     )
     grads_one = layer_grads(pairs_one)
-    mod_totals = (
-        lax.psum(mod_grad_one.astype(jnp.bfloat16), "seq").astype(jnp.float32),
-        lax.psum(mod_grad_two.astype(jnp.bfloat16), "seq").astype(jnp.float32),
-    )
-    low_one = mod_totals[0].astype(jnp.bfloat16)
-    low_two = mod_totals[1].astype(jnp.bfloat16)
-    mod_weight_one = jnp.einsum(
-        "cd,ce->de", silu_local, low_one, preferred_element_type=jnp.float32
-    )
-    mod_weight_two = jnp.einsum(
-        "cd,ce->de", silu_local, low_two, preferred_element_type=jnp.float32
+    mod_total = lax.psum(
+        jnp.concatenate([mod_grad_one, mod_grad_two], 1).astype(jnp.bfloat16), "seq"
+    ).astype(jnp.bfloat16)
+    mod_width = mod_grad_one.shape[1]
+    low_one, low_two = mod_total[:, :mod_width], mod_total[:, mod_width:]
+    every_mod = lax.all_gather(mod_total, "rep", axis=0, tiled=True)
+    every_silu = lax.all_gather(silu_local, "rep", axis=0, tiled=True)
+    mod_weights = jnp.einsum(
+        "cd,ce->de", every_silu, every_mod, preferred_element_type=jnp.float32
     )
     silu_grad = jnp.einsum("ce,de->cd", low_one, mod_first, preferred_element_type=jnp.float32)
     silu_grad = silu_grad + jnp.einsum(
@@ -343,16 +452,10 @@
     condition_local = lax.dynamic_slice_in_dim(conditioning, row_start, row_attn, 1)
     condition_grad = jax.vjp(jax.nn.silu, condition_local)[1](silu_grad)[0]
     summed = (
-        lax.psum(mod_weight_one.astype(jnp.bfloat16), "rep").astype(jnp.float32),
-        lax.psum(grads_one[0].astype(jnp.bfloat16), "rep").astype(jnp.float32),
-        lax.psum(grads_one[1].astype(jnp.bfloat16), "rep").astype(jnp.float32),
-        lax.psum(grads_one[2].astype(jnp.bfloat16), "rep").astype(jnp.float32),
-        lax.psum(grads_one[3].astype(jnp.bfloat16), "rep").astype(jnp.float32),
-        lax.psum(mod_weight_two.astype(jnp.bfloat16), "rep").astype(jnp.float32),
-        lax.psum(grads_two[0].astype(jnp.bfloat16), "rep").astype(jnp.float32),
-        lax.psum(grads_two[1].astype(jnp.bfloat16), "rep").astype(jnp.float32),
-        lax.psum(grads_two[2].astype(jnp.bfloat16), "rep").astype(jnp.float32),
-        lax.psum(grads_two[3].astype(jnp.bfloat16), "rep").astype(jnp.float32),
+        (mod_weights[:, :mod_width],)
+        + tuple(grads_one)
+        + (mod_weights[:, mod_width:],)
+        + tuple(grads_two)
     )
     out_shape = (clip_count, 1, frame_dev, half_places, features)
     return (

time: 1640 us -> 1450 us (0.88)
  waiting for transfers between devices: 974 us -> 573 us
  starting transfers between devices: 13.2 us -> 90.3 us
  local copies, waits for them, and re-layouts: 141 us -> 211 us
  other arithmetic: 90 us -> 147 us
    ppermute x0 -> x90, waiting for transfers between devices: none -> 394 us  [swap(): lax.ppermute(block, axis, [(at, at ^ 1 << bit) for at in range(count)])]
    psum x1 -> x0, waiting for transfers between devices: 387 us -> none  [per_device(): lax.psum(mod_weight_one.astype(jnp.bfloat16), 'rep').astype(jnp.float32)]
    reduce_scatter x8 -> x0, waiting for transfers between devices: 363 us -> none  [spread_rows_out(): lax.psum_scatter(jnp.einsum('nd,ne->de', left_flat, right_flat, preferred...]
    ppermute x0 -> x90, starting transfers between devices: none -> 73.5 us  [swap(): lax.ppermute(block, axis, [(at, at ^ 1 << bit) for at in range(count)])]
    convert_element_type x12 -> x69, other arithmetic: 22.4 us -> 54.4 us  [the longest x14 38.7 us: spread_rows_out(): held = kept.astype(jnp.bfloat16)]
    all_gather x0 -> x2, blocking collectives: none -> 25.8 us  [the longest x1 14.2 us: per_device(): every_mod = lax.all_gather(mod_total, 'rep', axis=0, tiled=True)]
    all_gather x2, waiting for transfers between devices: 70.6 us -> 49.3 us  [gather_layer(): lax.all_gather(up_w, 'seq', axis=0, tiled=True)]
    all_to_all x1 -> x0, blocking collectives: 19.3 us -> none  [to_frames(): lax.all_to_all(shortened(arranged), 'seq', split_axis=0, concat_axis=3, t...]
  transfers between devices with their start and end apart: 22 -> 104, of which waited for: 14 -> 61; matrix products, arithmetic and copies ran while one was open for 24% -> 35% of each run, Pallas kernels for 0% -> 0%
where the time goes in v1:
time: 1450 us; the launch traced here: 1440 us
  waiting for transfers between devices  573 us (40%)
  matrix products  328 us (23%)
  local copies, waits for them, and re-layouts  211 us (15%)
  other arithmetic  147 us (10%)
  starting transfers between devices  90.3 us (6%)
  blocking collectives  77.7 us (5%)
  between operations  17 us (1%)
    ppermute x90, waiting for transfers between devices, swap(): lax.ppermute(block, axis, [(at, at ^ 1 << bit) for at in range(count)])  394 us
    all_gather x2, waiting for transfers between devices, gather_layer(): lax.all_gather(down_w, 'seq', axis=0, tiled=True)  102 us
    dot_general x8, matrix products, project(): jnp.einsum('csld,de->csle', left_operand, right_operand, preferred_elemen...  87.6 us
    dot_general x8, matrix products, project_back(): jnp.einsum('csle,de->csld', incoming, right_operand, preferred_element_ty...  82.9 us
    dot_general x28, matrix products, product(): jnp.dot(left, right_operand, preferred_element_type=jnp.float32)  79.6 us
    ppermute x90, starting transfers between devices, swap(): lax.ppermute(block, axis, [(at, at ^ 1 << bit) for at in range(count)])  73.5 us
    all_gather x2, waiting for transfers between devices, gather_layer(): lax.all_gather(up_w, 'seq', axis=0, tiled=True)  49.3 us
    another operation x11, local copies, waits for them, and re-layouts  39.6 us
  transfers between devices with their start and end apart: 104, of which 61 were waited for; matrix products, arithmetic and copies ran while one was open for 35% of the time, Pallas kernels for 0%

profile of v1, /device:TPU:0, one launch (start us, length us, event | category | flops | bytes accessed | tf_op | source)
XLA Modules:
  0.0 1444.3 jit_solution(9031532522761724848)
XLA Ops:
  15.7 26.5 %all-reduce = (f32[1,6912]{1,0:T(1,128)S(1)}, f32[1,6912]{1,0:T(1,128)S(1)}) all-reduce(f32[1,6912]{1,0:T(1,128)S(1)} %fusion.263, f32[1,6912]{1,0:T(1,128)S(1)} %fusion.261), channel_id=1, replica_groups=mesh['rep'=4,'seq'=8] {'seq'}, use_global_device_ids=true, to_apply=%region_0.1 | all-reduce | flops 13824 | bytes 110592 | tf_op jit(solution)/shard_map/psum | solution.py:60
  43.6 21.9 %all-gather.11.cloned.1.call-done = bf16[1152,3456]{1,0:T(8,128)(2,1)} async-done(((bf16[144,3456]{1,0:T(8,128)(2,1)}), bf16[1152,3456]{1,0:T(8,128)(2,1)}) %all-gather.11.cloned.1.call-update) | async-done | bytes 7962640 | tf_op jit(solution)/shard_map/all_gather | solution.py:66
  65.5 8.8 fusion.54
  87.3 11.6 all-gather
  124.0 21.7 %fusion.129 = bf16[4,16,72,128]{3,2,1,0:T(8,128)(2,1)} fusion(bf16[1,4,128,16,72]{2,4,3,1,0:T(8,128)(2,1)} %bitcast.733, bf16[1,4,128,16,72]{2,4,3,1,0:T(8,128)(2,1)} %bitcast.731, f32[4,16,128]{2,1,0:T(8,128)S(1)} %get-tuple-element.166, f32[4,16,128,256]{3,2,1,0:T(8,128)} %copy-done.8), kind=kOutput, calls=%fused_computation.237 | convolution fusion | flops 317792512 | bytes 11960320 | tf_op jit(solution)/shard_map/cshlm,csmhe->cslhe/dot_general | solution.py:144
  153.1 22.6 %all-gather.15.cloned.1.call-done = bf16[1152,4608]{1,0:T(8,128)(2,1)} async-done(((bf16[144,4608]{1,0:T(8,128)(2,1)}), bf16[1152,4608]{1,0:T(8,128)(2,1)}) %all-gather.15.cloned.1.call-update) | async-done | bytes 10616848 | tf_op jit(solution)/shard_map/all_gather | solution.py:68
  175.7 14.8 %multiply_convert_fusion.1 = (bf16[4,128,4608]{2,1,0:T(8,128)(2,1)}, f32[4,128,4608]{2,1,0:T(8,128)}) fusion(bf16[4,128,1152]{2,1,0:T(8,128)(2,1)S(1)} %add_convert_fusion.27, bf16[1152,4608]{1,0:T(8,128)(2,1)} %all-gather.15.cloned.1.call-done), kind=kOutput, calls=%fused_computation.37 | convolution fusion | flops 5457051648 | bytes 25952256 | tf_op jit(solution)/shard_map/csld,de->csle/dot_general | solution.py:39
  190.5 50.8 %all-gather.17.cloned.1.call-done = bf16[4608,1152]{1,0:T(8,128)(2,1)} async-done(((bf16[576,1152]{1,0:T(8,128)(2,1)}), bf16[4608,1152]{1,0:T(8,128)(2,1)}) %all-gather.17.cloned.1.call-update) | async-done | bytes 10616848 | tf_op jit(solution)/shard_map/all_gather | solution.py:69
  241.3 12.6 add_convert_fusion.26
  305.3 9.0 fusion.51
  335.7 16.3 %fusion.302 = (f32[32,16,16]{2,1,0:T(8,128)S(1)}, f32[32,16,16,16]{2,3,1,0:T(8,128)S(1)}) fusion(f32[32,16,16,16]{2,3,1,0:T(8,128)S(1)} %fusion.119), kind=kOutput, calls=%fused_computation.639 | output fusion | flops 524303 | bytes 1081344 | tf_op jit(solution)/shard_map/sub | solution.py:141
  376.4 26.6 %all-gather.23.cloned.1.call-done = bf16[1152,4608]{1,0:T(8,128)(2,1)} async-done(((bf16[144,4608]{1,0:T(8,128)(2,1)}), bf16[1152,4608]{1,0:T(8,128)(2,1)}) %all-gather.23.cloned.1.call-update) | async-done | bytes 10616848 | tf_op jit(solution)/shard_map/all_gather | solution.py:68
  403.0 14.5 %multiply_convert_fusion = (bf16[32,16,4608]{2,1,0:T(8,128)(2,1)}, f32[32,16,4608]{2,1,0:T(8,128)}) fusion(bf16[32,16,1152]{2,1,0:T(8,128)(2,1)S(1)} %add_convert_fusion.24, bf16[1152,4608]{1,0:T(8,128)(2,1)} %all-gather.23.cloned.1.call-done), kind=kOutput, calls=%fused_computation.36 | convolution fusion | flops 5457051648 | bytes 25952256 | tf_op jit(solution)/shard_map/csld,de->csle/dot_general | solution.py:39
  417.5 51.3 %all-gather.25.cloned.1.call-done = bf16[4608,1152]{1,0:T(8,128)(2,1)} async-done(((bf16[576,1152]{1,0:T(8,128)(2,1)}), bf16[4608,1152]{1,0:T(8,128)(2,1)}) %all-gather.25.cloned.1.call-update) | async-done | bytes 10616848 | tf_op jit(solution)/shard_map/all_gather | solution.py:69
  468.7 15.7 %fusion.31 = bf16[32,16,4608]{2,1,0:T(8,128)(2,1)S(1)} fusion(f32[32,16,4608]{2,1,0:T(8,128)} %get-tuple-element.177, bf16[4608,1152]{1,0:T(8,128)(2,1)} %all-gather.25.cloned.1.call-done, f32[32,16,1152]{2,1,0:T(8,128)} %reshape.1789, f32[1152]{0:T(1024)S(1)} %get-tuple-element.25), kind=kOutput, calls=%fused_computation.35 | convolution fusion | flops 5484183552 | bytes 27136512 | tf_op jit(solution)/shard_map/csle,de->csld/dot_general | solution.py:45
  484.4 13.5 multiply_reduce_fusion.13
  502.3 15.7 %multiply_reduce_fusion.4 = (bf16[1152]{0:T(1024)(128)(2,1)}, bf16[32,16,1152]{2,1,0:T(8,128)(2,1)}, bf16[1152]{0:T(1024)(128)(2,1)}, f32[32,16,1152]{2,1,0:T(8,128)S(1)}) fusion(f32[32,16,1152]{2,1,0:T(8,128)} %reshape.1789, f32[32,16,1152]{2,1,0:T(8,128)} %get-tuple-element.44, f32[1152]{0:T(1024)S(1)} %get-tuple-element.25, ...), kind=kOutput, calls=%fused_computation.174 | convolution fusion | flops 5444663296 | bytes 28333568 | tf_op jit(solution)/shard_map/csld,de->csle/dot_general | solution.py:39
  624.9 10.7 multiply_reduce_fusion.12
  684.5 17.0 %fusion.24 = bf16[4,128,4608]{2,1,0:T(8,128)(2,1)} fusion(f32[4,128,4608]{2,1,0:T(8,128)} %get-tuple-element.170, bf16[4608,1152]{1,0:T(8,128)(2,1)} %all-gather.17.cloned.1.call-done, f32[4,128,1152]{2,1,0:T(8,128)S(1)} %bitcast.661, f32[1152]{0:T(1024)S(1)} %copy-done.123), kind=kOutput, calls=%fused_computation.28 | convolution fusion | flops 5484183552 | bytes 27136512 | tf_op jit(solution)/shard_map/csle,de->csld/dot_general | solution.py:45
  701.5 11.5 multiply_reduce_fusion.11
  725.3 22.1 %convolution_bitcast_fusion = f32[1,4,256,16,72]{2,4,3,1,0:T(8,128)} fusion(bf16[4,128,16,72]{1,3,2,0:T(8,128)(2,1)} %bitcast.741, f32[4,16,128]{2,1,0:T(8,128)S(1)} %copy-done.108, f32[4,16,128,256]{3,2,1,0:T(8,128)} %copy-done.8), kind=kOutput, calls=%fused_computation.206 | convolution fusion | flops 312484096 | bytes 14319616 | tf_op jit(solution)/shard_map/cshlm,cslhe->csmhe/dot_general | solution.py:221
  797.8 9.5 collective-permute-done.58
  872.4 7.4 collective-permute-done.14
  892.7 9.8 fusion.101
  915.3 25.3 %psum.24 = bf16[1,13824]{1,0:T(2,128)(2,1)} all-reduce(bf16[1,13824]{1,0:T(2,128)(2,1)} %constant_dynamic-update-slice_fusion), channel_id=1, replica_groups=mesh['rep'=4,'seq'=8] {'seq'}, use_global_device_ids=true, to_apply=%region_36.37 | all-reduce | flops 13824 | bytes 55296 | tf_op jit(solution)/shard_map/psum | solution.py:438
  950.6 14.2 all-gather.1
  974.0 7.7 collective-permute-done.61
  1000.3 15.1 %collective-permute-done.48 = bf16[2,144,2048]{2,1,0:T(8,128)(2,1)S(1)} collective-permute-done((bf16[2,144,2048]{2,1,0:T(8,128)(2,1)S(1)}, bf16[2,144,2048]{2,1,0:T(8,128)(2,1)S(1)}, u32[]{:S(2)}, u32[]{:S(2)}) %collective-permute-start.48) | collective-permute-done | bytes 1179680 | tf_op jit(solution)/shard_map/ppermute | solution.py:269
  1028.3 19.0 %collective-permute-done.66 = bf16[144,2048]{1,0:T(8,128)(2,1)S(1)} collective-permute-done((bf16[144,2048]{1,0:T(8,128)(2,1)}, bf16[144,2048]{1,0:T(8,128)(2,1)S(1)}, u32[]{:S(2)}, u32[]{:S(2)}) %collective-permute-start.66) | collective-permute-done | bytes 589856 | tf_op jit(solution)/shard_map/ppermute | solution.py:269
  1057.6 28.2 %collective-permute-done.87 = bf16[576,512]{1,0:T(8,128)(2,1)S(1)} collective-permute-done((bf16[576,512]{1,0:T(8,128)(2,1)S(1)}, bf16[576,512]{1,0:T(8,128)(2,1)S(1)}, u32[]{:S(2)}, u32[]{:S(2)}) %collective-permute-start.87) | collective-permute-done | bytes 589856 | tf_op jit(solution)/shard_map/ppermute | solution.py:269
  1103.1 8.3 collective-permute-done.68
  1111.4 9.2 collective-permute-done.51
  1120.7 8.9 collective-permute-done.89
  1138.9 8.9 collective-permute-done.52
  1147.9 9.1 collective-permute-done.90
  1159.6 7.3 collective-permute-done.70
  1173.0 7.4 collective-permute-done.91
  1183.3 10.6 collective-permute-done.21
  1195.9 10.5 collective-permute-done.42
  1209.2 16.7 %collective-permute-done.80 = bf16[576,640]{1,0:T(8,128)(2,1)S(1)} collective-permute-done((bf16[576,640]{1,0:T(8,128)(2,1)S(1)}, bf16[576,640]{1,0:T(8,128)(2,1)S(1)}, u32[]{:S(2)}, u32[]{:S(2)}) %collective-permute-start.80) | collective-permute-done | bytes 737312 | tf_op jit(solution)/shard_map/ppermute | solution.py:269
  1234.8 10.6 collective-permute-done.43
  1253.7 7.5 collective-permute-done.81
  1265.5 12.2 collective-permute-done.75
  1277.8 12.3 collective-permute-done.82
  1309.8 7.7 collective-permute-done.25
  1329.2 8.1 collective-permute-done.77
  1362.1 11.2 collective-permute-done.15
  1406.5 7.7 collective-permute-done.5
  (860 shorter events, 701.5 us)
Async XLA Ops:
  7.2 58.3 %all-gather.11.cloned.1.call-start = ((), (), s32[]{:S(2)}) async-start(), calls=%async_computation.4 | async-start | bytes 8957952 | tf_op jit(solution)/shard_map/all_gather | solution.py:66
  7.9 137.8 %all-gather.13.cloned.1.call-start = ((), (), s32[]{:S(2)}) async-start(), calls=%async_computation.5 | async-start | bytes 2985984 | tf_op jit(solution)/shard_map/all_gather | solution.py:67
  8.7 167.1 %all-gather.15.cloned.1.call-start = ((), (), s32[]{:S(2)}) async-start(), calls=%async_computation.6 | async-start | bytes 11943936 | tf_op jit(solution)/shard_map/all_gather | solution.py:68
  9.4 231.9 %all-gather.17.cloned.1.call-start = ((), (), s32[]{:S(2)}) async-start(), calls=%async_computation.7 | async-start | bytes 11943936 | tf_op jit(solution)/shard_map/all_gather | solution.py:69
  10.0 295.2 %all-gather.19.cloned.1.call-start = ((), (), s32[]{:S(2)}) async-start(), calls=%async_computation.8 | async-start | bytes 8957952 | tf_op jit(solution)/shard_map/all_gather | solution.py:66
  10.6 353.8 %all-gather.21.cloned.1.call-start = ((), (), s32[]{:S(2)}) async-start(), calls=%async_computation.9 | async-start | bytes 2985984 | tf_op jit(solution)/shard_map/all_gather | solution.py:67
  11.2 391.8 %all-gather.23.cloned.1.call-start = ((), (), s32[]{:S(2)}) async-start(), calls=%async_computation.10 | async-start | bytes 11943936 | tf_op jit(solution)/shard_map/all_gather | solution.py:68
  11.9 456.8 %all-gather.25.cloned.1.call-start = ((), (), s32[]{:S(2)}) async-start(), calls=%async_computation.11 | async-start | bytes 11943936 | tf_op jit(solution)/shard_map/all_gather | solution.py:69
  78.0 28.1 %collective-permute-start = (bf16[2,1,4,128,1152]{4,3,2,1,0:T(8,128)(2,1)}, bf16[2,1,4,128,1152]{4,3,2,1,0:T(8,128)(2,1)}, u32[]{:S(2)}, u32[]{:S(2)}) collective-permute-start(bf16[2,1,4,128,1152]{4,3,2,1,0:T(8,128)(2,1)} %pad_maximum_fusion), channel_id=1, source_target_pairs={{0,1},{1,0},{2,3},{3,2},{4,5},{5,4},{6,7},{7,6},{8,9},{9,8},{10,11... | collective-permute-start | bytes 7077896 | tf_op jit(solution)/shard_map/ppermute | solution.py:20
  81.2 173.8 %all-to-all-start.2 = ((bf16[1,1,4,8,16,1152]{5,4,2,1,0,3:T(8,128)(2,1)}), bf16[1,1,4,8,16,1152]{5,4,2,1,0,3:T(8,128)(2,1)}, u32[]{:S(2)}, u32[]{:S(2)}) async-start(bf16[1,1,4,8,16,1152]{5,4,2,1,0,3:T(8,128)(2,1)} %copy.372), calls=%async_computation.2 | async-start | bytes 2359296 | tf_op jit(solution)/shard_map/all_to_all | solution.py:94
  255.0 31.1 %all-to-all-start = ((bf16[1,1,4,8,16,1152]{5,4,2,1,0,3:T(8,128)(2,1)}), bf16[1,1,4,8,16,1152]{5,4,2,1,0,3:T(8,128)(2,1)S(1)}, u32[]{:S(2)}, u32[]{:S(2)}) async-start(bf16[1,1,4,8,16,1152]{5,4,2,1,0,3:T(8,128)(2,1)} %copy.353), calls=%async_computation | async-start | bytes 2359296 | tf_op jit(solution)/shard_map/all_to_all | solution.py:94
  624.0 164.0 %collective-permute-start.57 = (bf16[576,1152]{1,0:T(8,128)(2,1)}, bf16[576,1152]{1,0:T(8,128)(2,1)}, u32[]{:S(2)}, u32[]{:S(2)}) collective-permute-start(bf16[576,1152]{1,0:T(8,128)(2,1)} %convolution_convert_fusion.14), channel_id=1, source_target_pairs={{0,1},{1,0},{2,3},{3,2},{4,5},{5,4},{6,7},{7,6},{8,9},{9,8},{10,11... | collective-permute-start | bytes 3981320 | tf_op jit(solution)/shard_map/ppermute | solution.py:269
  647.5 30.3 %all-to-all-start.3 = ((bf16[8,1,4,1,16,1152]{5,4,2,3,1,0:T(8,128)(2,1)}), bf16[8,1,4,1,16,1152]{5,4,2,3,1,0:T(8,128)(2,1)S(1)}, u32[]{:S(2)}, u32[]{:S(2)}) async-start(bf16[8,1,4,1,16,1152]{5,4,2,3,1,0:T(8,128)(2,1)} %bitcast.690), calls=%async_computation.3 | async-start | bytes 2359296 | tf_op jit(solution)/shard_map/all_to_all | solution.py:116
  655.4 156.5 %collective-permute-start.54 = (bf16[576,1408]{1,0:T(8,128)(2,1)}, bf16[576,1408]{1,0:T(8,128)(2,1)}, u32[]{:S(2)}, u32[]{:S(2)}) collective-permute-start(bf16[576,1408]{1,0:T(8,128)(2,1)} %convolution_convert_fusion.24), channel_id=1, source_target_pairs={{0,1},{1,0},{2,3},{3,2},{4,5},{5,4},{6,7},{7,6},{8,9},{9,8},{10,11... | collective-permute-start | bytes 4866056 | tf_op jit(solution)/shard_map/ppermute | solution.py:269
  668.4 170.7 %collective-permute-start.64 = (bf16[576,2048]{1,0:T(8,128)(2,1)}, bf16[576,2048]{1,0:T(8,128)(2,1)}, u32[]{:S(2)}, u32[]{:S(2)}) collective-permute-start(bf16[576,2048]{1,0:T(8,128)(2,1)} %convolution_convert_fusion.12), channel_id=1, source_target_pairs={{0,1},{1,0},{2,3},{3,2},{4,5},{5,4},{6,7},{7,6},{8,9},{9,8},{10,11... | collective-permute-start | bytes 7077896 | tf_op jit(solution)/shard_map/ppermute | solution.py:269
  668.5 175.5 %collective-permute-start.85 = (bf16[2304,512]{1,0:T(8,128)(2,1)}, bf16[2304,512]{1,0:T(8,128)(2,1)}, u32[]{:S(2)}, u32[]{:S(2)}) collective-permute-start(bf16[2304,512]{1,0:T(8,128)(2,1)} %convolution_convert_fusion.8), channel_id=1, source_target_pairs={{0,1},{1,0},{2,3},{3,2},{4,5},{5,4},{6,7},{7,6},{8,9},{9,8},{10,11... | collective-permute-start | bytes 7077896 | tf_op jit(solution)/shard_map/ppermute | solution.py:269
  678.8 102.8 %all-to-all-start.1 = ((bf16[8,1,4,1,16,1152]{5,4,2,3,1,0:T(8,128)(2,1)}), bf16[8,1,4,1,16,1152]{5,4,2,3,1,0:T(8,128)(2,1)S(1)}, u32[]{:S(2)}, u32[]{:S(2)}) async-start(bf16[8,1,4,1,16,1152]{5,4,2,3,1,0:T(8,128)(2,1)} %bitcast.685), calls=%async_computation.1 | async-start | bytes 2359296 | tf_op jit(solution)/shard_map/all_to_all | solution.py:116
  764.0 56.1 %collective-permute-start.12 = (bf16[576,1152]{1,0:T(8,128)(2,1)}, bf16[576,1152]{1,0:T(8,128)(2,1)}, u32[]{:S(2)}, u32[]{:S(2)}) collective-permute-start(bf16[576,1152]{1,0:T(8,128)(2,1)} %convolution_convert_fusion.20), channel_id=1, source_target_pairs={{0,1},{1,0},{2,3},{3,2},{4,5},{5,4},{6,7},{7,6},{8,9},{9,8},{10,11... | collective-permute-start | bytes 3981320 | tf_op jit(solution)/shard_map/ppermute | solution.py:269
  811.9 36.3 %collective-permute-start.47 = (bf16[576,2048]{1,0:T(8,128)(2,1)}, bf16[576,2048]{1,0:T(8,128)(2,1)}, u32[]{:S(2)}, u32[]{:S(2)}) collective-permute-start(bf16[576,2048]{1,0:T(8,128)(2,1)} %convolution_convert_fusion.16), channel_id=1, source_target_pairs={{0,1},{1,0},{2,3},{3,2},{4,5},{5,4},{6,7},{7,6},{8,9},{9,8},{10,11... | collective-permute-start | bytes 7077896 | tf_op jit(solution)/shard_map/ppermute | solution.py:269
  820.1 34.9 %collective-permute-start.71 = (bf16[576,2560]{1,0:T(8,128)(2,1)}, bf16[576,2560]{1,0:T(8,128)(2,1)}, u32[]{:S(2)}, u32[]{:S(2)}) collective-permute-start(bf16[576,2560]{1,0:T(8,128)(2,1)} %convolution_convert_fusion.4), channel_id=1, source_target_pairs={{0,1},{1,0},{2,3},{3,2},{4,5},{5,4},{6,7},{7,6},{8,9},{9,8},{10,11... | collective-permute-start | bytes 8847368 | tf_op jit(solution)/shard_map/ppermute | solution.py:269
  844.0 125.8 %collective-permute-start.19 = (bf16[576,2048]{1,0:T(8,128)(2,1)}, bf16[576,2048]{1,0:T(8,128)(2,1)}, u32[]{:S(2)}, u32[]{:S(2)}) collective-permute-start(bf16[576,2048]{1,0:T(8,128)(2,1)} %convolution_convert_fusion.18), channel_id=1, source_target_pairs={{0,1},{1,0},{2,3},{3,2},{4,5},{5,4},{6,7},{7,6},{8,9},{9,8},{10,11... | collective-permute-start | bytes 7077896 | tf_op jit(solution)/shard_map/ppermute | solution.py:269
  848.2 32.5 %collective-permute-start.1 = (bf16[2,1,4,128,16,72]{3,5,4,2,1,0:T(8,128)(2,1)S(1)}, bf16[2,1,4,128,16,72]{3,5,4,2,1,0:T(8,128)(2,1)S(1)}, u32[]{:S(2)}, u32[]{:S(2)}) collective-permute-start(bf16[2,1,4,128,16,72]{3,5,4,2,1,0:T(8,128)(2,1)S(1)} %copy-done.56), channel_id=1, source_target_pairs={{0,1},{1,0},{2,3},{3,2},{4,5},{5,4},{6,7},{7,6},{8,9},{9,8},{10,11... | collective-permute-start | bytes 7077896 | tf_op jit(solution)/shard_map/ppermute | solution.py:20
  855.0 169.2 %collective-permute-start.26 = (bf16[576,2560]{1,0:T(8,128)(2,1)}, bf16[576,2560]{1,0:T(8,128)(2,1)}, u32[]{:S(2)}, u32[]{:S(2)}) collective-permute-start(bf16[576,2560]{1,0:T(8,128)(2,1)} %convolution_convert_fusion.6), channel_id=1, source_target_pairs={{0,1},{1,0},{2,3},{3,2},{4,5},{5,4},{6,7},{7,6},{8,9},{9,8},{10,11... | collective-permute-start | bytes 8847368 | tf_op jit(solution)/shard_map/ppermute | solution.py:269
  869.3 113.1 %collective-permute-start.40 = (bf16[2304,512]{1,0:T(8,128)(2,1)}, bf16[2304,512]{1,0:T(8,128)(2,1)}, u32[]{:S(2)}, u32[]{:S(2)}) collective-permute-start(bf16[2304,512]{1,0:T(8,128)(2,1)} %convolution_convert_fusion.10), channel_id=1, source_target_pairs={{0,1},{1,0},{2,3},{3,2},{4,5},{5,4},{6,7},{7,6},{8,9},{9,8},{10,11... | collective-permute-start | bytes 7077896 | tf_op jit(solution)/shard_map/ppermute | solution.py:269
  879.8 140.2 %collective-permute-start.33 = (bf16[2304,640]{1,0:T(8,128)(2,1)}, bf16[2304,640]{1,0:T(8,128)(2,1)}, u32[]{:S(2)}, u32[]{:S(2)}) collective-permute-start(bf16[2304,640]{1,0:T(8,128)(2,1)} %convolution_convert_fusion.2), channel_id=1, source_target_pairs={{0,1},{1,0},{2,3},{3,2},{4,5},{5,4},{6,7},{7,6},{8,9},{9,8},{10,11... | collective-permute-start | bytes 8847368 | tf_op jit(solution)/shard_map/ppermute | solution.py:269
  880.7 114.3 %collective-permute-start.65 = (bf16[2,144,2048]{2,1,0:T(8,128)(2,1)}, bf16[2,144,2048]{2,1,0:T(8,128)(2,1)}, u32[]{:S(2)}, u32[]{:S(2)}) collective-permute-start(bf16[2,144,2048]{2,1,0:T(8,128)(2,1)} %get-tuple-element.64), channel_id=1, source_target_pairs={{0,2},{1,3},{2,0},{3,1},{4,6},{5,7},{6,4},{7,5},{8,10},{9,11},{10,... | collective-permute-start | bytes 3538952 | tf_op jit(solution)/shard_map/ppermute | solution.py:269
  990.0 25.4 %collective-permute-start.48 = (bf16[2,144,2048]{2,1,0:T(8,128)(2,1)S(1)}, bf16[2,144,2048]{2,1,0:T(8,128)(2,1)S(1)}, u32[]{:S(2)}, u32[]{:S(2)}) collective-permute-start(bf16[2,144,2048]{2,1,0:T(8,128)(2,1)S(1)} %copy-done.84), channel_id=1, source_target_pairs={{0,2},{1,3},{2,0},{3,1},{4,6},{5,7},{6,4},{7,5},{8,10},{9,11},{10,... | collective-permute-start | bytes 3538952 | tf_op jit(solution)/shard_map/ppermute | solution.py:269
  999.4 101.1 %collective-permute-start.72 = (bf16[2,144,2560]{2,1,0:T(8,128)(2,1)S(1)}, bf16[2,144,2560]{2,1,0:T(8,128)(2,1)S(1)}, u32[]{:S(2)}, u32[]{:S(2)}) collective-permute-start(bf16[2,144,2560]{2,1,0:T(8,128)(2,1)S(1)} %copy-done.67), channel_id=1, source_target_pairs={{0,4},{1,5},{2,6},{3,7},{4,0},{5,1},{6,2},{7,3},{8,12},{9,13},{10,... | collective-permute-start | bytes 4423688 | tf_op jit(solution)/shard_map/ppermute | solution.py:269
  1015.4 85.9 %collective-permute-start.79 = (bf16[2,576,640]{2,1,0:T(8,128)(2,1)S(1)}, bf16[2,576,640]{2,1,0:T(8,128)(2,1)S(1)}, u32[]{:S(2)}, u32[]{:S(2)}) collective-permute-start(bf16[2,576,640]{2,1,0:T(8,128)(2,1)S(1)} %copy-done.68), channel_id=1, source_target_pairs={{0,2},{1,3},{2,0},{3,1},{4,6},{5,7},{6,4},{7,5},{8,10},{9,11},{10,... | collective-permute-start | bytes 4423688 | tf_op jit(solution)/shard_map/ppermute | solution.py:269
  1018.1 29.2 %collective-permute-start.66 = (bf16[144,2048]{1,0:T(8,128)(2,1)}, bf16[144,2048]{1,0:T(8,128)(2,1)S(1)}, u32[]{:S(2)}, u32[]{:S(2)}) collective-permute-start(bf16[144,2048]{1,0:T(8,128)(2,1)} %fusion.223), channel_id=1, source_target_pairs={{0,4},{1,5},{2,6},{3,7},{4,0},{5,1},{6,2},{7,3},{8,12},{9,13},{10,... | collective-permute-start | bytes 1769480 | tf_op jit(solution)/shard_map/ppermute | solution.py:269
  1020.0 82.3 %collective-permute-start.20 = (bf16[2,144,2048]{2,1,0:T(8,128)(2,1)}, bf16[2,144,2048]{2,1,0:T(8,128)(2,1)S(1)}, u32[]{:S(2)}, u32[]{:S(2)}) collective-permute-start(bf16[2,144,2048]{2,1,0:T(8,128)(2,1)} %get-tuple-element.72), channel_id=1, source_target_pairs={{0,2},{1,3},{2,0},{3,1},{4,6},{5,7},{6,4},{7,5},{8,10},{9,11},{10,... | collective-permute-start | bytes 3538952 | tf_op jit(solution)/shard_map/ppermute | solution.py:269
  1024.3 31.7 %collective-permute-start.49 = (bf16[144,2048]{1,0:T(8,128)(2,1)}, bf16[144,2048]{1,0:T(8,128)(2,1)S(1)}, u32[]{:S(2)}, u32[]{:S(2)}) collective-permute-start(bf16[144,2048]{1,0:T(8,128)(2,1)} %fusion.221), channel_id=1, source_target_pairs={{0,4},{1,5},{2,6},{3,7},{4,0},{5,1},{6,2},{7,3},{8,12},{9,13},{10,... | collective-permute-start | bytes 1769480 | tf_op jit(solution)/shard_map/ppermute | solution.py:269
  1047.3 38.5 %collective-permute-start.87 = (bf16[576,512]{1,0:T(8,128)(2,1)S(1)}, bf16[576,512]{1,0:T(8,128)(2,1)S(1)}, u32[]{:S(2)}, u32[]{:S(2)}) collective-permute-start(bf16[576,512]{1,0:T(8,128)(2,1)S(1)} %fusion.225), channel_id=1, source_target_pairs={{0,2},{1,3},{2,0},{3,1},{4,6},{5,7},{6,4},{7,5},{8,10},{9,11},{10,... | collective-permute-start | bytes 1769480 | tf_op jit(solution)/shard_map/ppermute | solution.py:269
  1056.0 30.1 %collective-permute-start.67 = (bf16[144,1024]{1,0:T(8,128)(2,1)S(1)}, bf16[144,1024]{1,0:T(8,128)(2,1)S(1)}, u32[]{:S(2)}, u32[]{:S(2)}) collective-permute-start(bf16[144,1024]{1,0:T(8,128)(2,1)S(1)} %broadcast_select_fusion.26), channel_id=1, source_target_pairs={{0,8},{8,0},{16,24},{24,16},{1,9},{9,1},{17,25},{25,17},{2,10},{10... | collective-permute-start | bytes 884744 | tf_op jit(solution)/shard_map/ppermute | solution.py:269
  1086.2 43.5 %collective-permute-start.41 = (bf16[2,576,512]{2,1,0:T(8,128)(2,1)S(1)}, bf16[2,576,512]{2,1,0:T(8,128)(2,1)S(1)}, u32[]{:S(2)}, u32[]{:S(2)}) collective-permute-start(bf16[2,576,512]{2,1,0:T(8,128)(2,1)S(1)} %copy-done.85), channel_id=1, source_target_pairs={{0,4},{1,5},{2,6},{3,7},{4,0},{5,1},{6,2},{7,3},{8,12},{9,13},{10,... | collective-permute-start | bytes 3538952 | tf_op jit(solution)/shard_map/ppermute | solution.py:269
  1100.4 56.7 %collective-permute-start.9 = (bf16[576,1408]{1,0:T(8,128)(2,1)S(1)}, bf16[576,1408]{1,0:T(8,128)(2,1)S(1)}, u32[]{:S(2)}, u32[]{:S(2)}) collective-permute-start(bf16[576,1408]{1,0:T(8,128)(2,1)S(1)} %copy-done.150), channel_id=1, source_target_pairs={{0,1},{1,0},{2,3},{3,2},{4,5},{5,4},{6,7},{7,6},{8,9},{9,8},{10,11... | collective-permute-start | bytes 4866056 | tf_op jit(solution)/shard_map/ppermute | solution.py:269
  1100.5 189.6 %collective-permute-start.2 = (bf16[576,2048]{1,0:T(8,128)(2,1)S(1)}, bf16[576,2048]{1,0:T(8,128)(2,1)S(1)}, u32[]{:S(2)}, u32[]{:S(2)}) collective-permute-start(bf16[576,2048]{1,0:T(8,128)(2,1)S(1)} %copy-done.149), channel_id=1, source_target_pairs={{0,1},{1,0},{2,3},{3,2},{4,5},{5,4},{6,7},{7,6},{8,9},{9,8},{10,11... | collective-permute-start | bytes 7077896 | tf_op jit(solution)/shard_map/ppermute | solution.py:269
  1101.3 144.3 %collective-permute-start.27 = (bf16[2,144,2560]{2,1,0:T(8,128)(2,1)S(1)}, bf16[2,144,2560]{2,1,0:T(8,128)(2,1)S(1)}, u32[]{:S(2)}, u32[]{:S(2)}) collective-permute-start(bf16[2,144,2560]{2,1,0:T(8,128)(2,1)S(1)} %get-tuple-element.58), channel_id=1, source_target_pairs={{0,4},{1,5},{2,6},{3,7},{4,0},{5,1},{6,2},{7,3},{8,12},{9,13},{10,... | collective-permute-start | bytes 4423688 | tf_op jit(solution)/shard_map/ppermute | solution.py:269
  1129.6 118.2 %collective-permute-start.34 = (bf16[2,576,640]{2,1,0:T(8,128)(2,1)S(1)}, bf16[2,576,640]{2,1,0:T(8,128)(2,1)S(1)}, u32[]{:S(2)}, u32[]{:S(2)}) collective-permute-start(bf16[2,576,640]{2,1,0:T(8,128)(2,1)S(1)} %get-tuple-element.56), channel_id=1, source_target_pairs={{0,2},{1,3},{2,0},{3,1},{4,6},{5,7},{6,4},{7,5},{8,10},{9,11},{10,... | collective-permute-start | bytes 4423688 | tf_op jit(solution)/shard_map/ppermute | solution.py:269
  1166.9 41.2 %collective-permute-start.73 = (bf16[144,2560]{1,0:T(8,128)(2,1)S(1)}, bf16[144,2560]{1,0:T(8,128)(2,1)S(1)}, u32[]{:S(2)}, u32[]{:S(2)}) collective-permute-start(bf16[144,2560]{1,0:T(8,128)(2,1)S(1)} %fusion.203), channel_id=1, source_target_pairs={{0,2},{1,3},{2,0},{3,1},{4,6},{5,7},{6,4},{7,5},{8,10},{9,11},{10,... | collective-permute-start | bytes 2211848 | tf_op jit(solution)/shard_map/ppermute | solution.py:269
  1208.1 92.8 %collective-permute-start.10 = (bf16[2,144,1408]{2,1,0:T(8,128)(2,1)S(1)}, bf16[2,144,1408]{2,1,0:T(8,128)(2,1)S(1)}, u32[]{:S(2)}, u32[]{:S(2)}) collective-permute-start(bf16[2,144,1408]{2,1,0:T(8,128)(2,1)S(1)} %get-tuple-element.88), channel_id=1, source_target_pairs={{0,4},{1,5},{2,6},{3,7},{4,0},{5,1},{6,2},{7,3},{8,12},{9,13},{10,... | collective-permute-start | bytes 2433032 | tf_op jit(solution)/shard_map/ppermute | solution.py:269
  1261.2 62.7 %collective-permute-start.28 = (bf16[144,2560]{1,0:T(8,128)(2,1)S(1)}, bf16[144,2560]{1,0:T(8,128)(2,1)S(1)}, u32[]{:S(2)}, u32[]{:S(2)}) collective-permute-start(bf16[144,2560]{1,0:T(8,128)(2,1)S(1)} %fusion.199), channel_id=1, source_target_pairs={{0,2},{1,3},{2,0},{3,1},{4,6},{5,7},{6,4},{7,5},{8,10},{9,11},{10,... | collective-permute-start | bytes 2211848 | tf_op jit(solution)/shard_map/ppermute | solution.py:269
  1262.5 63.9 %collective-permute-start.35 = (bf16[576,640]{1,0:T(8,128)(2,1)S(1)}, bf16[576,640]{1,0:T(8,128)(2,1)S(1)}, u32[]{:S(2)}, u32[]{:S(2)}) collective-permute-start(bf16[576,640]{1,0:T(8,128)(2,1)S(1)} %fusion.201), channel_id=1, source_target_pairs={{0,4},{1,5},{2,6},{3,7},{4,0},{5,1},{6,2},{7,3},{8,12},{9,13},{10,... | collective-permute-start | bytes 2211848 | tf_op jit(solution)/shard_map/ppermute | solution.py:269
  1300.9 91.2 %collective-permute-start.3 = (bf16[2,144,2048]{2,1,0:T(8,128)(2,1)S(1)}, bf16[2,144,2048]{2,1,0:T(8,128)(2,1)S(1)}, u32[]{:S(2)}, u32[]{:S(2)}) collective-permute-start(bf16[2,144,2048]{2,1,0:T(8,128)(2,1)S(1)} %get-tuple-element.74), channel_id=1, source_target_pairs={{0,2},{1,3},{2,0},{3,1},{4,6},{5,7},{6,4},{7,5},{8,10},{9,11},{10,... | collective-permute-start | bytes 3538952 | tf_op jit(solution)/shard_map/ppermute | solution.py:269
  1326.4 24.8 %collective-permute-start.29 = (bf16[144,1280]{1,0:T(8,128)(2,1)S(1)}, bf16[144,1280]{1,0:T(8,128)(2,1)S(1)}, u32[]{:S(2)}, u32[]{:S(2)}) collective-permute-start(bf16[144,1280]{1,0:T(8,128)(2,1)S(1)} %broadcast_select_fusion.14), channel_id=1, source_target_pairs={{0,8},{8,0},{16,24},{24,16},{1,9},{9,1},{17,25},{25,17},{2,10},{10... | collective-permute-start | bytes 1105928 | tf_op jit(solution)/shard_map/ppermute | solution.py:269
  1326.8 32.3 %collective-permute-start.36 = (bf16[288,640]{1,0:T(8,128)(2,1)S(1)}, bf16[288,640]{1,0:T(8,128)(2,1)S(1)}, u32[]{:S(2)}, u32[]{:S(2)}) collective-permute-start(bf16[288,640]{1,0:T(8,128)(2,1)S(1)} %broadcast_select_fusion.5), channel_id=1, source_target_pairs={{0,8},{8,0},{16,24},{24,16},{1,9},{9,1},{17,25},{25,17},{2,10},{10... | collective-permute-start | bytes 1105928 | tf_op jit(solution)/shard_map/ppermute | solution.py:269
  1337.3 36.0 %collective-permute-start.15 = (bf16[144,1280]{1,0:T(8,128)(2,1)S(1)}, bf16[144,1280]{1,0:T(8,128)(2,1)S(1)}, u32[]{:S(2)}, u32[]{:S(2)}) collective-permute-start(bf16[144,1280]{1,0:T(8,128)(2,1)S(1)} %broadcast_select_fusion.17), channel_id=1, source_target_pairs={{0,8},{8,0},{16,24},{24,16},{1,9},{9,1},{17,25},{25,17},{2,10},{10... | collective-permute-start | bytes 1105928 | tf_op jit(solution)/shard_map/ppermute | solution.py:269
  1396.7 25.4 %collective-permute-start.18 = (bf16[144,1280]{1,0:T(8,128)(2,1)S(1)}, bf16[144,1280]{1,0:T(8,128)(2,1)S(1)}, u32[]{:S(2)}, u32[]{:S(2)}) collective-permute-start(bf16[144,1280]{1,0:T(8,128)(2,1)S(1)} %pad_maximum_fusion.18), channel_id=1, source_target_pairs={{0,8},{8,0},{16,24},{24,16},{1,9},{9,1},{17,25},{25,17},{2,10},{10... | collective-permute-start | bytes 1105928 | tf_op jit(solution)/shard_map/ppermute | solution.py:269
  (221 other events, 2905.6 us)
Sparse Core Ops, SparseCore 0:
  9.9 55.5 all-gather.10
  67.4 39.3 all-gather.12
  108.7 67.0 all-gather.14
  177.5 63.8 all-gather.16
  243.1 62.1 all-gather.18
  307.0 30.2 all-gather.20
  339.1 63.8 all-gather.22
  404.9 63.8 all-gather.24

commit v2 on v1

--- a/solution.py
+++ b/solution.py
@@ -1,6 +1,10 @@
+import functools
+
 import jax
 import jax.numpy as jnp
 from jax import lax
+from jax.experimental import pallas as pl
+from jax.experimental.pallas import tpu as pltpu
 from jax.sharding import PartitionSpec as P
 
 HEADS = 16
@@ -47,36 +51,6 @@
 
 def mod_parts(modulation):
     return [segment[:, None, None, :] for segment in jnp.split(modulation, 6, axis=-1)]
-
-
-def modulations(conditioning, mod_one, mod_two):
-    row_count = mod_one.shape[0]
-    row_start = lax.axis_index("seq") * row_count
-    silu_local = lax.dynamic_slice_in_dim(
-        jax.nn.silu(conditioning), row_start, row_count, 1
-    ).astype(jnp.bfloat16)
-    part_one = jnp.dot(silu_local, mod_one, preferred_element_type=jnp.float32)
-    part_two = jnp.dot(silu_local, mod_two, preferred_element_type=jnp.float32)
-    summed = lax.psum((part_one, part_two), "seq")
-    return (summed[0], summed[1], silu_local, row_start)
-
-
-def gather_layer(qkv_w, out_w, up_w, down_w):
-    return (
-        lax.all_gather(qkv_w, "seq", axis=0, tiled=True),
-        lax.all_gather(out_w, "seq", axis=0, tiled=True),
-        lax.all_gather(up_w, "seq", axis=0, tiled=True),
-        lax.all_gather(down_w, "seq", axis=0, tiled=True),
-    )
-
-
-def gather_layer_again(qkv_w, out_w, up_w, down_w):
-    return (
-        lax.all_gather(qkv_w, "seq", axis=0, tiled=True),
-        lax.all_gather(out_w, "seq", axis=0, tiled=True),
-        lax.all_gather(up_w, "seq", axis=0, tiled=True),
-        lax.all_gather(down_w, "seq", axis=0, tiled=True),
-    )
 
 
 def partner_values(stacked):
@@ -384,10 +358,516 @@
     return (qkv, out, up, down)
 
 
-def seq_sum(block):
-    for bit in range(bit_count("seq")):
-        block = block + swap(block, "seq", bit)
-    return block
+AHEAD = 2
+
+
+def gather_pieces(shapes):
+    pieces = []
+    for at, (rows, columns) in enumerate(shapes):
+        last = at == len(shapes) - 1
+        if rows > columns // 3:
+            parts = 4 if last else 2
+            tall = rows // parts
+            pieces += [(at, j * tall, tall, 0, columns) for j in range(parts)]
+        elif columns % 256 == 0 and columns > 2048:
+            wide = columns // 2
+            pieces += [(at, 0, rows, j * wide, wide) for j in range(2)]
+        else:
+            pieces.append((at, 0, rows, 0, columns))
+    return pieces
+
+
+def gather_kernel(pieces, count, *refs):
+    shards, partial, condition = refs[:count], refs[count], refs[count + 1]
+    fulls = refs[count + 2 : 2 * count + 2]
+    partials, conditions = refs[2 * count + 2 : 2 * count + 4]
+    held = refs[2 * count + 4 : 3 * count + 4]
+    first_sem, second_sem, rep_sem, pair_sem, local_sem, small_sem = refs[3 * count + 4 :]
+    me, z = lax.axis_index("seq"), lax.axis_index("rep")
+    odd = z & 1
+    first, second = 2 + 2 * odd, 4 - 2 * odd
+
+    barrier = pltpu.get_barrier_semaphore()
+    for mask in range(1, 8):
+        pl.semaphore_signal(barrier, inc=1, device_id={"seq": me ^ mask})
+    for mask in range(1, 4):
+        pl.semaphore_signal(barrier, inc=1, device_id={"rep": z ^ mask})
+    pl.semaphore_wait(barrier, 10)
+
+    small = []
+    for mask in range(1, 8):
+        small.append(pltpu.make_async_remote_copy(
+            partial, partials.at[me], small_sem.at[0, mask], small_sem.at[1, mask],
+            device_id={"seq": me ^ mask}))
+    for mask in range(1, 4):
+        small.append(pltpu.make_async_remote_copy(
+            condition, conditions.at[z], small_sem.at[0, 7 + mask], small_sem.at[1, 7 + mask],
+            device_id={"rep": z ^ mask}))
+    small.append(pltpu.make_async_copy(partial, partials.at[me], small_sem.at[0, 0]))
+    small.append(pltpu.make_async_copy(condition, conditions.at[z], small_sem.at[1, 0]))
+    for copy in small:
+        copy.start()
+
+    def place(owner, piece):
+        at, row, rows, column, columns = piece
+        return fulls[at].at[owner, pl.ds(row, rows), pl.ds(column, columns)]
+
+    def own(piece):
+        at, row, rows, column, columns = piece
+        return shards[at].at[pl.ds(row, rows), pl.ds(column, columns)]
+
+    def send(source, owner, piece, sems, at, target):
+        return pltpu.make_async_remote_copy(
+            source, place(owner, piece), sems.at[0, at], sems.at[1, at], device_id=target)
+
+    firsts, pairs, others, stores = [], [], [], []
+    fetches = [
+        pltpu.make_async_copy(shard, hold, local_sem.at[0, at])
+        for at, (shard, hold) in enumerate(zip(shards, held))
+    ]
+    for copy in fetches:
+        copy.start()
+
+    def begin(at):
+        piece = pieces[at]
+        copy = send(own(piece), me, piece, first_sem, at, {"seq": me ^ first})
+        copy.start()
+        firsts.append(copy)
+        copy = send(own(piece), me, piece, pair_sem.at[0], at, {"seq": me ^ 1})
+        copy.start()
+        pairs.append(copy)
+
+    for at in range(AHEAD):
+        begin(at)
+    for at, copy in enumerate(fetches):
+        copy.wait()
+        stores.append(pltpu.make_async_copy(held[at], fulls[at].at[me], local_sem.at[1, at]))
+        stores[-1].start()
+
+    def forward(at):
+        others[at][0].wait_recv()
+        others[at][1].wait_recv()
+        piece = pieces[at]
+        for which, mask in ((2, first ^ second), (3, second)):
+            owner = me ^ mask
+            copy = send(place(owner, piece), owner, piece, pair_sem.at[which], at, {"seq": me ^ 1})
+            copy.start()
+            pairs.append(copy)
+
+    for at, piece in enumerate(pieces):
+        firsts[at].wait_recv()
+        if at + AHEAD < len(pieces):
+            begin(at + AHEAD)
+        owner = me ^ first
+        two = [
+            send(place(owner, piece), owner, piece, second_sem, at, {"seq": me ^ second}),
+            send(place(owner, piece), owner, piece, rep_sem, at, {"rep": z ^ 1}),
+        ]
+        copy = send(place(owner, piece), owner, piece, pair_sem.at[1], at, {"seq": me ^ 1})
+        for each in two + [copy]:
+            each.start()
+        others.append(two)
+        pairs.append(copy)
+        if at:
+            forward(at - 1)
+    forward(len(pieces) - 1)
+    for copy in firsts:
+        copy.wait_send()
+    for two in others:
+        for copy in two:
+            copy.wait_send()
+    for copy in pairs + stores + small:
+        copy.wait()
+
+
+def gather_weights(shards, partial, condition, cid):
+    shapes = [shard.shape for shard in shards]
+    pieces = gather_pieces(shapes)
+    count = len(shards)
+    dma = pltpu.SemaphoreType.DMA
+    size = len(pieces)
+    outs = [jax.ShapeDtypeStruct((8,) + shape, jnp.bfloat16) for shape in shapes]
+    outs.append(jax.ShapeDtypeStruct((8,) + partial.shape, partial.dtype))
+    outs.append(jax.ShapeDtypeStruct((4,) + condition.shape, condition.dtype))
+    got = pl.pallas_call(
+        functools.partial(gather_kernel, pieces, count),
+        out_shape=outs,
+        in_specs=[pl.BlockSpec(memory_space=pl.ANY)] * (count + 2),
+        out_specs=[pl.BlockSpec(memory_space=pl.ANY)] * len(outs),
+        scratch_shapes=[pltpu.VMEM(shape, jnp.bfloat16) for shape in shapes]
+        + [
+            dma((2, size)), dma((2, size)), dma((2, size)), dma((4, 2, size)), dma((2, count)), dma((2, 11)),
+        ],
+        compiler_params=pltpu.CompilerParams(
+            collective_id=cid, has_side_effects=True,
+        ),
+        name="gather_weights",
+    )(*shards, partial, condition)
+    fulls = [full.reshape(-1, full.shape[2]) for full in got[:count]]
+    return fulls, got[count], got[count + 1]
+
+
+SLOTS = 3
+BACK = 4
+
+
+def reduce_kernel(layers, rows, width, edge, *refs):
+    ins, mods = refs[: 8 * layers], refs[8 * layers]
+    outs, every_mod = refs[8 * layers + 1 : 12 * layers + 1], refs[12 * layers + 1]
+    (
+        left, right, away, pair_in, part,
+        first_in_a, first_in_b, mid_a, mid_b, second_in_a, second_in_b,
+        clip, rep_in, joined, inner_in, final, back_in, wide,
+        mod_in, load_sem, pair_sem, link_sem, rep_sem, back_sem, store_sem, mod_sem,
+    ) = refs[12 * layers + 2 :]
+    me, z = lax.axis_index("seq"), lax.axis_index("rep")
+    core, x, y = me & 1, (me >> 1) & 1, (me >> 2) & 1
+    inner = (z == 1) | (z == 2)
+    outer = (z == 0) | (z == 3)
+
+    barrier = pltpu.get_barrier_semaphore()
+    for mask in range(1, 8):
+        pl.semaphore_signal(barrier, inc=1, device_id={"seq": me ^ mask})
+    for mask in range(1, 4):
+        pl.semaphore_signal(barrier, inc=1, device_id={"rep": z ^ mask})
+    pl.semaphore_wait(barrier, 10)
+
+    mod_copies = [
+        pltpu.make_async_remote_copy(
+            mods, mod_in.at[me], mod_sem.at[0, mask], mod_sem.at[1, mask],
+            device_id={"seq": me ^ mask},
+        )
+        for mask in range(1, 8)
+    ]
+    clip_copies = [
+        pltpu.make_async_remote_copy(
+            every_mod.at[z], every_mod.at[z], mod_sem.at[0, 7 + mask], mod_sem.at[1, 7 + mask],
+            device_id={"rep": z ^ mask},
+        )
+        for mask in range(1, 4)
+    ]
+    for copy in mod_copies:
+        copy.start()
+    mod_in[me] = mods[...]
+
+    spans, start = [], 0
+    for layer in range(layers):
+        for kind in range(4):
+            shape = outs[4 * layer + kind].shape
+            count = shape[0] // rows * (shape[1] // width)
+            spans.append((layer, kind, start, count))
+            start += count
+    total = start
+
+    def loads(block, slot):
+        for layer, kind, first, count in spans:
+            @pl.when((block >= first) & (block < first + count))
+            def _():
+                source = ins[8 * layer + kind]
+                if kind == 3:
+                    source = source.at[:, :, block - first]
+                pltpu.make_async_copy(source, left.at[slot], load_sem.at[0, slot]).start()
+                source = ins[8 * layer + 4 + kind]
+                if kind in (0, 2):
+                    column = pl.multiple_of((block - first) * width, width)
+                    source = source.at[:, pl.ds(column, width)]
+                pltpu.make_async_copy(source, right.at[slot], load_sem.at[1, slot]).start()
+
+    def wait_loads(slot):
+        pltpu.make_async_copy(ins[0], left.at[slot], load_sem.at[0, slot]).wait()
+        pltpu.make_async_copy(ins[5], right.at[slot], load_sem.at[1, slot]).wait()
+
+    def store(block, slot):
+        for layer, kind, first, count in spans:
+            @pl.when((block >= first) & (block < first + count))
+            def _():
+                target = outs[4 * layer + kind]
+                if kind == 3:
+                    row = pl.multiple_of((block - first) * rows, rows)
+                    target = target.at[pl.ds(row, rows)]
+                elif kind in (0, 2):
+                    column = pl.multiple_of((block - first) * width, width)
+                    target = target.at[:, pl.ds(column, width)]
+                pltpu.make_async_copy(wide.at[slot], target, store_sem.at[slot]).start()
+
+    def to_seq(source, target, which, slot, mask):
+        return pltpu.make_async_remote_copy(
+            source, target, link_sem.at[0, which, slot], link_sem.at[1, which, slot],
+            device_id={"seq": me ^ mask},
+        )
+
+    def pair_copy(t):
+        slot = lax.rem(t, 2)
+        return pltpu.make_async_remote_copy(
+            away, pair_in.at[slot], pair_sem.at[0, slot], pair_sem.at[1, slot],
+            device_id={"seq": me ^ 1},
+        )
+
+    def first_copies(t):
+        slot, block = lax.rem(t, SLOTS), lax.rem(t - 1, SLOTS)
+        return (
+            to_seq(part.at[block, :, 1 - x, :, pl.ds(0, edge)], first_in_a.at[slot], 0, slot, 2),
+            to_seq(
+                part.at[block, 1 - y, :, :, pl.ds(edge, width - edge)],
+                first_in_b.at[slot], 1, slot, 4,
+            ),
+        )
+
+    def second_copies(t):
+        slot, block = lax.rem(t, SLOTS), lax.rem(t, 2)
+        return (
+            to_seq(mid_a.at[block, 1 - y], second_in_a.at[slot], 2, slot, 4),
+            to_seq(mid_b.at[block, 1 - x], second_in_b.at[slot], 3, slot, 2),
+        )
+
+    def rep_copy(t):
+        slot = lax.rem(t, SLOTS)
+        return pltpu.make_async_remote_copy(
+            clip.at[lax.rem(t, 2)], rep_in.at[slot], rep_sem.at[0, 0, slot], rep_sem.at[1, 0, slot],
+            device_id={"rep": z ^ 1},
+        )
+
+    def inner_copy(t):
+        slot = lax.rem(t, SLOTS)
+        return pltpu.make_async_remote_copy(
+            joined.at[lax.rem(t, 2)], inner_in.at[slot],
+            rep_sem.at[0, 1, slot], rep_sem.at[1, 1, slot],
+            device_id={"rep": z ^ 3},
+        )
+
+    def back_copy(t):
+        slot = lax.rem(t, BACK)
+        return pltpu.make_async_remote_copy(
+            final.at[lax.rem(t, 2)], back_in.at[slot], back_sem.at[0, slot], back_sem.at[1, slot],
+            device_id={"rep": z ^ 1},
+        )
+
+    loads(0, 0)
+
+    def turn(t, carry):
+        def stage(back):
+            return (t >= back) & (t < total + back)
+
+        now2, was2 = lax.rem(t, 2), lax.rem(t + 1, 2)
+        was3 = lax.rem(t + 2, SLOTS)
+
+        @pl.when(t + 1 < total)
+        def _():
+            loads(t + 1, was2)
+
+        @pl.when(stage(1))
+        def _():
+            for copy in first_copies(t):
+                copy.start()
+
+        @pl.when(stage(2))
+        def _():
+            block = lax.rem(t + 1, SLOTS)
+            for at in range(2):
+                mid_a[now2, at] = part[block, at, x, :, :edge] + first_in_a[was3, at]
+                mid_b[now2, at] = part[block, y, at, :, edge:] + first_in_b[was3, at]
+            for copy in second_copies(t):
+                copy.start()
+
+        @pl.when(stage(3))
+        def _():
+            clip[now2, :, :edge] = mid_a[was2, y] + second_in_a[was3]
+            clip[now2, :, edge:] = mid_b[was2, x] + second_in_b[was3]
+
+            @pl.when(outer)
+            def _():
+                rep_copy(t).start()
+
+        @pl.when(stage(4) & inner)
+        def _():
+            joined[now2] = clip[was2] + rep_in[was3]
+            inner_copy(t).start()
+
+        @pl.when(stage(5) & inner)
+        def _():
+            final[now2] = joined[was2] + inner_in[was3]
+            back_copy(t).start()
+
+        @pl.when(stage(6))
+        def _():
+            @pl.when(inner)
+            def _():
+                wide[now2] = final[was2].astype(jnp.float32)
+
+            @pl.when(outer)
+            def _():
+                wide[now2] = back_in[lax.rem(t + 3, BACK)].astype(jnp.float32)
+
+            store(t - 6, now2)
+
+        @pl.when(t < total)
+        def _():
+            wait_loads(now2)
+            slot3 = lax.rem(t, SLOTS)
+
+            def product(which):
+                def columns(j, carry):
+                    at = pl.ds(pl.multiple_of(j * (width // 3), width // 3), width // 3)
+                    block = left[now2, :, which]
+                    four, _, depth = block.shape
+                    got = jnp.dot(
+                        block.reshape(four * rows, depth), right[now2, :, at],
+                        preferred_element_type=jnp.float32,
+                    ).astype(jnp.bfloat16)
+                    return at, got.reshape(four, rows, width // 3)
+                return columns
+
+            def away_columns(j, carry):
+                at, got = product(1 - core)(j, carry)
+                away[:, :, at] = got
+                return carry
+
+            lax.fori_loop(0, 3, away_columns, 0)
+            pair_copy(t).start()
+
+            def kept_columns(j, carry):
+                at, got = product(core)(j, carry)
+                part[slot3, 0, :, :, at] = got[:2]
+                part[slot3, 1, :, :, at] = got[2:]
+                return carry
+
+            lax.fori_loop(0, 3, kept_columns, 0)
+            pair_copy(t).wait()
+
+            def add(j, carry):
+                part[slot3, j // 2, j % 2] = part[slot3, j // 2, j % 2] + pair_in[now2, j]
+                return carry
+
+            lax.fori_loop(0, 4, add, 0)
+
+        @pl.when(stage(1))
+        def _():
+            for copy in first_copies(t):
+                copy.wait()
+
+        @pl.when(stage(2))
+        def _():
+            for copy in second_copies(t):
+                copy.wait()
+
+        @pl.when(stage(3))
+        def _():
+            @pl.when(outer)
+            def _():
+                rep_copy(t).wait_send()
+
+            @pl.when(inner)
+            def _():
+                rep_copy(t).wait_recv()
+
+        @pl.when(stage(4) & inner)
+        def _():
+            inner_copy(t).wait()
+
+        @pl.when(stage(5))
+        def _():
+            @pl.when(inner)
+            def _():
+                back_copy(t).wait_send()
+
+            @pl.when(outer)
+            def _():
+                back_copy(t).wait_recv()
+
+        @pl.when(stage(6))
+        def _():
+            pltpu.make_async_copy(wide.at[now2], outs[1], store_sem.at[now2]).wait()
+
+        return carry
+
+    lax.fori_loop(0, 2, turn, 0)
+    for copy in mod_copies:
+        copy.wait()
+    mod_total = mod_in[0].astype(jnp.float32)
+    for device in range(1, 8):
+        mod_total += mod_in[device].astype(jnp.float32)
+    every_mod[z] = mod_total.astype(every_mod.dtype)
+    for copy in clip_copies:
+        copy.start()
+    lax.fori_loop(2, total + 6, turn, 0)
+    for copy in clip_copies:
+        copy.wait()
+
+
+def reduce_grads(layers, mods, cid):
+    tokens = layers[0][4].shape[0]
+    rows, width = layers[0][0].shape[2], layers[0][5].shape[1]
+    edge = width * 5 // 9 // 128 * 128
+    low = jnp.bfloat16
+    outs = []
+    for ops in layers:
+        for kind in range(4):
+            tall = ops[kind].shape[2] if kind == 3 else 1
+            outs.append(jax.ShapeDtypeStruct((tall * rows, ops[4 + kind].shape[1]), jnp.float32))
+    outs.append(jax.ShapeDtypeStruct((4,) + mods.shape, mods.dtype))
+    vm = pltpu.VMEM
+    dma = pltpu.SemaphoreType.DMA
+    flops = sum(2 * tokens * 8 * o.size for o in outs[:-1])
+    got = pl.pallas_call(
+        functools.partial(reduce_kernel, len(layers), rows, width, edge),
+        out_shape=outs,
+        in_specs=[pl.BlockSpec(memory_space=pl.ANY)] * (8 * len(layers))
+        + [pl.BlockSpec(memory_space=vm)],
+        out_specs=[pl.BlockSpec(memory_space=pl.ANY)] * (4 * len(layers))
+        + [pl.BlockSpec(memory_space=vm)],
+        scratch_shapes=[
+            vm((2, 4, 2, rows, tokens), low),
+            vm((2, tokens, width), low),
+            vm((4, rows, width), low),
+            vm((2, 4, rows, width), low),
+            vm((SLOTS, 2, 2, rows, width), low),
+            vm((SLOTS, 2, rows, edge), low),
+            vm((SLOTS, 2, rows, width - edge), low),
+            vm((2, 2, rows, edge), low),
+            vm((2, 2, rows, width - edge), low),
+            vm((SLOTS, rows, edge), low),
+            vm((SLOTS, rows, width - edge), low),
+            vm((2, rows, width), low),
+            vm((SLOTS, rows, width), low),
+            vm((2, rows, width), low),
+            vm((SLOTS, rows, width), low),
+            vm((2, rows, width), low),
+            vm((BACK, rows, width), low),
+            vm((2, rows, width), jnp.float32),
+            vm((8,) + mods.shape, mods.dtype),
+            dma((2, 2)),
+            dma((2, 2)),
+            dma((2, 4, SLOTS)),
+            dma((2, 2, SLOTS)),
+            dma((2, BACK)),
+            dma((2,)),
+            dma((2, 11)),
+        ],
+        compiler_params=pltpu.CompilerParams(
+            collective_id=cid, has_side_effects=True, vmem_limit_bytes=48 << 20
+        ),
+        cost_estimate=pl.CostEstimate(flops=flops, bytes_accessed=4 * sum(o.size for o in outs), transcendentals=0),
+        name="reduce_grads",
+    )(*[op for ops in layers for op in ops], mods)
+    return [tuple(got[4 * at : 4 * at + 4]) for at in range(len(layers))], got[-1]
+
+
+def turned_rows(operand, tall):
+    left = turned(operand)
+    rows = left.shape[0] // 8 // tall
+    shape = (4, 2, rows, left.shape[1]) if tall == 1 else (4, 2, tall, rows, left.shape[1])
+    return left.reshape(shape)
+
+
+def reduce_operands(grad_pairs):
+    qkv_pair, out_pair, up_pair, down_pair = grad_pairs
+    tall = down_pair[0].shape[-1] // down_pair[1].shape[-1]
+    return (
+        turned_rows(qkv_pair[0], 1),
+        turned_rows(out_pair[0], 1),
+        turned_rows(up_pair[0], 1),
+        turned_rows(down_pair[0], tall),
+    ) + tuple(flat(pair[1]) for pair in grad_pairs)
 
 
 def per_device(
@@ -405,73 +885,85 @@
     down_second,
     cotangent,
 ):
-    clip_count = frames_in.shape[0]
-    frame_dev = frames_in.shape[2]
-    half_places = frames_in.shape[3]
-    features = frames_in.shape[4]
+    clip_count, _, frame_dev, half_places, features = frames_in.shape
+    fused = lax.axis_size("seq") == 8 and lax.axis_size("rep") == 4 and clip_count == 1
     start_stream = frames_in.reshape(clip_count, frame_dev, half_places, features).astype(
         jnp.float32
     )
-    mod_one, mod_two, silu_local, row_start = modulations(conditioning, mod_first, mod_second)
-    weights_one = gather_layer(qkv_first, out_first, up_first, down_first)
-    spatial_out, unused_one = forward_layer(start_stream, mod_one, weights_one, True)
-    weights_two = gather_layer(qkv_second, out_second, up_second, down_second)
-    temporal_out, unused_two = forward_layer(to_places(spatial_out), mod_two, weights_two, False)
+    row_count = mod_first.shape[0]
+    row_start = lax.axis_index("seq") * row_count
+    mod_width = mod_first.shape[1]
+    rows_of = lambda whole: lax.dynamic_slice_in_dim(whole, row_start, row_count, 1)
+    silu_local = rows_of(jax.nn.silu(conditioning)).astype(jnp.bfloat16)
+    partial_mod = jnp.concatenate(
+        [
+            jnp.dot(silu_local, mod_first, preferred_element_type=jnp.float32),
+            jnp.dot(silu_local, mod_second, preferred_element_type=jnp.float32),
+        ],
+        1,
+    )
+    shards = (
+        qkv_first, out_first, up_first, down_first,
+        qkv_second, out_second, up_second, down_second,
+    )
+    if fused:
+        weights, partials, conditions = gather_weights(
+            shards, partial_mod.reshape(-1, 128), conditioning.reshape(-1, 128), 0
+        )
+        modulation = jnp.sum(partials, 0).reshape(1, -1)
+        every_silu = rows_of(jax.nn.silu(conditions.reshape(-1, features))).astype(jnp.bfloat16)
+    else:
+        weights = [lax.all_gather(shard, "seq", axis=0, tiled=True) for shard in shards]
+        modulation = lax.psum(partial_mod, "seq")
+        every_silu = lax.all_gather(silu_local, "rep", axis=0, tiled=True)
+    mod_one, mod_two = modulation[:, :mod_width], modulation[:, mod_width:]
+    weights_one, weights_two = weights[:4], weights[4:]
+    spatial_out, state_one = forward_layer(start_stream, mod_one, weights_one, True)
+    placed = to_places(spatial_out)
+    temporal_out, state_two = forward_layer(placed, mod_two, weights_two, False)
     block_out = to_frames(temporal_out, frame_dev)
-    mod_one, mod_two, silu_local, row_start = modulations(conditioning, mod_first, mod_second)
-    again_one = gather_layer_again(qkv_first, out_first, up_first, down_first)
-    spatial_again, state_one = forward_layer(start_stream, mod_one, again_one, True)
-    again_two = gather_layer_again(qkv_second, out_second, up_second, down_second)
-    placed_again = to_places(spatial_again)
-    unused_three, state_two = forward_layer(placed_again, mod_two, again_two, False)
     cotangent_sites = to_places(cotangent.reshape(clip_count, frame_dev, half_places, features))
     placed_grad, mod_grad_two, pairs_two = backward_layer(
-        cotangent_sites, placed_again, mod_two, again_two, state_two, False
-    )
-    row_attn = qkv_first.shape[0]
-    grads_two = layer_grads(pairs_two)
+        cotangent_sites, placed, mod_two, weights_two, state_two, False
+    )
     spatial_grad = to_frames(placed_grad, frame_dev)
     stream_grad, mod_grad_one, pairs_one = backward_layer(
-        spatial_grad, start_stream, mod_one, again_one, state_one, True
-    )
-    grads_one = layer_grads(pairs_one)
-    mod_total = lax.psum(
-        jnp.concatenate([mod_grad_one, mod_grad_two], 1).astype(jnp.bfloat16), "seq"
-    ).astype(jnp.bfloat16)
-    mod_width = mod_grad_one.shape[1]
+        spatial_grad, start_stream, mod_one, weights_one, state_one, True
+    )
+    mod_grads = jnp.concatenate([mod_grad_one, mod_grad_two], 1).astype(jnp.bfloat16)
+    if fused:
+        (grads_two, grads_one), every_mod = reduce_grads(
+            [reduce_operands(pairs_two), reduce_operands(pairs_one)],
+            mod_grads.reshape(-1, 128),
+            1,
+        )
+        every_mod = every_mod.reshape(-1, 2 * mod_width)
+        mod_total = lax.dynamic_slice_in_dim(every_mod, lax.axis_index("rep"), 1, 0)
+    else:
+        grads_two, grads_one = layer_grads(pairs_two), layer_grads(pairs_one)
+        mod_total = lax.psum(mod_grads, "seq").astype(jnp.bfloat16)
+        every_mod = lax.all_gather(mod_total, "rep", axis=0, tiled=True)
     low_one, low_two = mod_total[:, :mod_width], mod_total[:, mod_width:]
-    every_mod = lax.all_gather(mod_total, "rep", axis=0, tiled=True)
-    every_silu = lax.all_gather(silu_local, "rep", axis=0, tiled=True)
-    mod_weights = jnp.einsum(
-        "cd,ce->de", every_silu, every_mod, preferred_element_type=jnp.float32
+    mod_weight_one = jnp.einsum(
+        "cd,ce->de", every_silu, every_mod[:, :mod_width], preferred_element_type=jnp.float32
+    )
+    mod_weight_two = jnp.einsum(
+        "cd,ce->de", every_silu, every_mod[:, mod_width:], preferred_element_type=jnp.float32
     )
     silu_grad = jnp.einsum("ce,de->cd", low_one, mod_first, preferred_element_type=jnp.float32)
     silu_grad = silu_grad + jnp.einsum(
         "ce,de->cd", low_two, mod_second, preferred_element_type=jnp.float32
     )
-    condition_local = lax.dynamic_slice_in_dim(conditioning, row_start, row_attn, 1)
-    condition_grad = jax.vjp(jax.nn.silu, condition_local)[1](silu_grad)[0]
-    summed = (
-        (mod_weights[:, :mod_width],)
-        + tuple(grads_one)
-        + (mod_weights[:, mod_width:],)
-        + tuple(grads_two)
-    )
+    condition_grad = jax.vjp(jax.nn.silu, rows_of(conditioning))[1](silu_grad)[0]
     out_shape = (clip_count, 1, frame_dev, half_places, features)
     return (
         block_out.reshape(out_shape),
         stream_grad.reshape(out_shape),
         condition_grad,
-        summed[0],
-        summed[1],
-        summed[2],
-        summed[3],
-        summed[4],
-        summed[5],
-        summed[6],
-        summed[7],
-        summed[8],
-        summed[9],
+        mod_weight_one,
+        *grads_one,
+        mod_weight_two,
+        *grads_two,
     )
 
 

time: 1450 us -> 1090 us (0.75)
  waiting for transfers between devices: 573 us -> 8.11 us
  Pallas kernels: 0 us -> 522 us
  other arithmetic: 147 us -> 65.6 us
  matrix products: 328 us -> 249 us
  blocking collectives: 77.7 us -> 0 us
  starting transfers between devices: 90.3 us -> 18.8 us
  between operations: 17 us -> 2.12 us
    pallas_call x0 -> x2, Pallas kernels: none -> 522 us  [the longest x1 312 us: reduce_grads(): pl.pallas_call(functools.partial(reduce_kernel, len(layers), rows, width,...]
    ppermute x90 -> x0, waiting for transfers between devices: 394 us -> none  [swap(): lax.ppermute(block, axis, [(at, at ^ 1 << bit) for at in range(count)])]
    all_gather x8 -> x0, waiting for transfers between devices: 175 us -> none  [the longest x2 102 us: gather_layer(): lax.all_gather(down_w, 'seq', axis=0, tiled=True)]
    ppermute x90 -> x0, starting transfers between devices: 73.5 us -> none  [swap(): lax.ppermute(block, axis, [(at, at ^ 1 << bit) for at in range(count)])]
    dot_general x31 -> x4, matrix products: 83.1 us -> 10.3 us  [the longest x1 3.59 us: per_device(): jnp.einsum('cd,ce->de', every_silu, every_mod[:, :mod_width], preferred_e...]
    psum x2 -> x0, blocking collectives: 51.8 us -> none  [the longest x1 26.5 us: modulations(): summed = lax.psum((part_one, part_two), 'seq')]
    convert_element_type x66 -> x0, other arithmetic: 51.4 us -> none  [the longest x14 38.7 us: spread_rows_out(): held = kept.astype(jnp.bfloat16)]
    concatenate x9 -> x15, local copies, waits for them, and re-layouts: 32.9 us -> 60.6 us  [backward_layer(): jnp.concatenate([component.reshape(clip_count, seq_count, seq_len, featur...]
  transfers between devices with their start and end apart: 104 -> 6, of which waited for: 61 -> 1; matrix products, arithmetic and copies ran while one was open for 35% -> 23% of each run, Pallas kernels for 0% -> 0%
where the time goes in v2:
time: 1090 us; the launch traced here: 1080 us
  Pallas kernels  522 us (48%)
  matrix products  249 us (23%)
  local copies, waits for them, and re-layouts  214 us (20%)
  other arithmetic  65.6 us (6%)
  starting transfers between devices  18.8 us (2%)
    pallas_call x1, Pallas kernels, reduce_grads(): pl.pallas_call(functools.partial(reduce_kernel, len(layers), rows, width,...  312 us
    pallas_call x1, Pallas kernels, gather_weights(): pl.pallas_call(functools.partial(gather_kernel, pieces, count), out_shape...  210 us
    dot_general x8, matrix products, project_back(): jnp.einsum('csle,de->csld', incoming, right_operand, preferred_element_ty...  81.9 us
    dot_general x8, matrix products, project(): jnp.einsum('csld,de->csle', left_operand, right_operand, preferred_elemen...  78.4 us
    concatenate x15, local copies, waits for them, and re-layouts, backward_layer(): jnp.concatenate([component.reshape(clip_count, seq_count, seq_len, featur...  60.6 us
    another operation x8, local copies, waits for them, and re-layouts  33.6 us
    unnamed x221, local copies, waits for them, and re-layouts  29 us
    dot_general x2, matrix products, forward_layer(): jnp.einsum('cshlm,csmhe->cslhe', attention_low, values_all, preferred_ele...  25.8 us
  transfers between devices with their start and end apart: 6, of which 1 were waited for; matrix products, arithmetic and copies ran while one was open for 23% of the time, Pallas kernels for 0%

profile of v2, /device:TPU:0, one launch (start us, length us, event | category | flops | bytes accessed | tf_op | source)
XLA Modules:
  0.0 1080.1 jit_solution(4068449142916477674)
XLA Ops:
  5.4 209.8 %gather_weights.1 = (bf16[8,144,3456]{2,1,0:T(8,128)(2,1)}, bf16[8,144,1152]{2,1,0:T(8,128)(2,1)}, bf16[8,144,4608]{2,1,0:T(8,128)(2,1)}, bf16[8,576,1152]{2,1,0...) custom-call(bf16[144,3456]{1,0:T(8,128)(2,1)} %refs_0_.1, ...), custom_call_target="tpu_custom_call" | custom-call | tf_op jit(solution)/shard_map/gather_weights/pallas_call | solution.py:492
  217.9 8.9 fusion.17
  232.5 4.5 all-to-all-start.2
  253.1 4.9 fusion.152
  261.3 21.9 %fusion.80 = bf16[4,16,72,128]{3,2,1,0:T(8,128)(2,1)} fusion(bf16[1,4,128,16,72]{2,4,3,1,0:T(8,128)(2,1)} %bitcast.380, bf16[1,4,128,16,72]{2,4,3,1,0:T(8,128)(2,1)} %bitcast.378, f32[4,16,128]{2,1,0:T(8,128)S(1)} %get-tuple-element.108, f32[4,16,128,256]{3,2,1,0:T(8,128)} %copy-done.13), kind=kOutput, calls=%fused_computation.149 | convolution fusion | flops 317792512 | bytes 11960320 | tf_op jit(solution)/shard_map/cshlm,csmhe->cslhe/dot_general | solution.py:118
  283.3 5.6 fusion.148
  290.0 15.2 %multiply_convert_fusion.1 = (bf16[4,128,4608]{2,1,0:T(8,128)(2,1)S(1)}, f32[4,128,4608]{2,1,0:T(8,128)}) fusion(bf16[4,128,1152]{2,1,0:T(8,128)(2,1)S(1)} %add_convert_fusion.7, bf16[1152,4608,1]{1,0,2:T(8,128)(2,1)} %bitcast.405), kind=kOutput, calls=%fused_computation.21 | convolution fusion | flops 5457051648 | bytes 25952256 | tf_op jit(solution)/shard_map/csld,de->csle/dot_general | solution.py:43
  305.3 7.6 add_convert_fusion.6
  314.1 4.4 all-to-all-start
  327.1 8.1 all-to-all-done
  338.7 4.1 copy.335
  344.4 8.7 fusion.18
  354.8 5.7 reshape.1186
  360.5 5.7 reshape.1187
  373.2 5.1 reshape.1185
  378.2 3.9 convert_bitcast_fusion.1
  391.4 5.8 fusion.147
  398.1 14.2 %multiply_convert_fusion = (bf16[32,16,4608]{2,1,0:T(8,128)(2,1)S(1)}, f32[32,16,4608]{2,1,0:T(8,128)}) fusion(bf16[32,16,1152]{2,1,0:T(8,128)(2,1)S(1)} %add_convert_fusion.4, bf16[1152,4608,1]{1,0,2:T(8,128)(2,1)} %bitcast.413), kind=kOutput, calls=%fused_computation.20 | convolution fusion | flops 5457051648 | bytes 25952256 | tf_op jit(solution)/shard_map/csld,de->csle/dot_general | solution.py:43
  412.2 18.2 %fusion.15 = bf16[32,16,4608]{2,1,0:T(8,128)(2,1)} fusion(f32[32,16,4608]{2,1,0:T(8,128)} %get-tuple-element.119, bf16[4608,1152,1]{1,0,2:T(8,128)(2,1)} %bitcast.411, bf16[32,16,1152]{2,0,1:T(8,128)(2,1)S(1)} %bitcast.384), kind=kOutput, calls=%fused_computation.19 | convolution fusion | flops 5483003904 | bytes 25952256 | tf_op jit(solution)/shard_map/csle,de->csld/dot_general | solution.py:49
  430.4 11.6 %multiply_reduce_fusion.13 = (f32[32,16]{1,0:T(8,128)S(1)}, f32[32,16,1152]{2,1,0:T(8,128)S(1)}) fusion(f32[32,16,1152]{2,1,0:T(8,128)S(1)} %get-tuple-element.80, f32[1152]{0:T(1024)S(1)} %get-tuple-element.65, f32[32,16]{1,0:T(8,128)S(1)} %broadcast_multiply_fusion, bf16[32,16,4608]{2,1,0:T(8,128)(2,1)} %fusion.15, bf16[1152,4608,1]{1,0,2:T(8,128)(2,1)} %bitcast.414), kind=kOutput, calls=%fused_computation.119 | convolution fusion | flops 5438176768 | bytes 20062720 | tf_op jit(solution)/shard_map/csle,de->csld/dot_general | solution.py:49
  444.4 12.5 %multiply_reduce_fusion.4 = (bf16[1152]{0:T(1024)(128)(2,1)}, bf16[32,16,1152]{2,1,0:T(8,128)(2,1)}, bf16[1152]{0:T(1024)(128)(2,1)}, f32[32,16,1152]{2,1,0:T(8,128)S(1)}) fusion(f32[32,16,1152]{2,1,0:T(8,128)S(1)} %copy-done.46, f32[32,16,1152]{2,1,0:T(8,128)S(1)} %get-tuple-element.80, f32[1152]{0:T(1024)S(1)} %get-tuple-element.63, ...), kind=kOutput, calls=%fused_computation.99 | convolution fusion | flops 5444663296 | bytes 28333568 | tf_op jit(solution)/shard_map/csld,de->csle/dot_general | solution.py:43
  462.5 4.6 reshape.1193
  467.1 5.4 multiply_reduce_fusion.2
  489.0 4.6 concatenate.119
  497.1 4.6 concatenate.120
  502.0 9.9 multiply_reduce_fusion.12
  518.2 4.7 all-to-all-start.3
  531.8 6.6 copy.388
  543.0 4.6 concatenate.129
  547.6 4.6 concatenate.130
  552.2 4.6 concatenate.131
  560.6 4.6 reshape_reshape.8
  565.5 6.6 copy.380
  581.9 4.4 all-to-all-start.1
  587.9 16.4 %fusion.8 = bf16[4,128,4608]{2,1,0:T(8,128)(2,1)} fusion(f32[4,128,4608]{2,1,0:T(8,128)} %get-tuple-element.112, bf16[4,128,1152]{2,1,0:T(8,128)(2,1)S(1)} %bitcast.387, bf16[4608,1152,1]{1,0,2:T(8,128)(2,1)} %bitcast.407), kind=kOutput, calls=%fused_computation.12 | convolution fusion | flops 5483003904 | bytes 25952256 | tf_op jit(solution)/shard_map/csle,de->csld/dot_general | solution.py:49
  604.3 11.5 %multiply_reduce_fusion.11 = (f32[4,128]{1,0:T(4,128)S(1)}, f32[4,128,1152]{2,1,0:T(8,128)S(1)}) fusion(f32[4,128,1152]{2,1,0:T(8,128)S(1)} %copy-done.7, f32[1152]{0:T(1024)S(1)} %copy-done.65, f32[4,128]{1,0:T(4,128)S(1)} %copy-done.74, bf16[4,128,4608]{2,1,0:T(8,128)(2,1)} %fusion.8, bf16[1152,4608,1]{1,0,2:T(8,128)(2,1)} %bitcast.406), kind=kOutput, calls=%fused_computation.113 | convolution fusion | flops 5438176768 | bytes 20062720 | tf_op jit(solution)/shard_map/csle,de->csld/dot_general | solution.py:49
  628.5 22.3 %convolution_bitcast_fusion = f32[1,4,256,16,72]{2,4,3,1,0:T(8,128)} fusion(bf16[4,128,16,72]{1,3,2,0:T(8,128)(2,1)} %bitcast.385, f32[4,16,128]{2,1,0:T(8,128)S(1)} %copy-done.63, f32[4,16,128,256]{3,2,1,0:T(8,128)} %copy-done.13), kind=kOutput, calls=%fused_computation.130 | convolution fusion | flops 312484096 | bytes 14319616 | tf_op jit(solution)/shard_map/cshlm,cslhe->csmhe/dot_general | solution.py:195
  650.8 7.5 multiply_reduce_fusion
  675.4 4.3 copy.398
  679.7 4.6 reshape.1255
  684.3 4.2 fusion.48
  696.3 4.4 fusion.40
  700.7 4.3 copy.399
  707.4 4.3 copy.400
  714.1 9.7 fusion.54
  725.2 4.6 reshape.1256
  729.8 4.6 reshape.1257
  740.7 312.3 %reduce_grads.1 = (f32[144,3456]{1,0:T(8,128)}, f32[144,1152]{1,0:T(8,128)S(1)}, f32[144,4608]{1,0:T(8,128)}, f32[576,1152]{1,0:T(8,128)}, f32[144,3456]{1,0:T(8...) custom-call(bf16[4,2,144,512]{3,2,1,0:T(8,128)(2,1)S(1)} %bitcast.33, ...), custom_call_target="tpu_custom_call" | custom-call | flops 32614907904 | bytes 16146432 | tf_op jit(solution)/shard_map/reduce_grads/pallas_call | solution.py:811
  (352 shorter events, 206.8 us)
Async XLA Ops:
  5.4 211.1 %copy-start.8 = (bf16[1,1,4,128,1152]{4,3,2,1,0:T(8,128)(2,1)S(1)}, bf16[1,1,4,128,1152]{4,3,2,1,0:T(8,128)(2,1)}, u32[]{:S(2)}) copy-start(bf16[1,1,4,128,1152]{4,3,2,1,0:T(8,128)(2,1)} %param.13) | copy-start | bytes 3538948
  216.5 10.2 copy-start.66
  216.5 10.2 copy-start.75
  216.5 66.7 %copy-start.56 = (f32[1152]{0:T(1024)}, f32[1152]{0:T(1024)S(1)}, u32[]{:S(2)}) copy-start(f32[1152]{0:T(1024)S(1)} %get-tuple-element.74) | copy-start | bytes 13828
  216.5 72.7 %copy-start.64 = (f32[1152]{0:T(1024)}, f32[1152]{0:T(1024)S(1)}, u32[]{:S(2)}) copy-start(f32[1152]{0:T(1024)S(1)} %get-tuple-element.70) | copy-start | bytes 13828
  216.5 88.7 %copy-start.70 = (f32[1152]{0:T(1024)}, f32[1152]{0:T(1024)S(1)}, u32[]{:S(2)}) copy-start(f32[1152]{0:T(1024)S(1)} %get-tuple-element.71) | copy-start | bytes 13828
  216.5 127.3 %copy-start.58 = (f32[1152]{0:T(1024)}, f32[1152]{0:T(1024)S(1)}, u32[]{:S(2)}) copy-start(f32[1152]{0:T(1024)S(1)} %get-tuple-element.67) | copy-start | bytes 13828
  216.6 127.3 %copy-start.68 = (f32[1152]{0:T(1024)}, f32[1152]{0:T(1024)S(1)}, u32[]{:S(2)}) copy-start(f32[1152]{0:T(1024)S(1)} %get-tuple-element.66) | copy-start | bytes 13828
  217.4 9.4 copy-start.78
  217.8 8.9 copy-start.84
  217.9 8.9 copy-start.86
  230.4 13.8 %collective-permute-start = (bf16[2,1,4,128,1152]{4,3,2,1,0:T(8,128)(2,1)}, bf16[2,1,4,128,1152]{4,3,2,1,0:T(8,128)(2,1)}, u32[]{:S(2)}, u32[]{:S(2)}) collective-permute-start(bf16[2,1,4,128,1152]{4,3,2,1,0:T(8,128)(2,1)} %pad_maximum_fusion.2), channel_id=1, source_target_pairs={{0,1},{1,0},{2,3},{3,2},{4,5},{5,4},{6,7},{7,6},{8,9},{9,8},{10,11... | collective-permute-start | bytes 7077896 | tf_op jit(solution)/shard_map/ppermute | solution.py:24
  232.5 81.5 %all-to-all-start.2 = ((bf16[1,1,4,8,16,1152]{5,4,2,1,0,3:T(8,128)(2,1)}), bf16[1,1,4,8,16,1152]{5,4,2,1,0,3:T(8,128)(2,1)}, u32[]{:S(2)}, u32[]{:S(2)}) async-start(bf16[1,1,4,8,16,1152]{5,4,2,1,0,3:T(8,128)(2,1)} %copy.346), calls=%async_computation.2 | async-start | bytes 2359296 | tf_op jit(solution)/shard_map/all_to_all | solution.py:68
  253.1 5.8 copy-start.13
  259.0 24.3 %copy-start.62 = (f32[4,16,128]{2,1,0:T(8,128)}, f32[4,16,128]{2,1,0:T(8,128)S(1)}, u32[]{:S(2)}) copy-start(f32[4,16,128]{2,1,0:T(8,128)S(1)} %get-tuple-element.108) | copy-start | bytes 98308
  288.8 16.4 %copy-start.6 = (f32[4,128,1152]{2,1,0:T(8,128)}, f32[4,128,1152]{2,1,0:T(8,128)S(1)}, u32[]{:S(2)}) copy-start(f32[4,128,1152]{2,1,0:T(8,128)S(1)} %get-tuple-element.82) | copy-start | bytes 7077892
  289.2 16.0 %copy-start.82 = (f32[4,128]{1,0:T(4,128)}, f32[4,128]{1,0:T(4,128)S(1)}, u32[]{:S(2)}) copy-start(f32[4,128]{1,0:T(4,128)S(1)} %multiply_reduce_fusion.16) | copy-start | bytes 6148
  289.2 16.0 %copy-start.80 = (f32[4,128]{1,0:T(4,128)}, f32[4,128]{1,0:T(4,128)S(1)}, u32[]{:S(2)}) copy-start(f32[4,128]{1,0:T(4,128)S(1)} %fusion.114) | copy-start | bytes 6148
  289.2 16.0 %slice-start.2 = ((s8[10616832]{0:T(1024)(128)(4,1)}), s8[4194304]{0:T(1024)(128)(4,1)S(1)}, s32[]{:S(2)}) async-start(s8[10616832]{0:T(1024)(128)(4,1)} %bitcast.408), calls=%async_computation.6 | async-start | bytes 8388608
  290.0 15.2 %copy-start.38 = (bf16[4,128,1152]{2,1,0:T(8,128)(2,1)}, bf16[4,128,1152]{2,1,0:T(8,128)(2,1)S(1)}, u32[]{:S(2)}) copy-start(bf16[4,128,1152]{2,1,0:T(8,128)(2,1)S(1)} %add_convert_fusion.7) | copy-start | bytes 3538948
  290.0 15.3 %slice-start.3 = ((s8[10616832]{0:T(1024)(128)(4,1)}), s8[4194304]{0:T(1024)(128)(4,1)S(1)}, s32[]{:S(2)}) async-start(s8[10616832]{0:T(1024)(128)(4,1)} %bitcast.408), calls=%async_computation.7 | async-start | bytes 8388608
  290.0 15.3 %slice-start.4 = ((s8[10616832]{0:T(1024)(128)(4,1)}), s8[2228224]{0:T(1024)(128)(4,1)S(1)}, s32[]{:S(2)}) async-start(s8[10616832]{0:T(1024)(128)(4,1)} %bitcast.408), calls=%async_computation.8 | async-start | bytes 4456448
  305.2 7.7 copy-start.35
  314.1 21.1 %all-to-all-start = ((bf16[1,1,4,8,16,1152]{5,4,2,1,0,3:T(8,128)(2,1)}), bf16[1,1,4,8,16,1152]{5,4,2,1,0,3:T(8,128)(2,1)S(1)}, u32[]{:S(2)}, u32[]{:S(2)}) async-start(bf16[1,1,4,8,16,1152]{5,4,2,1,0,3:T(8,128)(2,1)} %copy.333), calls=%async_computation | async-start | bytes 2359296 | tf_op jit(solution)/shard_map/all_to_all | solution.py:68
  398.0 14.2 %copy-start.34 = (bf16[32,16,1152]{2,1,0:T(8,128)(2,1)}, bf16[32,16,1152]{2,1,0:T(8,128)(2,1)S(1)}, u32[]{:S(2)}) copy-start(bf16[32,16,1152]{2,1,0:T(8,128)(2,1)S(1)} %add_convert_fusion.4) | copy-start | bytes 3538948
  398.1 14.2 %copy-start.53 = (bf16[1,2,16,4,4,1152]{5,2,1,4,3,0:T(8,128)(2,1)S(1)}, bf16[1,2,16,4,4,1152]{5,2,1,4,3,0:T(8,128)(2,1)}, u32[]{:S(2)}) copy-start(bf16[1,2,16,4,4,1152]{5,2,1,4,3,0:T(8,128)(2,1)} %copy.349) | copy-start | bytes 3538948
  412.2 31.5 %copy-start.36 = (bf16[32,16,4608]{2,1,0:T(8,128)(2,1)}, bf16[32,16,4608]{2,1,0:T(8,128)(2,1)S(1)}, u32[]{:S(2)}) copy-start(bf16[32,16,4608]{2,1,0:T(8,128)(2,1)S(1)} %get-tuple-element.118) | copy-start | bytes 14155780
  467.1 5.4 copy-start.19
  497.1 4.9 copy-start.59
  502.0 9.9 copy-start.12
  515.6 7.3 copy-start.9
  518.2 63.7 %all-to-all-start.3 = ((bf16[8,1,4,1,16,1152]{5,4,2,3,1,0:T(8,128)(2,1)}), bf16[8,1,4,1,16,1152]{5,4,2,3,1,0:T(8,128)(2,1)}, u32[]{:S(2)}, u32[]{:S(2)}) async-start(bf16[8,1,4,1,16,1152]{5,4,2,3,1,0:T(8,128)(2,1)} %bitcast.366), calls=%async_computation.3 | async-start | bytes 2359296 | tf_op jit(solution)/shard_map/all_to_all | solution.py:90
  579.4 7.0 copy-start.71
  581.9 109.5 %all-to-all-start.1 = ((bf16[8,1,4,1,16,1152]{5,4,2,3,1,0:T(8,128)(2,1)}), bf16[8,1,4,1,16,1152]{5,4,2,3,1,0:T(8,128)(2,1)}, u32[]{:S(2)}, u32[]{:S(2)}) async-start(bf16[8,1,4,1,16,1152]{5,4,2,3,1,0:T(8,128)(2,1)} %bitcast.365), calls=%async_computation.1 | async-start | bytes 2359296 | tf_op jit(solution)/shard_map/all_to_all | solution.py:90
  587.8 16.4 %copy-start.7 = (f32[4,128,1152]{2,1,0:T(8,128)S(1)}, f32[4,128,1152]{2,1,0:T(8,128)}, u32[]{:S(2)}) copy-start(f32[4,128,1152]{2,1,0:T(8,128)} %copy-done.6) | copy-start | bytes 7077892
  587.8 16.4 %copy-start.65 = (f32[1152]{0:T(1024)S(1)}, f32[1152]{0:T(1024)}, u32[]{:S(2)}) copy-start(f32[1152]{0:T(1024)} %copy-done.64) | copy-start | bytes 13828
  587.8 16.4 %copy-start.74 = (f32[4,128]{1,0:T(4,128)S(1)}, f32[4,128]{1,0:T(4,128)}, u32[]{:S(2)}) copy-start(f32[4,128]{1,0:T(4,128)} %copy-done.73) | copy-start | bytes 6148
  604.2 11.5 %copy-start.83 = (f32[4,128]{1,0:T(4,128)S(1)}, f32[4,128]{1,0:T(4,128)}, u32[]{:S(2)}) copy-start(f32[4,128]{1,0:T(4,128)} %copy-done.82) | copy-start | bytes 6148
  604.2 11.5 %copy-start.81 = (f32[4,128]{1,0:T(4,128)S(1)}, f32[4,128]{1,0:T(4,128)}, u32[]{:S(2)}) copy-start(f32[4,128]{1,0:T(4,128)} %copy-done.80) | copy-start | bytes 6148
  650.8 7.5 slice-start
  650.8 7.5 slice-start.1
  667.2 27.0 %collective-permute-start.1 = (bf16[2,1,4,128,16,72]{3,5,4,2,1,0:T(8,128)(2,1)}, bf16[2,1,4,128,16,72]{3,5,4,2,1,0:T(8,128)(2,1)}, u32[]{:S(2)}, u32[]{:S(2)}) collective-permute-start(bf16[2,1,4,128,16,72]{3,5,4,2,1,0:T(8,128)(2,1)} %pad_maximum_fusion.3), channel_id=1, source_target_pairs={{0,1},{1,0},{2,3},{3,2},{4,5},{5,4},{6,7},{7,6},{8,9},{9,8},{10,11... | collective-permute-start | bytes 7077896 | tf_op jit(solution)/shard_map/ppermute | solution.py:24
  707.4 6.7 copy-start.67
  707.4 6.7 copy-start.79
  714.1 9.7 copy-start.85
  714.1 9.8 copy-start.10
  714.1 9.8 copy-start.87
  1056.5 6.3 copy-start.26
  (57 other events, 151.3 us)

commit v3 on v2

--- a/solution.py
+++ b/solution.py
@@ -358,6 +358,725 @@
     return (qkv, out, up, down)
 
 
+LOW = jnp.bfloat16
+WIDE = jnp.float32
+LANES = 128
+STRIP = 64
+KEYS = 256
+
+
+def whole_block(shape):
+    return pl.BlockSpec(shape, lambda *at: (0,) * len(shape))
+
+
+def strips(total, body):
+    def step(j, carry):
+        body(pl.ds(pl.multiple_of(j * STRIP, STRIP), STRIP))
+        return carry
+
+    lax.fori_loop(0, total // STRIP, step, 0)
+
+
+def turn_into(target, source):
+    for j in range(source.shape[1] // LANES):
+        target[j * LANES : (j + 1) * LANES, :] = source[:, j * LANES : (j + 1) * LANES].T
+
+
+def unit_rows(block):
+    centred = block - jnp.mean(block, axis=-1, keepdims=True)
+    spread = lax.rsqrt(jnp.mean(centred * centred, axis=-1, keepdims=True) + norm_epsilon)
+    return centred * spread, spread
+
+
+def into_norm(grad, scaled, unit, spread):
+    inner = grad * scaled
+    level = jnp.mean(inner, axis=-1, keepdims=True)
+    slope = jnp.mean(inner * unit, axis=-1, keepdims=True)
+    return spread * (inner - level - unit * slope)
+
+
+def times(left, right):
+    return jnp.dot(left, right, preferred_element_type=WIDE)
+
+
+def times_turned(left, right):
+    return lax.dot_general(left, right, (((1,), (1,)), ((), ())), preferred_element_type=WIDE)
+
+
+def turned_times(left, right):
+    return lax.dot_general(left, right, (((0,), (0,)), ((), ())), preferred_element_type=WIDE)
+
+
+def params(size, cid=None):
+    if cid is None:
+        return pltpu.CompilerParams(vmem_limit_bytes=size << 20)
+    return pltpu.CompilerParams(
+        vmem_limit_bytes=size << 20, collective_id=cid, has_side_effects=True
+    )
+
+
+def cost(flops, size):
+    return pl.CostEstimate(flops=flops, bytes_accessed=size, transcendentals=0)
+
+
+def qkv_kernel(x_ref, mod_ref, w_ref, qkv_ref, turned_ref, held):
+    @pl.when(pl.program_id(0) == 0)
+    def _():
+        scaled, shift = 1.0 + mod_ref[1:2], mod_ref[0:1]
+
+        def norm(at):
+            unit, _ = unit_rows(x_ref[at].astype(WIDE))
+            held[at] = (unit * scaled + shift).astype(LOW)
+
+        strips(held.shape[0], norm)
+        turn_into(turned_ref, held)
+
+    qkv_ref[...] = times(held[...], w_ref[...]).astype(LOW)
+
+
+def qkv_forward(x, mod, weight):
+    tokens, features = x.shape
+    steps = weight.shape[1] // features
+    return pl.pallas_call(
+        qkv_kernel,
+        grid=(steps,),
+        in_specs=[
+            whole_block(x.shape),
+            whole_block(mod.shape),
+            pl.BlockSpec((features, features), lambda j: (0, j)),
+        ],
+        out_specs=[
+            pl.BlockSpec((tokens, features), lambda j: (0, j)),
+            whole_block((features, tokens)),
+        ],
+        out_shape=[
+            jax.ShapeDtypeStruct((tokens, weight.shape[1]), LOW),
+            jax.ShapeDtypeStruct((features, tokens), LOW),
+        ],
+        scratch_shapes=[pltpu.VMEM((tokens, features), LOW)],
+        compiler_params=params(40),
+        cost_estimate=cost(2 * tokens * weight.size, 2 * weight.size),
+        name="qkv_forward",
+    )(x, mod, weight)
+
+
+def window(head):
+    low, high = head * HEAD_WIDTH, (head + 1) * HEAD_WIDTH
+    start = low // LANES * LANES
+    stop = -(-high // LANES) * LANES
+    return start, stop - start, low - start
+
+
+def head_mask(head):
+    start, wide, offset = window(head)
+    lane = lax.broadcasted_iota(jnp.int32, (1, wide), 1)
+    return ((lane >= offset) & (lane < offset + HEAD_WIDTH)).astype(WIDE).astype(LOW)
+
+
+def add_window(total, head, block):
+    start, wide, _ = window(head)
+    for j in range(wide // LANES):
+        tile = start // LANES + j
+        lanes = slice(tile * LANES, (tile + 1) * LANES)
+        piece = block[:, j * LANES : (j + 1) * LANES]
+        if head == tile * LANES // HEAD_WIDTH:
+            total[:, lanes] = piece
+        else:
+            total[:, lanes] = total[:, lanes] + piece
+
+
+def group_rows(ref, group, column, wide, spatial):
+    lanes = slice(column, column + wide)
+    if spatial:
+        return ref[group, :, lanes]
+    block = ref[:, group, :, lanes]
+    return block.reshape(-1, wide)
+
+
+def same_place():
+    row = lax.broadcasted_iota(jnp.int32, (KEYS, KEYS), 0)
+    column = lax.broadcasted_iota(jnp.int32, (KEYS, KEYS), 1)
+    return (row & 15) == (column & 15)
+
+
+def put_rows(ref, group, block, spatial):
+    if spatial:
+        ref[group] = block
+    else:
+        ref[:, group] = block.reshape(ref.shape[0], ref.shape[2], ref.shape[3])
+
+
+def sibling_barrier(me):
+    barrier = pltpu.get_barrier_semaphore()
+    pl.semaphore_signal(barrier, inc=1, device_id={"seq": me ^ 1})
+    pl.semaphore_wait(barrier, 1)
+
+
+def attend_kernel(spatial, *refs):
+    qkv_ref, x_ref, mod_ref, w_ref = refs[:4]
+    prob_ref, turned_ref, x1_ref, branch_ref, h2_ref, h2_turned_ref = refs[4:10]
+    if spatial:
+        other_ref, held, total, branch, other, send_sem, arrive_sem, keep_sem = refs[10:]
+    else:
+        held, total, branch = refs[10:]
+    group, groups = pl.program_id(0), pl.num_programs(0)
+    features = x_ref.shape[1]
+
+    if spatial:
+        me = lax.axis_index("seq")
+
+        def exchange(j):
+            return pltpu.make_async_remote_copy(
+                qkv_ref.at[j, :, pl.ds(features, 2 * features)], other.at[j],
+                send_sem.at[j], arrive_sem.at[j], device_id={"seq": me ^ 1},
+            )
+
+        @pl.when(group == 0)
+        def _():
+            sibling_barrier(me)
+            for j in range(other.shape[0]):
+                exchange(j).start()
+
+        exchange(group).wait_recv()
+    else:
+        allowed = same_place()
+
+    for head in range(HEADS):
+        start, wide, _ = window(head)
+        mask = head_mask(head)
+        queries = group_rows(qkv_ref, group, start, wide, spatial) * mask
+        keys = group_rows(qkv_ref, group, features + start, wide, spatial)
+        values = group_rows(qkv_ref, group, 2 * features + start, wide, spatial)
+        if spatial:
+            keys = jnp.concatenate([keys, other[group, :, start : start + wide]], 0)
+            values = jnp.concatenate(
+                [values, other[group, :, features + start : features + start + wide]], 0
+            )
+        scores = times_turned(queries, keys) * HEAD_WIDTH ** (-0.5)
+        if not spatial:
+            scores = jnp.where(allowed, scores, -3e38)
+        grown = jnp.exp(scores - jnp.max(scores, axis=-1, keepdims=True))
+        prob = (grown / jnp.sum(grown, axis=-1, keepdims=True)).astype(LOW)
+        prob_ref[0, head] = prob
+        add_window(total, head, times(prob, values * mask))
+    put_rows(held, group, total[...].astype(LOW), spatial)
+
+    @pl.when(group == groups - 1)
+    def _():
+        if spatial:
+            keep = pltpu.make_async_copy(other, other_ref, keep_sem)
+            keep.start()
+        attended = held[...].reshape(-1, features)
+        branch[...] = times(attended, w_ref[...])
+        for j in range(features // LANES):
+            lanes = slice(j * LANES, (j + 1) * LANES)
+            turned_ref[lanes, :] = attended[:, lanes].T
+        gate, shift, scaled = mod_ref[2:3], mod_ref[3:4], 1.0 + mod_ref[4:5]
+
+        def finish(at):
+            part = branch[at]
+            branch_ref[at] = part.astype(LOW)
+            middle = x_ref[at].astype(WIDE) + gate * part
+            x1_ref[at] = middle
+            unit, _ = unit_rows(middle)
+            h2_ref[at] = (unit * scaled + shift).astype(LOW)
+
+        strips(x_ref.shape[0], finish)
+        turn_into(h2_turned_ref, h2_ref)
+        if spatial:
+            for j in range(other.shape[0]):
+                exchange(j).wait_send()
+            keep.wait()
+
+
+def attention_forward(qkv, x, mod, weight, spatial, groups, cid=None):
+    tokens, features = x.shape
+    span = tokens // groups
+    shape = (groups, span, 3 * features) if spatial else (4, groups, span // 4, 3 * features)
+    rest = shape[:-1]
+    out_shape = [
+        jax.ShapeDtypeStruct((groups, HEADS, span, KEYS), LOW),
+        jax.ShapeDtypeStruct((features, tokens), LOW),
+        jax.ShapeDtypeStruct((tokens, features), WIDE),
+        jax.ShapeDtypeStruct((tokens, features), LOW),
+        jax.ShapeDtypeStruct((tokens, features), LOW),
+        jax.ShapeDtypeStruct((features, tokens), LOW),
+    ]
+    out_specs = [pl.BlockSpec((1, HEADS, span, KEYS), lambda g: (g, 0, 0, 0))]
+    out_specs += [whole_block(o.shape) for o in out_shape[1:]]
+    scratch = [
+        pltpu.VMEM(rest + (features,), LOW),
+        pltpu.VMEM((span, features), WIDE),
+        pltpu.VMEM((tokens, features), WIDE),
+    ]
+    if spatial:
+        both = rest + (2 * features,)
+        out_shape.append(jax.ShapeDtypeStruct(both, LOW))
+        out_specs.append(pl.BlockSpec(memory_space=pl.ANY))
+        scratch += [
+            pltpu.VMEM(both, LOW),
+            pltpu.SemaphoreType.DMA((groups,)),
+            pltpu.SemaphoreType.DMA((groups,)),
+            pltpu.SemaphoreType.DMA(()),
+        ]
+    return pl.pallas_call(
+        functools.partial(attend_kernel, spatial),
+        grid=(groups,),
+        in_specs=[
+            whole_block(shape), whole_block(x.shape), whole_block(mod.shape), whole_block(weight.shape),
+        ],
+        out_specs=out_specs,
+        out_shape=out_shape,
+        scratch_shapes=scratch,
+        compiler_params=params(56, cid),
+        cost_estimate=cost(2 * tokens * (weight.size + 2 * features * KEYS), 4 * qkv.size),
+        name="attend_spatial" if spatial else "attend_temporal",
+    )(qkv.reshape(shape), x, mod, weight)
+
+
+def attend_back_kernel(spatial, *refs):
+    if spatial:
+        (
+            da_ref, qkv_ref, prob_ref, w_ref, other_ref, dqkv_ref,
+            dout, total_q, total_k, total_v, other, give, take, load_sem, send_sem, arrive_sem,
+        ) = refs
+    else:
+        da_ref, qkv_ref, prob_ref, w_ref, dqkv_ref, dout, total_q, total_k, total_v = refs
+    group, groups = pl.program_id(0), pl.num_programs(0)
+    features = da_ref.shape[1]
+    root = HEAD_WIDTH ** (-0.5)
+    if spatial:
+        me = lax.axis_index("seq")
+
+        def exchange(j):
+            return pltpu.make_async_remote_copy(
+                give.at[j], take.at[j], send_sem.at[j], arrive_sem.at[j], device_id={"seq": me ^ 1},
+            )
+
+    @pl.when(group == 0)
+    def _():
+        if spatial:
+            load = pltpu.make_async_copy(other_ref, other, load_sem)
+            load.start()
+            sibling_barrier(me)
+        half = da_ref.shape[0] // 2
+        for j in range(2):
+            got = times_turned(da_ref[j * half : (j + 1) * half], w_ref[...]).astype(LOW)
+            if spatial:
+                dout[2 * j : 2 * j + 2] = got.reshape(2, half // 2, features)
+            else:
+                dout[2 * j : 2 * j + 2] = got.reshape(2, 2, half // 4, features)
+        if spatial:
+            load.wait()
+
+    for head in range(HEADS):
+        start, wide, _ = window(head)
+        mask = head_mask(head)
+        queries = group_rows(qkv_ref, group, start, wide, spatial) * mask
+        keys = group_rows(qkv_ref, group, features + start, wide, spatial)
+        values = group_rows(qkv_ref, group, 2 * features + start, wide, spatial)
+        grads = group_rows(dout, group, start, wide, spatial) * mask
+        if spatial:
+            keys = jnp.concatenate([keys, other[group, :, start : start + wide]], 0)
+            values = jnp.concatenate(
+                [values, other[group, :, features + start : features + start + wide]], 0
+            )
+        prob = prob_ref[0, head]
+        known = prob.astype(WIDE)
+        dprob = times_turned(grads, values)
+        level = jnp.sum(dprob * known, axis=-1, keepdims=True)
+        dscores = (known * (dprob - level)).astype(LOW)
+        add_window(total_q, head, times(dscores, keys * mask))
+        add_window(total_k, head, turned_times(dscores, queries))
+        add_window(total_v, head, turned_times(prob, grads))
+
+    own = total_q.shape[0]
+    pieces = (
+        (total_q[...] * root).astype(LOW),
+        (total_k[:own] * root).astype(LOW),
+        total_v[:own].astype(LOW),
+    )
+    for j, piece in enumerate(pieces):
+        lanes = slice(j * features, (j + 1) * features)
+        if spatial:
+            dqkv_ref[group, :, lanes] = piece
+        else:
+            dqkv_ref[:, group, :, lanes] = piece.reshape(4, -1, features)
+    if spatial:
+        give[group, :, :features] = (total_k[own:] * root).astype(LOW)
+        give[group, :, features:] = total_v[own:].astype(LOW)
+        exchange(group).start()
+
+        @pl.when(group == groups - 1)
+        def _():
+            for j in range(take.shape[0]):
+                exchange(j).wait()
+                lanes = slice(features, 3 * features)
+                dqkv_ref[j, :, lanes] = dqkv_ref[j, :, lanes] + take[j]
+
+
+def attention_backward(da, qkv, prob, weight, other, spatial, cid=None):
+    tokens, features = da.shape
+    groups = prob.shape[0]
+    span = tokens // groups
+    shape = (groups, span, 3 * features) if spatial else (4, groups, span // 4, 3 * features)
+    rest = shape[:-1]
+    in_specs = [
+        whole_block(da.shape),
+        whole_block(shape),
+        pl.BlockSpec((1, HEADS, span, KEYS), lambda g: (g, 0, 0, 0)),
+        whole_block(weight.shape),
+    ]
+    scratch = [
+        pltpu.VMEM(rest + (features,), LOW),
+        pltpu.VMEM((span, features), WIDE),
+        pltpu.VMEM((KEYS, features), WIDE),
+        pltpu.VMEM((KEYS, features), WIDE),
+    ]
+    args = [da, qkv.reshape(shape), prob, weight]
+    if spatial:
+        in_specs.append(pl.BlockSpec(memory_space=pl.ANY))
+        args.append(other)
+        scratch += [pltpu.VMEM(other.shape, LOW)] * 3
+        scratch += [
+            pltpu.SemaphoreType.DMA(()),
+            pltpu.SemaphoreType.DMA((groups,)),
+            pltpu.SemaphoreType.DMA((groups,)),
+        ]
+    got = pl.pallas_call(
+        functools.partial(attend_back_kernel, spatial),
+        grid=(groups,),
+        in_specs=in_specs,
+        out_specs=whole_block(shape),
+        out_shape=jax.ShapeDtypeStruct(shape, LOW),
+        scratch_shapes=scratch,
+        compiler_params=params(56, cid),
+        cost_estimate=cost(2 * tokens * (weight.size + 5 * features * KEYS), 4 * qkv.size),
+        name="attend_spatial_back" if spatial else "attend_temporal_back",
+    )(*args)
+    return got.reshape(tokens, 3 * features)
+
+
+def seq_barrier(me):
+    barrier = pltpu.get_barrier_semaphore()
+    for mask in range(1, 8):
+        pl.semaphore_signal(barrier, inc=1, device_id={"seq": me ^ mask})
+    pl.semaphore_wait(barrier, 7)
+
+
+def moves(source, target, sems, local_sem, me, to_places):
+    part = source.shape[-2] // 8 if to_places else source.shape[-2]
+
+    def ends(device):
+        if to_places:
+            return source.at[:, pl.ds(pl.multiple_of(device * part, part), part)], target.at[me]
+        return source.at[device], target.at[:, pl.ds(pl.multiple_of(me * part, part), part)]
+
+    copies = [pltpu.make_async_copy(*ends(me), local_sem)]
+    for mask in (6, 7, 2, 3, 4, 5, 1):
+        copies.append(
+            pltpu.make_async_remote_copy(
+                *ends(me ^ mask), sems.at[0, mask], sems.at[1, mask], device_id={"seq": me ^ mask}
+            )
+        )
+    return copies
+
+
+def move_scratch():
+    return [pltpu.SemaphoreType.DMA((2, 8)), pltpu.SemaphoreType.DMA(())]
+
+
+def gelu_and_slope(value):
+    inner = 0.7978845608028654 * (value + 0.044715 * value * value * value)
+    bent = jnp.tanh(inner)
+    half = 0.5 * (1.0 + bent)
+    slope = half + 0.5 * value * (1.0 - bent * bent) * (
+        0.7978845608028654 * (1.0 + 3 * 0.044715 * value * value)
+    )
+    return value * half, slope
+
+
+def mlp_kernel(send, *refs):
+    x1_ref, h2_ref, mod_ref, up_ref, down_ref = refs[:5]
+    turned_ref, slope_ref, out_ref, mlp_ref, total = refs[5:10]
+    step, steps = pl.program_id(0), pl.num_programs(0)
+    half = h2_ref.shape[0] // 2
+
+    for j in range(2):
+        rows = slice(j * half, (j + 1) * half)
+        hidden, slope = gelu_and_slope(times(h2_ref[rows], up_ref[...]))
+        slope_ref[rows] = slope.astype(LOW)
+        hidden = hidden.astype(LOW)
+        turned_ref[:, rows] = hidden.T
+        part = times(hidden, down_ref[...])
+
+        @pl.when(step == 0)
+        def _():
+            total[rows] = part
+
+        @pl.when(step > 0)
+        def _():
+            total[rows] = total[rows] + part
+
+    @pl.when(step == steps - 1)
+    def _():
+        gate = mod_ref[5:6]
+        if send:
+            ready, sems, local_sem = refs[10:]
+            me = lax.axis_index("seq")
+            seq_barrier(me)
+            target = ready
+        else:
+            target = out_ref
+        per = target.shape[1] if send else target.shape[0]
+
+        def finish(at):
+            mlp = total[at]
+            mlp_ref[at] = mlp.astype(LOW)
+            total[at] = x1_ref[at] + gate * mlp
+
+        strips(total.shape[0], finish)
+        if send:
+            ready[...] = total[...].astype(LOW).reshape(ready.shape)
+            copies = moves(ready, out_ref, sems, local_sem, me, True)
+            for copy in copies:
+                copy.start()
+            for copy in copies:
+                copy.wait()
+        else:
+            out_ref[...] = total[...].astype(LOW)
+
+
+def mlp_forward(x1, h2, mod, up, down, frames=None, cid=None):
+    tokens, features = x1.shape
+    wide = up.shape[1]
+    block = 768
+    out_shape = [
+        jax.ShapeDtypeStruct((wide, tokens), LOW),
+        jax.ShapeDtypeStruct((tokens, wide), LOW),
+        jax.ShapeDtypeStruct((tokens, features), LOW),
+        jax.ShapeDtypeStruct((tokens, features), LOW),
+    ]
+    scratch = [pltpu.VMEM((tokens, features), WIDE)]
+    send = frames is not None
+    if send:
+        places = tokens // frames
+        out_shape[2] = jax.ShapeDtypeStruct((8, frames, places // 8, features), LOW)
+        scratch += [pltpu.VMEM((frames, places, features), LOW)] + move_scratch()
+    out_specs = [
+        pl.BlockSpec((block, tokens), lambda j: (j, 0)),
+        pl.BlockSpec((tokens, block), lambda j: (0, j)),
+        pl.BlockSpec(memory_space=pl.ANY) if send else whole_block((tokens, features)),
+        whole_block((tokens, features)),
+    ]
+    return pl.pallas_call(
+        functools.partial(mlp_kernel, send),
+        grid=(wide // block,),
+        in_specs=[
+            whole_block(x1.shape), whole_block(h2.shape), whole_block(mod.shape),
+            pl.BlockSpec((features, block), lambda j: (0, j)),
+            pl.BlockSpec((block, features), lambda j: (j, 0)),
+        ],
+        out_specs=out_specs,
+        out_shape=out_shape,
+        scratch_shapes=scratch,
+        compiler_params=params(56, cid),
+        cost_estimate=cost(4 * tokens * up.size, 4 * up.size),
+        name="mlp_forward",
+    )(x1, h2, mod, up, down)
+
+
+def mlp_back_kernel(send, *refs):
+    g_ref, x1_ref, branch_ref, mlp_ref, mod_ref, up_ref, down_ref, slope_ref = refs[:8]
+    refs = refs[8:]
+    if send:
+        done_ref, refs = refs[0], refs[1:]
+    du_ref, df_ref, dx1_ref, da_ref, sums_ref = refs[:5]
+    refs = refs[5:]
+    if send:
+        moved_ref, refs = refs[0], refs[1:]
+    df, total = refs[:2]
+    step, steps = pl.program_id(0), pl.num_programs(0)
+    if send:
+        me = lax.axis_index("seq")
+        copies = moves(done_ref, moved_ref, refs[2], refs[3], me, False)
+
+    @pl.when(step == 0)
+    def _():
+        if send:
+            seq_barrier(me)
+            for copy in copies:
+                copy.start()
+        gate = mod_ref[5:6]
+        sums_ref[...] = jnp.zeros_like(sums_ref)
+
+        def begin(at):
+            grad = g_ref[at].astype(WIDE)
+            low = (gate * grad).astype(LOW)
+            df[at] = low
+            df_ref[at] = low
+            sums_ref[3:4] += jnp.sum(grad * mlp_ref[at].astype(WIDE), axis=0, keepdims=True)
+
+        strips(df.shape[0], begin)
+
+    half = df.shape[0] // 2
+    for j in range(2):
+        rows = slice(j * half, (j + 1) * half)
+        du = times_turned(df[rows], down_ref[...]) * slope_ref[rows].astype(WIDE)
+        du = du.astype(LOW)
+        du_ref[rows] = du
+        part = times_turned(du, up_ref[...])
+
+        @pl.when(step == 0)
+        def _():
+            total[rows] = part
+
+        @pl.when(step > 0)
+        def _():
+            total[rows] = total[rows] + part
+
+    @pl.when(step == steps - 1)
+    def _():
+        gate, scaled = mod_ref[2:3], 1.0 + mod_ref[4:5]
+
+        def finish(at):
+            grad = total[at]
+            unit, spread = unit_rows(x1_ref[at])
+            middle = g_ref[at].astype(WIDE) + into_norm(grad, scaled, unit, spread)
+            dx1_ref[at] = middle
+            da_ref[at] = (gate * middle).astype(LOW)
+            sums_ref[0:1] += jnp.sum(
+                middle * branch_ref[at].astype(WIDE), axis=0, keepdims=True
+            )
+            sums_ref[1:2] += jnp.sum(grad, axis=0, keepdims=True)
+            sums_ref[2:3] += jnp.sum(grad * unit, axis=0, keepdims=True)
+
+        strips(df.shape[0], finish)
+        if send:
+            for copy in copies:
+                copy.wait()
+
+
+def mlp_backward(g, x1, branch, mlp, mod, up, down, slope, done=None, cid=None):
+    tokens, features = x1.shape
+    wide = up.shape[1]
+    block = 768
+    send = done is not None
+    in_specs = [
+        whole_block(g.shape), whole_block(x1.shape), whole_block(branch.shape),
+        whole_block(mlp.shape), whole_block(mod.shape),
+        pl.BlockSpec((features, block), lambda j: (0, j)),
+        pl.BlockSpec((block, features), lambda j: (j, 0)),
+        pl.BlockSpec((tokens, block), lambda j: (0, j)),
+    ]
+    args = [g, x1, branch, mlp, mod, up, down, slope]
+    out_shape = [
+        jax.ShapeDtypeStruct((tokens, wide), LOW),
+        jax.ShapeDtypeStruct((tokens, features), LOW),
+        jax.ShapeDtypeStruct((tokens, features), WIDE),
+        jax.ShapeDtypeStruct((tokens, features), LOW),
+        jax.ShapeDtypeStruct((8, features), WIDE),
+    ]
+    out_specs = [pl.BlockSpec((tokens, block), lambda j: (0, j))]
+    out_specs += [whole_block(o.shape) for o in out_shape[1:]]
+    scratch = [pltpu.VMEM((tokens, features), LOW), pltpu.VMEM((tokens, features), WIDE)]
+    if send:
+        in_specs.append(pl.BlockSpec(memory_space=pl.ANY))
+        args.append(done)
+        out_shape.append(
+            jax.ShapeDtypeStruct((done.shape[1], 8 * done.shape[2], features), LOW)
+        )
+        out_specs.append(pl.BlockSpec(memory_space=pl.ANY))
+        scratch += move_scratch()
+    return pl.pallas_call(
+        functools.partial(mlp_back_kernel, send),
+        grid=(wide // block,),
+        in_specs=in_specs,
+        out_specs=out_specs,
+        out_shape=out_shape,
+        scratch_shapes=scratch,
+        compiler_params=params(56, cid),
+        cost_estimate=cost(4 * tokens * up.size, 4 * up.size),
+        name="mlp_backward",
+    )(*args)
+
+
+def qkv_back_kernel(send, *refs):
+    dqkv_ref, w_ref, x_ref, dx1_ref, mod_ref, dx_ref, sums_ref, total = refs[:8]
+    step, steps = pl.program_id(0), pl.num_programs(0)
+    part = times_turned(dqkv_ref[...], w_ref[...])
+
+    @pl.when(step == 0)
+    def _():
+        total[...] = part
+
+    @pl.when(step > 0)
+    def _():
+        total[...] = total[...] + part
+
+    @pl.when(step == steps - 1)
+    def _():
+        scaled = 1.0 + mod_ref[1:2]
+        sums_ref[...] = jnp.zeros_like(sums_ref)
+        if send:
+            ready, sems, local_sem = refs[8:]
+            me = lax.axis_index("seq")
+            seq_barrier(me)
+
+        def finish(at):
+            grad = total[at]
+            unit, spread = unit_rows(x_ref[at].astype(WIDE))
+            sums_ref[0:1] += jnp.sum(grad, axis=0, keepdims=True)
+            sums_ref[1:2] += jnp.sum(grad * unit, axis=0, keepdims=True)
+            got = dx1_ref[at] + into_norm(grad, scaled, unit, spread)
+            if send:
+                total[at] = got
+            else:
+                dx_ref[at] = got
+
+        strips(total.shape[0], finish)
+        if send:
+            ready[...] = total[...].astype(LOW).reshape(ready.shape)
+            copies = moves(ready, dx_ref, sems, local_sem, me, False)
+            for copy in copies:
+                copy.start()
+            for copy in copies:
+                copy.wait()
+
+
+def qkv_backward(dqkv, weight, x, dx1, mod, frames=None, cid=None):
+    tokens, features = x.shape
+    steps = weight.shape[1] // features
+    send = frames is not None
+    out_shape = [
+        jax.ShapeDtypeStruct((tokens, features), WIDE),
+        jax.ShapeDtypeStruct((8, features), WIDE),
+    ]
+    scratch = [pltpu.VMEM((tokens, features), WIDE)]
+    if send:
+        places = tokens // frames
+        out_shape[0] = jax.ShapeDtypeStruct((frames, places, features), LOW)
+        scratch += [pltpu.VMEM((8, frames, places // 8, features), LOW)] + move_scratch()
+    return pl.pallas_call(
+        functools.partial(qkv_back_kernel, send),
+        grid=(steps,),
+        in_specs=[
+            pl.BlockSpec((tokens, features), lambda j: (0, j)),
+            pl.BlockSpec((features, features), lambda j: (0, j)),
+            whole_block(x.shape), whole_block(dx1.shape), whole_block(mod.shape),
+        ],
+        out_specs=[
+            pl.BlockSpec(memory_space=pl.ANY) if send else whole_block((tokens, features)),
+            whole_block((8, features)),
+        ],
+        out_shape=out_shape,
+        scratch_shapes=scratch,
+        compiler_params=params(48, cid),
+        cost_estimate=cost(2 * tokens * weight.size, 2 * weight.size),
+        name="qkv_backward",
+    )(dqkv, weight, x, dx1, mod)
+
+
 AHEAD = 2
 
 
@@ -378,11 +1097,13 @@
 
 
 def gather_kernel(pieces, count, *refs):
-    shards, partial, condition = refs[:count], refs[count], refs[count + 1]
-    fulls = refs[count + 2 : 2 * count + 2]
-    partials, conditions = refs[2 * count + 2 : 2 * count + 4]
-    held = refs[2 * count + 4 : 3 * count + 4]
-    first_sem, second_sem, rep_sem, pair_sem, local_sem, small_sem = refs[3 * count + 4 :]
+    shards, partial, condition, tokens = refs[:count], *refs[count : count + 3]
+    fulls = refs[count + 3 : 2 * count + 3]
+    partials, conditions, moved = refs[2 * count + 3 : 2 * count + 6]
+    held = refs[2 * count + 6 : 3 * count + 6]
+    (
+        first_sem, second_sem, rep_sem, pair_sem, local_sem, small_sem, move_sem, stay_sem,
+    ) = refs[3 * count + 6 :]
     me, z = lax.axis_index("seq"), lax.axis_index("rep")
     odd = z & 1
     first, second = 2 + 2 * odd, 4 - 2 * odd
@@ -405,6 +1126,7 @@
             device_id={"rep": z ^ mask}))
     small.append(pltpu.make_async_copy(partial, partials.at[me], small_sem.at[0, 0]))
     small.append(pltpu.make_async_copy(condition, conditions.at[z], small_sem.at[1, 0]))
+    small += moves(tokens, moved, move_sem, stay_sem, me, True)
     for copy in small:
         copy.start()
 
@@ -480,7 +1202,7 @@
         copy.wait()
 
 
-def gather_weights(shards, partial, condition, cid):
+def gather_weights(shards, partial, condition, tokens, cid):
     shapes = [shard.shape for shard in shards]
     pieces = gather_pieces(shapes)
     count = len(shards)
@@ -489,22 +1211,25 @@
     outs = [jax.ShapeDtypeStruct((8,) + shape, jnp.bfloat16) for shape in shapes]
     outs.append(jax.ShapeDtypeStruct((8,) + partial.shape, partial.dtype))
     outs.append(jax.ShapeDtypeStruct((4,) + condition.shape, condition.dtype))
+    frames, places, features = tokens.shape
+    outs.append(jax.ShapeDtypeStruct((8, frames, places // 8, features), tokens.dtype))
     got = pl.pallas_call(
         functools.partial(gather_kernel, pieces, count),
         out_shape=outs,
-        in_specs=[pl.BlockSpec(memory_space=pl.ANY)] * (count + 2),
+        in_specs=[pl.BlockSpec(memory_space=pl.ANY)] * (count + 3),
         out_specs=[pl.BlockSpec(memory_space=pl.ANY)] * len(outs),
         scratch_shapes=[pltpu.VMEM(shape, jnp.bfloat16) for shape in shapes]
         + [
             dma((2, size)), dma((2, size)), dma((2, size)), dma((4, 2, size)), dma((2, count)), dma((2, 11)),
-        ],
+        ]
+        + move_scratch(),
         compiler_params=pltpu.CompilerParams(
             collective_id=cid, has_side_effects=True,
         ),
         name="gather_weights",
-    )(*shards, partial, condition)
+    )(*shards, partial, condition, tokens)
     fulls = [full.reshape(-1, full.shape[2]) for full in got[:count]]
-    return fulls, got[count], got[count + 1]
+    return fulls, got[count:]
 
 
 SLOTS = 3
@@ -852,22 +1577,72 @@
     return [tuple(got[4 * at : 4 * at + 4]) for at in range(len(layers))], got[-1]
 
 
-def turned_rows(operand, tall):
-    left = turned(operand)
-    rows = left.shape[0] // 8 // tall
-    shape = (4, 2, rows, left.shape[1]) if tall == 1 else (4, 2, tall, rows, left.shape[1])
-    return left.reshape(shape)
-
-
-def reduce_operands(grad_pairs):
-    qkv_pair, out_pair, up_pair, down_pair = grad_pairs
-    tall = down_pair[0].shape[-1] // down_pair[1].shape[-1]
+def reduce_operands(lefts, rights):
+    features = rights[1].shape[1]
+    shaped = []
+    for left in lefts:
+        tall, tokens = left.shape[0] // features, left.shape[1]
+        shape = (4, 2, features // 8, tokens) if tall == 1 else (4, 2, tall, features // 8, tokens)
+        shaped.append(left.reshape(shape))
+    return (*shaped, *rights)
+
+
+def layer_forward(x, mod, weights, spatial, groups, frames=None, cids=(None, None)):
+    qkv_w, out_w, up_w, down_w = weights
+    qkv, h_turned = qkv_forward(x, mod, qkv_w)
+    prob, o_turned, x1, branch, h2, h2_turned, *other = attention_forward(
+        qkv, x, mod, out_w, spatial, groups, cids[0]
+    )
+    z_turned, slope, out, mlp = mlp_forward(x1, h2, mod, up_w, down_w, frames, cids[1])
+    lefts = (h_turned, o_turned, h2_turned, z_turned)
+    return out, (qkv, prob, other[0] if spatial else None, x1, branch, slope, mlp), lefts
+
+
+def layer_backward(g, x, mod, weights, kept, lefts, spatial, done=None, frames=None, cids=(None,) * 3):
+    qkv_w, out_w, up_w, down_w = weights
+    qkv, prob, other, x1, branch, slope, mlp = kept
+    du, df, dx1, da, sums, *moved = mlp_backward(
+        g, x1, branch, mlp, mod, up_w, down_w, slope, done, cids[0]
+    )
+    dqkv = attention_backward(da, qkv, prob, out_w, other, spatial, cids[1])
+    dx, last_sums = qkv_backward(dqkv, qkv_w, x, dx1, mod, frames, cids[2])
+    mod_grad = jnp.concatenate([last_sums[:2], sums[:4]], 0).reshape(1, -1)
+    return dx, moved, mod_grad, reduce_operands(lefts, (dqkv, da, du, df))
+
+
+def fused_device(frames_in, conditioning, shards, partial_mod, cotangent):
+    _, _, frames, places, features = frames_in.shape
+    tokens = frames * places
+    low_cotangent = cotangent.reshape(frames, places, features).astype(LOW)
+    weights, (partials, conditions, g_two) = gather_weights(
+        shards, partial_mod.reshape(-1, LANES), conditioning.reshape(-1, LANES), low_cotangent, 0
+    )
+    modulation = jnp.sum(partials, 0).reshape(2, 6, features)
+    mod_one, mod_two = modulation[0], modulation[1]
+    weights_one, weights_two = weights[:4], weights[4:]
+    x_one = frames_in.reshape(tokens, features)
+    x_two, kept_one, lefts_one = layer_forward(
+        x_one, mod_one, weights_one, True, frames, frames, (2, 4)
+    )
+    x_two = x_two.reshape(tokens, features)
+    y_two, kept_two, lefts_two = layer_forward(x_two, mod_two, weights_two, False, 2)
+    g_one, (block_out,), mod_grad_two, operands_two = layer_backward(
+        g_two.reshape(tokens, features), x_two, mod_two, weights_two, kept_two, lefts_two, False,
+        y_two.reshape(g_two.shape), frames, (5, None, 6),
+    )
+    input_grad, _, mod_grad_one, operands_one = layer_backward(
+        g_one.reshape(tokens, features), x_one, mod_one, weights_one, kept_one, lefts_one, True,
+        cids=(None, 3, None),
+    )
+    mod_grads = jnp.concatenate([mod_grad_one, mod_grad_two], 1).astype(LOW)
+    (grads_two, grads_one), every_mod = reduce_grads(
+        [operands_two, operands_one], mod_grads.reshape(-1, LANES), 1
+    )
+    every_mod = every_mod.reshape(-1, mod_grads.shape[1])
     return (
-        turned_rows(qkv_pair[0], 1),
-        turned_rows(out_pair[0], 1),
-        turned_rows(up_pair[0], 1),
-        turned_rows(down_pair[0], tall),
-    ) + tuple(flat(pair[1]) for pair in grad_pairs)
+        block_out.astype(WIDE), input_grad, grads_one, grads_two, every_mod,
+        conditions.reshape(-1, features),
+    )
 
 
 def per_device(
@@ -887,9 +1662,6 @@
 ):
     clip_count, _, frame_dev, half_places, features = frames_in.shape
     fused = lax.axis_size("seq") == 8 and lax.axis_size("rep") == 4 and clip_count == 1
-    start_stream = frames_in.reshape(clip_count, frame_dev, half_places, features).astype(
-        jnp.float32
-    )
     row_count = mod_first.shape[0]
     row_start = lax.axis_index("seq") * row_count
     mod_width = mod_first.shape[1]
@@ -907,39 +1679,35 @@
         qkv_second, out_second, up_second, down_second,
     )
     if fused:
-        weights, partials, conditions = gather_weights(
-            shards, partial_mod.reshape(-1, 128), conditioning.reshape(-1, 128), 0
+        block_out, stream_grad, grads_one, grads_two, every_mod, conditions = fused_device(
+            frames_in, conditioning, shards, partial_mod, cotangent
         )
-        modulation = jnp.sum(partials, 0).reshape(1, -1)
-        every_silu = rows_of(jax.nn.silu(conditions.reshape(-1, features))).astype(jnp.bfloat16)
+        every_silu = rows_of(jax.nn.silu(conditions)).astype(jnp.bfloat16)
+        mod_total = lax.dynamic_slice_in_dim(every_mod, lax.axis_index("rep"), 1, 0)
     else:
         weights = [lax.all_gather(shard, "seq", axis=0, tiled=True) for shard in shards]
         modulation = lax.psum(partial_mod, "seq")
         every_silu = lax.all_gather(silu_local, "rep", axis=0, tiled=True)
-    mod_one, mod_two = modulation[:, :mod_width], modulation[:, mod_width:]
-    weights_one, weights_two = weights[:4], weights[4:]
-    spatial_out, state_one = forward_layer(start_stream, mod_one, weights_one, True)
-    placed = to_places(spatial_out)
-    temporal_out, state_two = forward_layer(placed, mod_two, weights_two, False)
-    block_out = to_frames(temporal_out, frame_dev)
-    cotangent_sites = to_places(cotangent.reshape(clip_count, frame_dev, half_places, features))
-    placed_grad, mod_grad_two, pairs_two = backward_layer(
-        cotangent_sites, placed, mod_two, weights_two, state_two, False
-    )
-    spatial_grad = to_frames(placed_grad, frame_dev)
-    stream_grad, mod_grad_one, pairs_one = backward_layer(
-        spatial_grad, start_stream, mod_one, weights_one, state_one, True
-    )
-    mod_grads = jnp.concatenate([mod_grad_one, mod_grad_two], 1).astype(jnp.bfloat16)
-    if fused:
-        (grads_two, grads_one), every_mod = reduce_grads(
-            [reduce_operands(pairs_two), reduce_operands(pairs_one)],
-            mod_grads.reshape(-1, 128),
-            1,
+        mod_one, mod_two = modulation[:, :mod_width], modulation[:, mod_width:]
+        weights_one, weights_two = weights[:4], weights[4:]
+        start_stream = frames_in.reshape(clip_count, frame_dev, half_places, features).astype(
+            jnp.float32
         )
-        every_mod = every_mod.reshape(-1, 2 * mod_width)
-        mod_total = lax.dynamic_slice_in_dim(every_mod, lax.axis_index("rep"), 1, 0)
-    else:
+        spatial_out, state_one = forward_layer(start_stream, mod_one, weights_one, True)
+        placed = to_places(spatial_out)
+        temporal_out, state_two = forward_layer(placed, mod_two, weights_two, False)
+        block_out = to_frames(temporal_out, frame_dev)
+        cotangent_sites = to_places(
+            cotangent.reshape(clip_count, frame_dev, half_places, features)
+        )
+        placed_grad, mod_grad_two, pairs_two = backward_layer(
+            cotangent_sites, placed, mod_two, weights_two, state_two, False
+        )
+        spatial_grad = to_frames(placed_grad, frame_dev)
+        stream_grad, mod_grad_one, pairs_one = backward_layer(
+            spatial_grad, start_stream, mod_one, weights_one, state_one, True
+        )
+        mod_grads = jnp.concatenate([mod_grad_one, mod_grad_two], 1).astype(jnp.bfloat16)
         grads_two, grads_one = layer_grads(pairs_two), layer_grads(pairs_one)
         mod_total = lax.psum(mod_grads, "seq").astype(jnp.bfloat16)
         every_mod = lax.all_gather(mod_total, "rep", axis=0, tiled=True)

time: 1090 us -> 882 us (0.81)
  Pallas kernels: 522 us -> 820 us
  matrix products: 249 us -> 9.98 us
  local copies, waits for them, and re-layouts: 214 us -> 33.3 us
  other arithmetic: 65.6 us -> 7.6 us
  starting transfers between devices: 18.8 us -> 0 us
    pallas_call x0 -> x12, Pallas kernels: none -> 286 us  [the longest x2 70.5 us: mlp_forward(): pl.pallas_call(functools.partial(mlp_kernel, send), grid=(wide // block,)...]
    dot_general x28 -> x0, matrix products: 237 us -> none  [the longest x8 81.9 us: project_back(): jnp.einsum('csle,de->csld', incoming, right_operand, preferred_element_ty...]
    concatenate x16 -> x0, local copies, waits for them, and re-layouts: 60.6 us -> none  [the longest x15 60.6 us: backward_layer(): jnp.concatenate([component.reshape(clip_count, seq_count, seq_len, featur...]
    another operation x10 -> x0, local copies, waits for them, and re-layouts: 41.9 us -> none
    reshape x8 -> x0, local copies, waits for them, and re-layouts: 31.7 us -> none  [the longest x4 17.3 us: turned(): return operand.reshape(-1, operand.shape[-1]).T]
    convert_element_type x17 -> x1, other arithmetic: 23.2 us -> 1.14 us  [fused_device(): low_cotangent = cotangent.reshape(frames, places, features).astype(LOW)]
    convert_element_type x12 -> x0, local copies, waits for them, and re-layouts: 19.9 us -> none  [the longest x4 9.49 us: shortened(): a.astype(jnp.bfloat16)]
    all_to_all x4 -> x0, starting transfers between devices: 18 us -> none  [the longest x2 9.09 us: to_frames(): lax.all_to_all(shortened(arranged), 'seq', split_axis=0, concat_axis=3, t...]
  transfers between devices with their start and end apart: 6 -> 0, of which waited for: 1 -> 0; matrix products, arithmetic and copies ran while one was open for 23% -> 0% of each run, Pallas kernels for 0% -> 0%
where the time goes in v3:
time: 882 us; the launch traced here: 873 us
  Pallas kernels  820 us (93%)
  local copies, waits for them, and re-layouts  33.3 us (4%)
  matrix products  9.98 us (1%)
    pallas_call x1, Pallas kernels, reduce_grads(): pl.pallas_call(functools.partial(reduce_kernel, len(layers), rows, width,...  312 us
    pallas_call x1, Pallas kernels, gather_weights(): pl.pallas_call(functools.partial(gather_kernel, pieces, count), out_shape...  223 us
    pallas_call x2, Pallas kernels, mlp_forward(): pl.pallas_call(functools.partial(mlp_kernel, send), grid=(wide // block,)...  70.5 us
    pallas_call x2, Pallas kernels, mlp_backward(): pl.pallas_call(functools.partial(mlp_back_kernel, send), grid=(wide // bl...  60.5 us
    pallas_call x2, Pallas kernels, attention_backward(): pl.pallas_call(functools.partial(attend_back_kernel, spatial), grid=(grou...  52.4 us
    pallas_call x2, Pallas kernels, attention_forward(): pl.pallas_call(functools.partial(attend_kernel, spatial), grid=(groups,),...  44.6 us
    pallas_call x2, Pallas kernels, qkv_backward(): pl.pallas_call(functools.partial(qkv_back_kernel, send), grid=(steps,), i...  40 us
    unnamed x70, local copies, waits for them, and re-layouts  31.7 us

profile of v3, /device:TPU:0, one launch (start us, length us, event | category | flops | bytes accessed | tf_op | source)
XLA Modules:
  0.0 872.6 jit_solution(12829264863284921462)
XLA Ops:
  0.7 1.4 reduce.1
  2.1 2.2 fusion.11
  4.3 1.1 fusion.9
  5.4 0.8 maximum_reduce_fusion
  6.2 1.1 convert_bitcast_fusion.refs_10_
  7.3 222.7 %gather_weights.1 = (bf16[8,144,3456]{2,1,0:T(8,128)(2,1)}, bf16[8,144,1152]{2,1,0:T(8,128)(2,1)}, bf16[8,144,4608]{2,1,0:T(8,128)(2,1)}, bf16[8,576,1152]{2,1,0...) custom-call(bf16[144,3456]{1,0:T(8,128)(2,1)} %refs_0_.1, ...), custom_call_target="tpu_custom_call" | custom-call | tf_op jit(solution)/shard_map/gather_weights/pallas_call | solution.py:1216
  230.0 0.8 copy.33
  230.8 1.1 reduce_sum.9
  231.9 3.3 copy-done.12
  235.2 8.6 qkv_forward.2
  243.8 1.8 copy-done.2
  245.6 1.0 copy-done.16
  246.6 28.5 %attend_spatial.1 = (bf16[4,16,128,256]{3,2,1,0:T(8,128)(2,1)}, bf16[1152,512]{1,0:T(8,128)(2,1)}, f32[512,1152]{1,0:T(8,128)}, bf16[512,1152]{1,0:T(8,128)(2,1)...) custom-call(bf16[4,128,3456]{2,1,0:T(8,128)(2,1)} %bitcast.70, ...), custom_call_target="tpu_custom_call" | custom-call | flops 1962934272 | bytes 7077888 | tf_op jit(solution)/shard_map/attend_spatial/pallas_call | solution.py:622
  275.1 42.9 %mlp_forward.2 = (bf16[4608,512]{1,0:T(8,128)(2,1)}, bf16[512,4608]{1,0:T(8,128)(2,1)}, bf16[8,4,16,1152]{3,2,1,0:T(8,128)(2,1)}, bf16[512,1152]{1,0:T(8,128)(2,1)}) custom-call(f32[512,1152]{1,0:T(8,128)} %get-tuple-element.78.refs_0_.refs_1_, bf16[512,1152]{1,0:T(8,128)(2,1)} %get-tuple-element.79.refs_1_, f32[6,1152]{1,0:T(8,128)} %copy-done.8, ...), custom_call_target="tpu_custom_call" | custom-call | flops 10871635968 | bytes 21233664 | tf_op jit(solution)/shard_map/mlp_forward/pallas_call | solution.py:872
  318.0 1.3 copy-done.6
  319.3 3.3 copy-done.13
  322.5 9.1 %qkv_forward.3 = (bf16[512,3456]{1,0:T(8,128)(2,1)S(1)}, bf16[1152,512]{1,0:T(8,128)(2,1)S(1)}) custom-call(bf16[512,1152]{1,0:T(8,128)(2,1)S(1)} %bitcast.76, f32[6,1152]{1,0:T(8,128)S(1)} %squeeze.7.mod_ref.refs_2_.refs_4_, bf16[1152,3456]{1,0:T(8,128)(2,1)S(1)} %bitcast.83), custom_call_target="tpu_custom_call" | custom-call | flops 4076863488 | bytes 7962624 | tf_op jit(solution)/shard_map/qkv_forward/pallas_call | solution.py:440
  331.6 1.8 copy-done.1
  333.4 16.1 %attend_temporal.1 = (bf16[2,16,256,256]{3,2,1,0:T(8,128)(2,1)}, bf16[1152,512]{1,0:T(8,128)(2,1)}, f32[512,1152]{1,0:T(8,128)}, bf16[512,1152]{1,0:T(8,128)(2,1...) custom-call(bf16[4,2,64,3456]{3,2,1,0:T(8,128)(2,1)} %bitcast.68, bf16[512,1152]{1,0:T(8,128)(2,1)} %bitcast.75, ...), custom_call_target="tpu_custom_call" | custom-call | flops 1962934272 | bytes 7077888 | tf_op jit(solution)/shard_map/attend_temporal/pallas_call | solution.py:622
  349.5 27.6 %mlp_forward.3 = (bf16[4608,512]{1,0:T(8,128)(2,1)}, bf16[512,4608]{1,0:T(8,128)(2,1)}, bf16[512,1152]{1,0:T(8,128)(2,1)}, bf16[512,1152]{1,0:T(8,128)(2,1)}) custom-call(f32[512,1152]{1,0:T(8,128)} %get-tuple-element.86.refs_0_.refs_1_, bf16[512,1152]{1,0:T(8,128)(2,1)} %get-tuple-element.88.refs_1_, f32[6,1152]{1,0:T(8,128)} %copy-done.10, ...), custom_call_target="tpu_custom_call" | custom-call | flops 10871635968 | bytes 21233664 | tf_op jit(solution)/shard_map/mlp_forward/pallas_call | solution.py:872
  377.2 31.3 %mlp_backward.2 = (bf16[512,4608]{1,0:T(8,128)(2,1)}, bf16[512,1152]{1,0:T(8,128)(2,1)}, f32[512,1152]{1,0:T(8,128)}, bf16[512,1152]{1,0:T(8,128)(2,1)}, f32[8,1...) custom-call(bf16[512,1152]{1,0:T(8,128)(2,1)} %bitcast.121, f32[512,1152]{1,0:T(8,128)} %get-tuple-element.86.refs_0_.refs_1_, ...), custom_call_target="tpu_custom_call" | custom-call | flops 10871635968 | bytes 21233664 | tf_op jit(solution)/shard_map/mlp_backward/pallas_call | solution.py:991
  408.5 20.3 %attend_temporal_back.1 = bf16[4,2,64,3456]{3,2,1,0:T(8,128)(2,1)} custom-call(bf16[512,1152]{1,0:T(8,128)(2,1)} %get-tuple-element.95.refs_0_.refs_5_, bf16[4,2,64,3456]{3,2,1,0:T(8,128)(2,1)} %bitcast.69, bf16[2,16,256,256]{3,2,1,0:T(8,128)(2,1)} %get-tuple-element.96.refs_2_, bf16[1152,1152]{1,0:T(8,128)(2,1)} %bitcast.90), custom_call_target="tpu_custom_call" | custom-call | flops 2868903936 | bytes 7077888 | tf_op jit(solution)/shard_map/attend_temporal_back/pallas_call | solution.py:746
  428.8 27.4 %qkv_backward.2 = (bf16[4,128,1152]{2,1,0:T(8,128)(2,1)S(1)}, f32[8,1152]{1,0:T(8,128)S(1)}) custom-call(bf16[512,3456]{1,0:T(8,128)(2,1)} %bitcast.93, bf16[1152,3456]{1,0:T(8,128)(2,1)} %bitcast.82, bf16[512,1152]{1,0:T(8,128)(2,1)S(1)} %bitcast.77, f32[512,1152]{1,0:T(8,128)S(1)} %copy-done.18, f32[6,1152]{1,0:T(8,128)S(1)} %copy-done.11), custom_call_target="tpu_custom_call" | custom-call | flops 4076863488 | bytes 7962624 | tf_op jit(solution)/shard_map/qkv_backward/pallas_call | solution.py:1060
  456.3 1.0 copy-done.17
  457.3 29.2 %mlp_backward.3 = (bf16[512,4608]{1,0:T(8,128)(2,1)}, bf16[512,1152]{1,0:T(8,128)(2,1)}, f32[512,1152]{1,0:T(8,128)}, bf16[512,1152]{1,0:T(8,128)(2,1)}, f32[8,1152]{1,0:T(8,128)}) custom-call(bf16[512,1152]{1,0:T(8,128)(2,1)} %bitcast.88, f32[512,1152]{1,0:T(8,128)} %get-tuple-element.78.refs_0_.refs_1_, bf16[512,1152]{1,0:T(8,128)(2,1)} %get-tuple-element.99.refs_2_, ...), custom_call_target="tpu_custom_call" | custom-call | flops 10871635968 | bytes 21233664 | tf_op jit(solution)/shard_map/mlp_backward/pallas_call | solution.py:991
  486.5 32.1 %attend_spatial_back.1 = bf16[4,128,3456]{2,1,0:T(8,128)(2,1)} custom-call(bf16[512,1152]{1,0:T(8,128)(2,1)} %get-tuple-element.102.refs_0_.refs_13_, bf16[4,128,3456]{2,1,0:T(8,128)(2,1)} %bitcast.71, bf16[4,16,128,256]{3,2,1,0:T(8,128)(2,1)} %get-tuple-element.103.refs_2_, bf16[1152,1152]{1,0:T(8,128)(2,1)} %bitcast.92, ...), custom_call_target="tpu_custom_call" | custom-call | flops 2868903936 | bytes 7077888 | tf_op jit(solution)/shard_map/attend_spatial_back/pallas_call | solution.py:746
  518.6 1.7 copy-done.19
  520.3 12.6 %qkv_backward.3 = (f32[512,1152]{1,0:T(8,128)}, f32[8,1152]{1,0:T(8,128)S(1)}) custom-call(bf16[512,3456]{1,0:T(8,128)(2,1)} %bitcast.95, bf16[1152,3456]{1,0:T(8,128)(2,1)} %bitcast.80, bf16[512,1152]{1,0:T(8,128)(2,1)S(1)} %bitcast.74, f32[512,1152]{1,0:T(8,128)S(1)} %copy-done.19, f32[6,1152]{1,0:T(8,128)S(1)} %copy-done.9), custom_call_target="tpu_custom_call" | custom-call | flops 4076863488 | bytes 7962624 | tf_op jit(solution)/shard_map/qkv_backward/pallas_call | solution.py:1060
  532.9 0.8 slice.63
  533.7 0.8 slice.62
  534.8 311.9 %reduce_grads.1 = (f32[144,3456]{1,0:T(8,128)}, f32[144,1152]{1,0:T(8,128)S(1)}, f32[144,4608]{1,0:T(8,128)}, f32[576,1152]{1,0:T(8,128)}, f32[144,3456]{1,0:T(8...) custom-call(bf16[4,2,144,512]{3,2,1,0:T(8,128)(2,1)S(1)} %bitcast.87, ...), custom_call_target="tpu_custom_call" | custom-call | flops 32614907904 | bytes 16146432 | tf_op jit(solution)/shard_map/reduce_grads/pallas_call | solution.py:1536
  846.7 0.6 fusion.4
  847.3 0.9 copy-done.20
  848.8 1.4 fusion.8
  850.2 1.6 bitcast_convert_fusion
  851.8 2.7 fusion
  854.5 2.7 fusion.2
  857.3 1.3 copy.42
  858.5 0.8 copy.43
  860.0 1.5 copy.44
  861.5 1.2 copy-done.23
  862.7 1.5 copy.45
  864.2 1.0 copy-done.26
  865.2 1.3 copy.46
  866.5 0.8 copy.47
  867.9 1.5 copy.48
  869.4 1.2 copy-done.21
  870.6 1.5 copy.49
  (59 shorter events, 2.2 us)
Async XLA Ops:
  0.6 3.6 copy-start
  2.1 4.1 copy-start.25
  7.3 224.6 %copy-start.4 = (bf16[1,1,4,128,1152]{4,3,2,1,0:T(8,128)(2,1)S(1)}, bf16[1,1,4,128,1152]{4,3,2,1,0:T(8,128)(2,1)}, u32[]{:S(2)}) copy-start(bf16[1,1,4,128,1152]{4,3,2,1,0:T(8,128)(2,1)} %param.13) | copy-start | bytes 3538948
  231.9 86.1 %copy-start.10 = (f32[6,1152]{1,0:T(8,128)}, f32[6,1152]{1,0:T(8,128)S(1)}, u32[]{:S(2)}) copy-start(f32[6,1152]{1,0:T(8,128)S(1)} %squeeze.7.mod_ref.refs_2_.refs_4_) | copy-start | bytes 82948
  231.9 3.3 copy-start.12
  235.2 8.6 copy-start.8
  243.8 1.8 copy-start.2
  245.6 1.0 copy-start.16
  318.0 1.3 copy-start.6
  319.3 3.3 copy-start.13
  331.6 1.8 copy-start.1
  408.5 20.3 %copy-start.7 = (bf16[8,4,16,1152]{3,2,1,0:T(8,128)(2,1)S(1)}, bf16[8,4,16,1152]{3,2,1,0:T(8,128)(2,1)}, u32[]{:S(2)}) copy-start(bf16[8,4,16,1152]{3,2,1,0:T(8,128)(2,1)} %get-tuple-element.82) | copy-start | bytes 3538948
  408.5 20.3 %copy-start.11 = (f32[6,1152]{1,0:T(8,128)S(1)}, f32[6,1152]{1,0:T(8,128)}, u32[]{:S(2)}) copy-start(f32[6,1152]{1,0:T(8,128)} %copy-done.10) | copy-start | bytes 82948
  408.5 20.3 %copy-start.18 = (f32[512,1152]{1,0:T(8,128)S(1)}, f32[512,1152]{1,0:T(8,128)}, u32[]{:S(2)}) copy-start(f32[512,1152]{1,0:T(8,128)} %get-tuple-element.97.refs_3_) | copy-start | bytes 7077892
  456.3 1.0 copy-start.17
  486.5 32.1 %copy-start.5 = (bf16[1,1,4,128,1152]{4,3,2,1,0:T(8,128)(2,1)S(1)}, bf16[1,1,4,128,1152]{4,3,2,1,0:T(8,128)(2,1)}, u32[]{:S(2)}) copy-start(bf16[1,1,4,128,1152]{4,3,2,1,0:T(8,128)(2,1)} %param.13) | copy-start | bytes 3538948
  486.5 32.1 %copy-start.9 = (f32[6,1152]{1,0:T(8,128)S(1)}, f32[6,1152]{1,0:T(8,128)}, u32[]{:S(2)}) copy-start(f32[6,1152]{1,0:T(8,128)} %copy-done.8) | copy-start | bytes 82948
  518.6 1.7 copy-start.19
  520.3 14.4 %copy-start.3 = (bf16[512,1152]{1,0:T(8,128)(2,1)S(1)}, bf16[512,1152]{1,0:T(8,128)(2,1)}, u32[]{:S(2)}) copy-start(bf16[512,1152]{1,0:T(8,128)(2,1)} %get-tuple-element.95.refs_0_.refs_5_) | copy-start | bytes 3538948
  520.3 14.4 %copy-start.14 = (bf16[1152,512]{1,0:T(8,128)(2,1)S(1)}, bf16[1152,512]{1,0:T(8,128)(2,1)}, u32[]{:S(2)}) copy-start(bf16[1152,512]{1,0:T(8,128)(2,1)} %get-tuple-element.108) | copy-start | bytes 3538948
  520.3 14.4 %copy-start.15 = (bf16[1152,512]{1,0:T(8,128)(2,1)S(1)}, bf16[1152,512]{1,0:T(8,128)(2,1)}, u32[]{:S(2)}) copy-start(bf16[1152,512]{1,0:T(8,128)(2,1)} %get-tuple-element.109) | copy-start | bytes 3538948
  846.6 1.6 copy-start.20
  846.7 3.5 copy-start.28
  854.5 2.8 copy-start.27
  857.3 2.7 copy-start.24
  860.0 2.7 copy-start.23
  862.7 2.5 copy-start.26
  865.2 2.7 copy-start.22
  867.9 2.7 copy-start.21

commit v4 on v3

--- a/solution.py
+++ b/solution.py
@@ -1,4 +1,5 @@
 import functools
+import math
 
 import jax
 import jax.numpy as jnp
@@ -358,6 +359,152 @@
     return (qkv, out, up, down)
 
 
+AHEAD = 2
+
+
+def gather_pieces(shapes):
+    features = math.gcd(*(columns for _, columns in shapes), 8 * shapes[0][0])
+    rows_of = features // 8
+    return rows_of, features, [
+        (at, row, column)
+        for at, (rows, columns) in enumerate(shapes)
+        for row in range(0, rows, rows_of)
+        for column in range(0, columns, features)
+    ]
+
+
+class Gather:
+    def __init__(self, shapes, refs):
+        count = len(shapes)
+        self.count = count
+        self.least, self.wide, self.pieces = gather_pieces(shapes)
+        self.shards, self.fulls = refs[0], refs[1]
+        self.held = refs[2][: count // 2]
+        self.first_sem, self.second_sem, self.rep_sem, self.pair_sem, self.local_sem = refs[2][
+            count // 2 :
+        ]
+        self.me, self.z = lax.axis_index("seq"), lax.axis_index("rep")
+        odd = self.z & 1
+        self.first, self.second = 2 + 2 * odd, 4 - 2 * odd
+
+    @staticmethod
+    def scratch(shapes):
+        size = len(gather_pieces(shapes)[2])
+        dma = pltpu.SemaphoreType.DMA
+        half = shapes[: len(shapes) // 2]
+        return [pltpu.VMEM(shape, jnp.bfloat16) for shape in half] + [
+            dma((2, size)), dma((2, size)), dma((2, size)), dma((4, 2, size)), dma((2, len(shapes))),
+        ]
+
+    @staticmethod
+    def outs(shapes):
+        return [jax.ShapeDtypeStruct((8,) + shape, jnp.bfloat16) for shape in shapes]
+
+    def place(self, owner, at):
+        weight, row, column = self.pieces[at]
+        return self.fulls[weight].at[owner, pl.ds(row, self.least), pl.ds(column, self.wide)]
+
+    def own(self, at):
+        weight, row, column = self.pieces[at]
+        return self.shards[weight].at[pl.ds(row, self.least), pl.ds(column, self.wide)]
+
+    def to_seq(self, source, owner, at, sems, mask):
+        return pltpu.make_async_remote_copy(
+            source, self.place(owner, at), sems.at[0, at], sems.at[1, at],
+            device_id={"seq": self.me ^ mask},
+        )
+
+    def first_copy(self, at):
+        return self.to_seq(self.own(at), self.me, at, self.first_sem, self.first)
+
+    def second_copy(self, at):
+        owner = self.me ^ self.first
+        return self.to_seq(self.place(owner, at), owner, at, self.second_sem, self.second)
+
+    def rep_copy(self, at):
+        owner = self.me ^ self.first
+        return pltpu.make_async_remote_copy(
+            self.place(owner, at), self.place(owner, at), self.rep_sem.at[0, at], self.rep_sem.at[1, at],
+            device_id={"rep": self.z ^ 1},
+        )
+
+    def pair_copy(self, which, at):
+        if which == 0:
+            return self.to_seq(self.own(at), self.me, at, self.pair_sem.at[0], 1)
+        owner = self.me ^ (self.first, self.first ^ self.second, self.second)[which - 1]
+        return self.to_seq(self.place(owner, at), owner, at, self.pair_sem.at[which], 1)
+
+    def begin(self, at):
+        self.first_copy(at).start()
+        self.pair_copy(0, at).start()
+
+    def fetch(self, weight):
+        return pltpu.make_async_copy(
+            self.shards[weight], self.held[weight % len(self.held)], self.local_sem.at[0, weight]
+        )
+
+    def keep(self, weight):
+        return pltpu.make_async_copy(
+            self.held[weight % len(self.held)], self.fulls[weight].at[self.me], self.local_sem.at[1, weight]
+        )
+
+    def start(self):
+        for at in range(AHEAD):
+            self.begin(at)
+        self.local(0)
+
+    def local(self, first):
+        for weight in range(first, first + len(self.held)):
+            self.fetch(weight).start()
+        for weight in range(first, first + len(self.held)):
+            self.fetch(weight).wait()
+            self.keep(weight).start()
+
+    def ready(self, weight):
+        for at, piece in enumerate(self.pieces):
+            if piece[0] == weight:
+                for which in range(4):
+                    self.pair_copy(which, at).wait_recv()
+        self.keep(weight).wait()
+
+    def advance(self, at):
+        self.first_copy(at).wait_recv()
+        if at + AHEAD < len(self.pieces):
+            self.begin(at + AHEAD)
+        self.second_copy(at).start()
+        self.rep_copy(at).start()
+        self.pair_copy(1, at).start()
+        if at:
+            self.share(at - 1)
+
+    def share(self, at):
+        self.second_copy(at).wait_recv()
+        self.rep_copy(at).wait_recv()
+        self.pair_copy(2, at).start()
+        self.pair_copy(3, at).start()
+
+    def finish(self):
+        for at in range(len(self.pieces)):
+            for copy in (self.first_copy(at), self.second_copy(at), self.rep_copy(at)):
+                copy.wait_send()
+            for which in range(4):
+                self.pair_copy(which, at).wait_send()
+
+
+def enter(seq_masks, rep_masks):
+    me, z = lax.axis_index("seq"), lax.axis_index("rep")
+    barrier = pltpu.get_barrier_semaphore()
+    for mask in seq_masks:
+        pl.semaphore_signal(barrier, inc=1, device_id={"seq": me ^ mask})
+    for mask in rep_masks:
+        pl.semaphore_signal(barrier, inc=1, device_id={"rep": z ^ mask})
+    pl.semaphore_wait(barrier, len(seq_masks) + len(rep_masks))
+
+
+def joined_rows(fulls):
+    return [full.reshape(-1, full.shape[2]) for full in fulls]
+
+
 LOW = jnp.bfloat16
 WIDE = jnp.float32
 LANES = 128
@@ -417,47 +564,6 @@
 
 def cost(flops, size):
     return pl.CostEstimate(flops=flops, bytes_accessed=size, transcendentals=0)
-
-
-def qkv_kernel(x_ref, mod_ref, w_ref, qkv_ref, turned_ref, held):
-    @pl.when(pl.program_id(0) == 0)
-    def _():
-        scaled, shift = 1.0 + mod_ref[1:2], mod_ref[0:1]
-
-        def norm(at):
-            unit, _ = unit_rows(x_ref[at].astype(WIDE))
-            held[at] = (unit * scaled + shift).astype(LOW)
-
-        strips(held.shape[0], norm)
-        turn_into(turned_ref, held)
-
-    qkv_ref[...] = times(held[...], w_ref[...]).astype(LOW)
-
-
-def qkv_forward(x, mod, weight):
-    tokens, features = x.shape
-    steps = weight.shape[1] // features
-    return pl.pallas_call(
-        qkv_kernel,
-        grid=(steps,),
-        in_specs=[
-            whole_block(x.shape),
-            whole_block(mod.shape),
-            pl.BlockSpec((features, features), lambda j: (0, j)),
-        ],
-        out_specs=[
-            pl.BlockSpec((tokens, features), lambda j: (0, j)),
-            whole_block((features, tokens)),
-        ],
-        out_shape=[
-            jax.ShapeDtypeStruct((tokens, weight.shape[1]), LOW),
-            jax.ShapeDtypeStruct((features, tokens), LOW),
-        ],
-        scratch_shapes=[pltpu.VMEM((tokens, features), LOW)],
-        compiler_params=params(40),
-        cost_estimate=cost(2 * tokens * weight.size, 2 * weight.size),
-        name="qkv_forward",
-    )(x, mod, weight)
 
 
 def window(head):
@@ -510,128 +616,6 @@
     barrier = pltpu.get_barrier_semaphore()
     pl.semaphore_signal(barrier, inc=1, device_id={"seq": me ^ 1})
     pl.semaphore_wait(barrier, 1)
-
-
-def attend_kernel(spatial, *refs):
-    qkv_ref, x_ref, mod_ref, w_ref = refs[:4]
-    prob_ref, turned_ref, x1_ref, branch_ref, h2_ref, h2_turned_ref = refs[4:10]
-    if spatial:
-        other_ref, held, total, branch, other, send_sem, arrive_sem, keep_sem = refs[10:]
-    else:
-        held, total, branch = refs[10:]
-    group, groups = pl.program_id(0), pl.num_programs(0)
-    features = x_ref.shape[1]
-
-    if spatial:
-        me = lax.axis_index("seq")
-
-        def exchange(j):
-            return pltpu.make_async_remote_copy(
-                qkv_ref.at[j, :, pl.ds(features, 2 * features)], other.at[j],
-                send_sem.at[j], arrive_sem.at[j], device_id={"seq": me ^ 1},
-            )
-
-        @pl.when(group == 0)
-        def _():
-            sibling_barrier(me)
-            for j in range(other.shape[0]):
-                exchange(j).start()
-
-        exchange(group).wait_recv()
-    else:
-        allowed = same_place()
-
-    for head in range(HEADS):
-        start, wide, _ = window(head)
-        mask = head_mask(head)
-        queries = group_rows(qkv_ref, group, start, wide, spatial) * mask
-        keys = group_rows(qkv_ref, group, features + start, wide, spatial)
-        values = group_rows(qkv_ref, group, 2 * features + start, wide, spatial)
-        if spatial:
-            keys = jnp.concatenate([keys, other[group, :, start : start + wide]], 0)
-            values = jnp.concatenate(
-                [values, other[group, :, features + start : features + start + wide]], 0
-            )
-        scores = times_turned(queries, keys) * HEAD_WIDTH ** (-0.5)
-        if not spatial:
-            scores = jnp.where(allowed, scores, -3e38)
-        grown = jnp.exp(scores - jnp.max(scores, axis=-1, keepdims=True))
-        prob = (grown / jnp.sum(grown, axis=-1, keepdims=True)).astype(LOW)
-        prob_ref[0, head] = prob
-        add_window(total, head, times(prob, values * mask))
-    put_rows(held, group, total[...].astype(LOW), spatial)
-
-    @pl.when(group == groups - 1)
-    def _():
-        if spatial:
-            keep = pltpu.make_async_copy(other, other_ref, keep_sem)
-            keep.start()
-        attended = held[...].reshape(-1, features)
-        branch[...] = times(attended, w_ref[...])
-        for j in range(features // LANES):
-            lanes = slice(j * LANES, (j + 1) * LANES)
-            turned_ref[lanes, :] = attended[:, lanes].T
-        gate, shift, scaled = mod_ref[2:3], mod_ref[3:4], 1.0 + mod_ref[4:5]
-
-        def finish(at):
-            part = branch[at]
-            branch_ref[at] = part.astype(LOW)
-            middle = x_ref[at].astype(WIDE) + gate * part
-            x1_ref[at] = middle
-            unit, _ = unit_rows(middle)
-            h2_ref[at] = (unit * scaled + shift).astype(LOW)
-
-        strips(x_ref.shape[0], finish)
-        turn_into(h2_turned_ref, h2_ref)
-        if spatial:
-            for j in range(other.shape[0]):
-                exchange(j).wait_send()
-            keep.wait()
-
-
-def attention_forward(qkv, x, mod, weight, spatial, groups, cid=None):
-    tokens, features = x.shape
-    span = tokens // groups
-    shape = (groups, span, 3 * features) if spatial else (4, groups, span // 4, 3 * features)
-    rest = shape[:-1]
-    out_shape = [
-        jax.ShapeDtypeStruct((groups, HEADS, span, KEYS), LOW),
-        jax.ShapeDtypeStruct((features, tokens), LOW),
-        jax.ShapeDtypeStruct((tokens, features), WIDE),
-        jax.ShapeDtypeStruct((tokens, features), LOW),
-        jax.ShapeDtypeStruct((tokens, features), LOW),
-        jax.ShapeDtypeStruct((features, tokens), LOW),
-    ]
-    out_specs = [pl.BlockSpec((1, HEADS, span, KEYS), lambda g: (g, 0, 0, 0))]
-    out_specs += [whole_block(o.shape) for o in out_shape[1:]]
-    scratch = [
-        pltpu.VMEM(rest + (features,), LOW),
-        pltpu.VMEM((span, features), WIDE),
-        pltpu.VMEM((tokens, features), WIDE),
-    ]
-    if spatial:
-        both = rest + (2 * features,)
-        out_shape.append(jax.ShapeDtypeStruct(both, LOW))
-        out_specs.append(pl.BlockSpec(memory_space=pl.ANY))
-        scratch += [
-            pltpu.VMEM(both, LOW),
-            pltpu.SemaphoreType.DMA((groups,)),
-            pltpu.SemaphoreType.DMA((groups,)),
-            pltpu.SemaphoreType.DMA(()),
-        ]
-    return pl.pallas_call(
-        functools.partial(attend_kernel, spatial),
-        grid=(groups,),
-        in_specs=[
-            whole_block(shape), whole_block(x.shape), whole_block(mod.shape), whole_block(weight.shape),
-        ],
-        out_specs=out_specs,
-        out_shape=out_shape,
-        scratch_shapes=scratch,
-        compiler_params=params(56, cid),
-        cost_estimate=cost(2 * tokens * (weight.size + 2 * features * KEYS), 4 * qkv.size),
-        name="attend_spatial" if spatial else "attend_temporal",
-    )(qkv.reshape(shape), x, mod, weight)
 
 
 def attend_back_kernel(spatial, *refs):
@@ -796,94 +780,432 @@
     return value * half, slope
 
 
-def mlp_kernel(send, *refs):
-    x1_ref, h2_ref, mod_ref, up_ref, down_ref = refs[:5]
-    turned_ref, slope_ref, out_ref, mlp_ref, total = refs[5:10]
-    step, steps = pl.program_id(0), pl.num_programs(0)
-    half = h2_ref.shape[0] // 2
-
-    for j in range(2):
-        rows = slice(j * half, (j + 1) * half)
-        hidden, slope = gelu_and_slope(times(h2_ref[rows], up_ref[...]))
-        slope_ref[rows] = slope.astype(LOW)
-        hidden = hidden.astype(LOW)
-        turned_ref[:, rows] = hidden.T
-        part = times(hidden, down_ref[...])
-
-        @pl.when(step == 0)
-        def _():
-            total[rows] = part
-
-        @pl.when(step > 0)
-        def _():
-            total[rows] = total[rows] + part
-
-    @pl.when(step == steps - 1)
-    def _():
-        gate = mod_ref[5:6]
-        if send:
-            ready, sems, local_sem = refs[10:]
-            me = lax.axis_index("seq")
-            seq_barrier(me)
-            target = ready
+OUTS = ("qkv", "prob", "h", "o", "h2", "z", "slope", "x1", "branch", "mlp")
+CHUNK = 768
+
+
+def forward_kernel(shapes, *refs):
+    count = len(shapes)
+    shards, refs = refs[:count], refs[count:]
+    partial, condition, tokens, x_ref = refs[:4]
+    fulls, refs = refs[4 : 4 + count], refs[4 + count :]
+    mod_ref, conditions, moved, other_ref, x2_ref, y_ref = refs[:6]
+    outs = [dict(zip(OUTS, refs[6:16])), dict(zip(OUTS, refs[16:26]))]
+    refs = refs[26:]
+    (
+        partials, x2, qkv, other, held, normed, total, middle, part, prob, turned, low, ready,
+        tall, short, hidden, slope, small_sem, move_sem, stay_sem, next_move_sem, next_stay_sem, next_sem,
+        pair_sem, weight_sem, out_sem, prob_sem, chunk_sem,
+    ) = refs[:28]
+    gather = Gather(shapes, (shards, fulls, refs[28:]))
+    me, z = gather.me, gather.z
+    features = x_ref.shape[1]
+    steps = shapes[2][1] // CHUNK
+    enter(range(1, 8), range(1, 4))
+
+    small = []
+    for mask in range(1, 8):
+        small.append(pltpu.make_async_remote_copy(
+            partial, partials.at[me], small_sem.at[0, mask], small_sem.at[1, mask],
+            device_id={"seq": me ^ mask}))
+    for mask in range(1, 4):
+        small.append(pltpu.make_async_remote_copy(
+            condition, conditions.at[z], small_sem.at[0, 7 + mask], small_sem.at[1, 7 + mask],
+            device_id={"rep": z ^ mask}))
+    small.append(pltpu.make_async_copy(partial, partials.at[me], small_sem.at[0, 0]))
+    small.append(pltpu.make_async_copy(condition, conditions.at[z], small_sem.at[1, 0]))
+    for copy in small:
+        copy.start()
+    gather.start()
+    gather.advance(0)
+    later = moves(tokens, moved, move_sem, stay_sem, me, True)
+    for copy in later:
+        copy.start()
+    for copy in small:
+        copy.wait()
+    modulation = partials[0]
+    for device in range(1, 8):
+        modulation = modulation + partials[device]
+    width = features // LANES
+    for row in range(12):
+        for j in range(width):
+            at = row * width + j
+            mod_ref[row // 6, row % 6 : row % 6 + 1, j * LANES : (j + 1) * LANES] = modulation[
+                at : at + 1
+            ]
+
+    pending = {}
+    names = ("turned", "qkv", "other", "low", "middle", "ready")
+
+    def begin(name, source, target):
+        settle(name)
+        pending[name] = pltpu.make_async_copy(source, target, out_sem.at[names.index(name)])
+        pending[name].start()
+
+    def settle(name):
+        copy = pending.pop(name, None)
+        if copy is not None:
+            copy.wait()
+
+    def full(weight):
+        return fulls[weight]
+
+    def load(slot, source):
+        return pltpu.make_async_copy(source, tall.at[slot], weight_sem.at[slot])
+
+    def column_block(weight, column):
+        return full(weight).at[:, :, pl.ds(column, features)]
+
+    def exchange(j):
+        return pltpu.make_async_remote_copy(
+            qkv.at[pl.ds(2 * j, 2), :, pl.ds(features, 2 * features)], other.at[pl.ds(2 * j, 2)],
+            pair_sem.at[0, j], pair_sem.at[1, j], device_id={"seq": me ^ 1},
+        )
+
+    def rows_of(ref, group, column, wide, spatial):
+        lanes = slice(column, column + wide)
+        if spatial:
+            return ref[pl.ds(2 * group, 2), :, lanes].reshape(-1, wide)
+        return jnp.concatenate([ref[2 * block + group, :, lanes] for block in range(4)], 0)
+
+    def attend(layer, spatial, group, span, allowed):
+        for head in range(HEADS):
+            start, wide, _ = window(head)
+            mask = head_mask(head)
+            queries = rows_of(qkv, group, start, wide, spatial) * mask
+            keys = rows_of(qkv, group, features + start, wide, spatial)
+            values = rows_of(qkv, group, 2 * features + start, wide, spatial)
+            if spatial:
+                keys = jnp.concatenate([keys, rows_of(other, group, start, wide, True)], 0)
+                values = jnp.concatenate(
+                    [values, rows_of(other, group, features + start, wide, True)], 0
+                )
+            scores = times_turned(queries, keys) * HEAD_WIDTH ** (-0.5)
+            if not spatial:
+                scores = jnp.where(allowed, scores, -3e38)
+            grown = jnp.exp(scores - jnp.max(scores, axis=-1, keepdims=True))
+            chance = (grown / jnp.sum(grown, axis=-1, keepdims=True)).astype(LOW)
+            prob[head, :span] = chance
+            add_window(part.at[pl.ds(0, span)], head, times(chance, values * mask))
+        got = part[:span].astype(LOW)
+        if spatial:
+            held[pl.ds(2 * group, 2)] = got.reshape(2, -1, features)
         else:
-            target = out_ref
-        per = target.shape[1] if send else target.shape[0]
+            for block in range(4):
+                held[2 * block + group] = got[block * 64 : (block + 1) * 64]
+
+    def flat_rows(ref):
+        return ref[...].reshape(-1, features)
+
+    def turn_out(source, target):
+        settle("turned")
+        for j in range(features // LANES):
+            lanes = slice(j * LANES, (j + 1) * LANES)
+            turned[lanes, :] = source[:, lanes].T
+        begin("turned", turned, target)
+
+    def layer(at_layer, spatial, x, plan):
+        first = 4 * at_layer
+        out = outs[at_layer]
+        groups = 4 if spatial else 2
+        span = x.shape[0] // groups
+        mod = mod_ref.at[at_layer]
+
+        def go(place):
+            for at in plan.get(place, ()):
+                if at is None:
+                    gather.share(len(gather.pieces) - 1)
+                else:
+                    gather.advance(at)
+
+        def go_when(place, index):
+            for key, pieces in plan.items():
+                if isinstance(key, tuple) and key[0] == place:
+                    @pl.when(index == key[1])
+                    def _():
+                        for at in pieces:
+                            gather.advance(at)
+
+        scaled, shift = 1.0 + mod[1:2], mod[0:1]
+
+        def norm(at):
+            unit, _ = unit_rows(x[at].astype(WIDE))
+            normed[at] = (unit * scaled + shift).astype(LOW)
+
+        strips(x.shape[0], norm)
+        turn_out(normed[...], out["h"])
+        go("norm")
+        gather.ready(first)
+        load(0, column_block(first, 0)).start()
+        settle("qkv")
+        for j in range(3):
+            load(j % 2, column_block(first, 0)).wait()
+            if j < 2:
+                load((j + 1) % 2, column_block(first, (j + 1) * features)).start()
+            got = times(normed[...], tall[j % 2].reshape(features, features)).astype(LOW)
+            qkv[:, :, j * features : (j + 1) * features] = got.reshape(8, -1, features)
+            go(f"qkv{j}")
+        begin("qkv", qkv, out["qkv"])
+        if spatial:
+            for j in range(groups):
+                exchange(j).start()
+        allowed = None if spatial else same_place()
+
+        def prob_copy(group):
+            return pltpu.make_async_copy(
+                prob.at[:, pl.ds(0, span)], out["prob"].at[group], prob_sem
+            )
+
+        def one_group(group, carry):
+            go_when("group", group)
+            if spatial:
+                exchange(group).wait_recv()
+
+            @pl.when(group > 0)
+            def _():
+                prob_copy(group).wait()
+
+            attend(at_layer, spatial, group, span, allowed)
+            prob_copy(group).start()
+            return carry
+
+        lax.fori_loop(0, groups, one_group, 0)
+        prob_copy(0).wait()
+        if spatial:
+            begin("other", other, other_ref)
+            for j in range(groups):
+                exchange(j).wait_send()
+        go("attended")
+        gather.ready(first + 1)
+        load(0, full(first + 1)).start()
+        attended = flat_rows(held)
+        turn_out(attended, out["o"])
+        load(0, full(first + 1)).wait()
+        total[...] = times(attended, tall[0].reshape(features, features))
+        gate, move, grow = mod[2:3], mod[3:4], 1.0 + mod[4:5]
+        settle("low")
+        settle("middle")
 
         def finish(at):
-            mlp = total[at]
-            mlp_ref[at] = mlp.astype(LOW)
-            total[at] = x1_ref[at] + gate * mlp
-
-        strips(total.shape[0], finish)
-        if send:
-            ready[...] = total[...].astype(LOW).reshape(ready.shape)
-            copies = moves(ready, out_ref, sems, local_sem, me, True)
+            branch = total[at]
+            low[at] = branch.astype(LOW)
+            got = x[at].astype(WIDE) + gate * branch
+            middle[at] = got
+            unit, _ = unit_rows(got)
+            normed[at] = (unit * grow + move).astype(LOW)
+
+        strips(x.shape[0], finish)
+        begin("low", low, out["branch"])
+        begin("middle", middle, out["x1"])
+        turn_out(normed[...], out["h2"])
+        go("middle")
+        gather.ready(first + 2)
+        gather.ready(first + 3)
+
+        down = full(first + 3)
+        per = down.shape[0] * down.shape[1] // steps
+
+        def chunk_loads(step, slot):
+            column = pl.multiple_of(step * CHUNK, CHUNK)
+            owner = step * CHUNK // down.shape[1]
+            copies = [
+                pltpu.make_async_copy(
+                    full(first + 2).at[:, :, pl.ds(column, CHUNK)],
+                    tall.at[slot, :, :, pl.ds(0, CHUNK)], weight_sem.at[slot],
+                )
+            ]
+            return copies, column, owner
+
+        def start_loads(step, slot):
+            copies, column, owner = chunk_loads(step, slot)
             for copy in copies:
                 copy.start()
-            for copy in copies:
+            pltpu.make_async_copy(
+                down_rows(step), short.at[slot], weight_sem.at[2 + slot]
+            ).start()
+
+        def down_rows(step):
+            return fulls_flat[at_layer].at[pl.ds(pl.multiple_of(step * 4, 4), 4)]
+
+        fulls_flat = [fulls[3].reshape(*split_rows(fulls[3].shape)), fulls[7].reshape(*split_rows(fulls[7].shape))]
+
+        def wait_loads(slot):
+            for copy in chunk_loads(0, slot)[0]:
                 copy.wait()
-        else:
-            out_ref[...] = total[...].astype(LOW)
-
-
-def mlp_forward(x1, h2, mod, up, down, frames=None, cid=None):
-    tokens, features = x1.shape
-    wide = up.shape[1]
-    block = 768
-    out_shape = [
-        jax.ShapeDtypeStruct((wide, tokens), LOW),
-        jax.ShapeDtypeStruct((tokens, wide), LOW),
-        jax.ShapeDtypeStruct((tokens, features), LOW),
-        jax.ShapeDtypeStruct((tokens, features), LOW),
+            pltpu.make_async_copy(down_rows(0), short.at[slot], weight_sem.at[2 + slot]).wait()
+
+        def chunk_outs(step, slot):
+            column = pl.multiple_of(step * CHUNK, CHUNK)
+            return (
+                pltpu.make_async_copy(
+                    hidden.at[slot], out["z"].at[pl.ds(column, CHUNK)], chunk_sem.at[0, slot]
+                ),
+                pltpu.make_async_copy(
+                    slope.at[slot], out["slope"].at[:, pl.ds(column, CHUNK)], chunk_sem.at[1, slot]
+                ),
+            )
+
+        start_loads(0, 0)
+        half = x.shape[0] // 2
+
+        def chunk(step, carry):
+            slot = lax.rem(step, 2)
+            go_when("chunk", step)
+            wait_loads(slot)
+
+            @pl.when(step + 1 < steps)
+            def _():
+                start_loads(step + 1, 1 - slot)
+
+            @pl.when(step >= 2)
+            def _():
+                for copy in chunk_outs(step, slot):
+                    copy.wait()
+
+            up = tall[slot, :, :, :CHUNK].reshape(features, CHUNK)
+            for j in range(2):
+                rows = slice(j * half, (j + 1) * half)
+                value, bend = gelu_and_slope(times(normed[rows], up))
+                slope[slot, rows] = bend.astype(LOW)
+                value = value.astype(LOW)
+                hidden[slot, :, rows] = value.T
+                got = times(value, short[slot].reshape(CHUNK, features))
+
+                @pl.when(step == 0)
+                def _():
+                    total[rows] = got
+
+                @pl.when(step > 0)
+                def _():
+                    total[rows] = total[rows] + got
+
+            for copy in chunk_outs(step, slot):
+                copy.start()
+            return carry
+
+        lax.fori_loop(0, steps, chunk, 0)
+        for slot in range(2):
+            for copy in chunk_outs(0, slot):
+                copy.wait()
+        last = mod[5:6]
+        settle("low")
+
+        def close(at):
+            mlp = total[at]
+            low[at] = mlp.astype(LOW)
+            total[at] = middle[at] + last * mlp
+
+        strips(x.shape[0], close)
+        begin("low", low, out["mlp"])
+        ready[...] = total[...].astype(LOW).reshape(ready.shape)
+
+    layer(0, True, x_ref, {
+        "norm": (1, 2, 3), "qkv1": (4,), ("group", 0): (5,), ("group", 1): (6,), ("group", 2): (7,),
+        ("group", 3): (8,), "attended": (9,), "middle": (10, 11, 12), ("chunk", 1): (13,),
+        ("chunk", 3): (14,), ("chunk", 4): (15,),
+    })
+    copies = moves(ready, x2_ref, next_move_sem, next_stay_sem, me, True)
+    for copy in later:
+        copy.wait()
+    for copy in copies:
+        copy.start()
+    gather.local(4)
+    gather.advance(16)
+    gather.advance(17)
+    for copy in copies:
+        copy.wait()
+    fetch = pltpu.make_async_copy(x2_ref, x2, next_sem)
+    fetch.start()
+    fetch.wait()
+    x2_rows = x2.reshape(x_ref.shape)
+    layer(1, False, x2_rows, {
+        "norm": (18,), "qkv0": (19,), "qkv2": (20,), ("group", 1): (21,), "attended": (22,),
+        "middle": (23, None),
+    })
+    begin("ready", ready, y_ref)
+    for name in names:
+        settle(name)
+    gather.finish()
+
+
+def split_rows(shape):
+    return (shape[0] * shape[1] // (CHUNK // 4), CHUNK // 4, shape[2])
+
+
+def forward(shards, partial, condition, cotangent, x, cid):
+    shapes = [shard.shape for shard in shards]
+    count = len(shapes)
+    tokens, features = x.shape
+    frames, places, _ = cotangent.shape
+    wide = shapes[2][1]
+    any_ = pl.BlockSpec(memory_space=pl.ANY)
+    struct = jax.ShapeDtypeStruct
+    moved = struct((8, frames, places // 8, features), LOW)
+    outs = Gather.outs(shapes) + [
+        struct((2, 6, features), WIDE),
+        struct((4,) + condition.shape, condition.dtype),
+        moved,
+        struct((8, tokens // 8, 2 * features), LOW),
+        moved,
+        struct((frames, places, features), LOW),
     ]
-    scratch = [pltpu.VMEM((tokens, features), WIDE)]
-    send = frames is not None
-    if send:
-        places = tokens // frames
-        out_shape[2] = jax.ShapeDtypeStruct((8, frames, places // 8, features), LOW)
-        scratch += [pltpu.VMEM((frames, places, features), LOW)] + move_scratch()
-    out_specs = [
-        pl.BlockSpec((block, tokens), lambda j: (j, 0)),
-        pl.BlockSpec((tokens, block), lambda j: (0, j)),
-        pl.BlockSpec(memory_space=pl.ANY) if send else whole_block((tokens, features)),
-        whole_block((tokens, features)),
-    ]
-    return pl.pallas_call(
-        functools.partial(mlp_kernel, send),
-        grid=(wide // block,),
-        in_specs=[
-            whole_block(x1.shape), whole_block(h2.shape), whole_block(mod.shape),
-            pl.BlockSpec((features, block), lambda j: (0, j)),
-            pl.BlockSpec((block, features), lambda j: (j, 0)),
-        ],
-        out_specs=out_specs,
-        out_shape=out_shape,
-        scratch_shapes=scratch,
-        compiler_params=params(56, cid),
-        cost_estimate=cost(4 * tokens * up.size, 4 * up.size),
-        name="mlp_forward",
-    )(x1, h2, mod, up, down)
+    for groups in (4, 2):
+        outs += [
+            struct((8, tokens // 8, 3 * features), LOW),
+            struct((groups, HEADS, tokens // groups, KEYS), LOW),
+            struct((features, tokens), LOW),
+            struct((features, tokens), LOW),
+            struct((features, tokens), LOW),
+            struct((wide, tokens), LOW),
+            struct((tokens, wide), LOW),
+            struct((tokens, features), WIDE),
+            struct((tokens, features), LOW),
+            struct((tokens, features), LOW),
+        ]
+    dma = pltpu.SemaphoreType.DMA
+    vm = pltpu.VMEM
+    flops = 2 * tokens * 8 * sum(shape[0] * shape[1] for shape in shapes)
+    got = pl.pallas_call(
+        functools.partial(forward_kernel, shapes),
+        out_shape=outs,
+        in_specs=[any_] * (count + 3) + [pl.BlockSpec(memory_space=vm)],
+        out_specs=[any_] * count + [pl.BlockSpec(memory_space=vm)] + [any_] * (len(outs) - count - 1),
+        scratch_shapes=[
+            vm((8,) + partial.shape, WIDE),
+            vm(moved.shape, LOW),
+            vm((8, tokens // 8, 3 * features), LOW),
+            vm((8, tokens // 8, 2 * features), LOW),
+            vm((8, tokens // 8, features), LOW),
+            vm((tokens, features), LOW),
+            vm((tokens, features), WIDE),
+            vm((tokens, features), WIDE),
+            vm((KEYS, features), WIDE),
+            vm((HEADS, KEYS, KEYS), LOW),
+            vm((features, tokens), LOW),
+            vm((tokens, features), LOW),
+            vm((frames, places, features), LOW),
+            vm((2, 8, features // 8, features), LOW),
+            vm((2, 4, CHUNK // 4, features), LOW),
+            vm((2, CHUNK, tokens), LOW),
+            vm((2, tokens, CHUNK), LOW),
+            dma((2, 11)),
+            *move_scratch(),
+            *move_scratch(),
+            dma(()),
+            dma((2, 4)),
+            dma((4,)),
+            dma((8,)),
+            dma(()),
+            dma((2, 2)),
+        ]
+        + Gather.scratch(shapes),
+        compiler_params=params(60, cid),
+        cost_estimate=cost(flops, 4 * flops // tokens),
+        name="forward",
+    )(*shards, partial, condition, cotangent, x)
+    weights = joined_rows(got[:count])
+    named = [dict(zip(OUTS, got[count + 6 + 10 * at : count + 16 + 10 * at])) for at in range(2)]
+    return weights, got[count : count + 6], named
 
 
 def mlp_back_kernel(send, *refs):
@@ -1075,161 +1397,6 @@
         cost_estimate=cost(2 * tokens * weight.size, 2 * weight.size),
         name="qkv_backward",
     )(dqkv, weight, x, dx1, mod)
-
-
-AHEAD = 2
-
-
-def gather_pieces(shapes):
-    pieces = []
-    for at, (rows, columns) in enumerate(shapes):
-        last = at == len(shapes) - 1
-        if rows > columns // 3:
-            parts = 4 if last else 2
-            tall = rows // parts
-            pieces += [(at, j * tall, tall, 0, columns) for j in range(parts)]
-        elif columns % 256 == 0 and columns > 2048:
-            wide = columns // 2
-            pieces += [(at, 0, rows, j * wide, wide) for j in range(2)]
-        else:
-            pieces.append((at, 0, rows, 0, columns))
-    return pieces
-
-
-def gather_kernel(pieces, count, *refs):
-    shards, partial, condition, tokens = refs[:count], *refs[count : count + 3]
-    fulls = refs[count + 3 : 2 * count + 3]
-    partials, conditions, moved = refs[2 * count + 3 : 2 * count + 6]
-    held = refs[2 * count + 6 : 3 * count + 6]
-    (
-        first_sem, second_sem, rep_sem, pair_sem, local_sem, small_sem, move_sem, stay_sem,
-    ) = refs[3 * count + 6 :]
-    me, z = lax.axis_index("seq"), lax.axis_index("rep")
-    odd = z & 1
-    first, second = 2 + 2 * odd, 4 - 2 * odd
-
-    barrier = pltpu.get_barrier_semaphore()
-    for mask in range(1, 8):
-        pl.semaphore_signal(barrier, inc=1, device_id={"seq": me ^ mask})
-    for mask in range(1, 4):
-        pl.semaphore_signal(barrier, inc=1, device_id={"rep": z ^ mask})
-    pl.semaphore_wait(barrier, 10)
-
-    small = []
-    for mask in range(1, 8):
-        small.append(pltpu.make_async_remote_copy(
-            partial, partials.at[me], small_sem.at[0, mask], small_sem.at[1, mask],
-            device_id={"seq": me ^ mask}))
-    for mask in range(1, 4):
-        small.append(pltpu.make_async_remote_copy(
-            condition, conditions.at[z], small_sem.at[0, 7 + mask], small_sem.at[1, 7 + mask],
-            device_id={"rep": z ^ mask}))
-    small.append(pltpu.make_async_copy(partial, partials.at[me], small_sem.at[0, 0]))
-    small.append(pltpu.make_async_copy(condition, conditions.at[z], small_sem.at[1, 0]))
-    small += moves(tokens, moved, move_sem, stay_sem, me, True)
-    for copy in small:
-        copy.start()
-
-    def place(owner, piece):
-        at, row, rows, column, columns = piece
-        return fulls[at].at[owner, pl.ds(row, rows), pl.ds(column, columns)]
-
-    def own(piece):
-        at, row, rows, column, columns = piece
-        return shards[at].at[pl.ds(row, rows), pl.ds(column, columns)]
-
-    def send(source, owner, piece, sems, at, target):
-        return pltpu.make_async_remote_copy(
-            source, place(owner, piece), sems.at[0, at], sems.at[1, at], device_id=target)
-
-    firsts, pairs, others, stores = [], [], [], []
-    fetches = [
-        pltpu.make_async_copy(shard, hold, local_sem.at[0, at])
-        for at, (shard, hold) in enumerate(zip(shards, held))
-    ]
-    for copy in fetches:
-        copy.start()
-
-    def begin(at):
-        piece = pieces[at]
-        copy = send(own(piece), me, piece, first_sem, at, {"seq": me ^ first})
-        copy.start()
-        firsts.append(copy)
-        copy = send(own(piece), me, piece, pair_sem.at[0], at, {"seq": me ^ 1})
-        copy.start()
-        pairs.append(copy)
-
-    for at in range(AHEAD):
-        begin(at)
-    for at, copy in enumerate(fetches):
-        copy.wait()
-        stores.append(pltpu.make_async_copy(held[at], fulls[at].at[me], local_sem.at[1, at]))
-        stores[-1].start()
-
-    def forward(at):
-        others[at][0].wait_recv()
-        others[at][1].wait_recv()
-        piece = pieces[at]
-        for which, mask in ((2, first ^ second), (3, second)):
-            owner = me ^ mask
-            copy = send(place(owner, piece), owner, piece, pair_sem.at[which], at, {"seq": me ^ 1})
-            copy.start()
-            pairs.append(copy)
-
-    for at, piece in enumerate(pieces):
-        firsts[at].wait_recv()
-        if at + AHEAD < len(pieces):
-            begin(at + AHEAD)
-        owner = me ^ first
-        two = [
-            send(place(owner, piece), owner, piece, second_sem, at, {"seq": me ^ second}),
-            send(place(owner, piece), owner, piece, rep_sem, at, {"rep": z ^ 1}),
-        ]
-        copy = send(place(owner, piece), owner, piece, pair_sem.at[1], at, {"seq": me ^ 1})
-        for each in two + [copy]:
-            each.start()
-        others.append(two)
-        pairs.append(copy)
-        if at:
-            forward(at - 1)
-    forward(len(pieces) - 1)
-    for copy in firsts:
-        copy.wait_send()
-    for two in others:
-        for copy in two:
-            copy.wait_send()
-    for copy in pairs + stores + small:
-        copy.wait()
-
-
-def gather_weights(shards, partial, condition, tokens, cid):
-    shapes = [shard.shape for shard in shards]
-    pieces = gather_pieces(shapes)
-    count = len(shards)
-    dma = pltpu.SemaphoreType.DMA
-    size = len(pieces)
-    outs = [jax.ShapeDtypeStruct((8,) + shape, jnp.bfloat16) for shape in shapes]
-    outs.append(jax.ShapeDtypeStruct((8,) + partial.shape, partial.dtype))
-    outs.append(jax.ShapeDtypeStruct((4,) + condition.shape, condition.dtype))
-    frames, places, features = tokens.shape
-    outs.append(jax.ShapeDtypeStruct((8, frames, places // 8, features), tokens.dtype))
-    got = pl.pallas_call(
-        functools.partial(gather_kernel, pieces, count),
-        out_shape=outs,
-        in_specs=[pl.BlockSpec(memory_space=pl.ANY)] * (count + 3),
-        out_specs=[pl.BlockSpec(memory_space=pl.ANY)] * len(outs),
-        scratch_shapes=[pltpu.VMEM(shape, jnp.bfloat16) for shape in shapes]
-        + [
-            dma((2, size)), dma((2, size)), dma((2, size)), dma((4, 2, size)), dma((2, count)), dma((2, 11)),
-        ]
-        + move_scratch(),
-        compiler_params=pltpu.CompilerParams(
-            collective_id=cid, has_side_effects=True,
-        ),
-        name="gather_weights",
-    )(*shards, partial, condition, tokens)
-    fulls = [full.reshape(-1, full.shape[2]) for full in got[:count]]
-    return fulls, got[count:]
 
 
 SLOTS = 3
@@ -1587,26 +1754,15 @@
     return (*shaped, *rights)
 
 
-def layer_forward(x, mod, weights, spatial, groups, frames=None, cids=(None, None)):
+def layer_backward(g, x, mod, weights, kept, other, spatial, done=None, frames=None, cids=(None,) * 3):
     qkv_w, out_w, up_w, down_w = weights
-    qkv, h_turned = qkv_forward(x, mod, qkv_w)
-    prob, o_turned, x1, branch, h2, h2_turned, *other = attention_forward(
-        qkv, x, mod, out_w, spatial, groups, cids[0]
-    )
-    z_turned, slope, out, mlp = mlp_forward(x1, h2, mod, up_w, down_w, frames, cids[1])
-    lefts = (h_turned, o_turned, h2_turned, z_turned)
-    return out, (qkv, prob, other[0] if spatial else None, x1, branch, slope, mlp), lefts
-
-
-def layer_backward(g, x, mod, weights, kept, lefts, spatial, done=None, frames=None, cids=(None,) * 3):
-    qkv_w, out_w, up_w, down_w = weights
-    qkv, prob, other, x1, branch, slope, mlp = kept
     du, df, dx1, da, sums, *moved = mlp_backward(
-        g, x1, branch, mlp, mod, up_w, down_w, slope, done, cids[0]
-    )
-    dqkv = attention_backward(da, qkv, prob, out_w, other, spatial, cids[1])
+        g, kept["x1"], kept["branch"], kept["mlp"], mod, up_w, down_w, kept["slope"], done, cids[0]
+    )
+    dqkv = attention_backward(da, kept["qkv"], kept["prob"], out_w, other, spatial, cids[1])
     dx, last_sums = qkv_backward(dqkv, qkv_w, x, dx1, mod, frames, cids[2])
     mod_grad = jnp.concatenate([last_sums[:2], sums[:4]], 0).reshape(1, -1)
+    lefts = [kept[name] for name in ("h", "o", "h2", "z")]
     return dx, moved, mod_grad, reduce_operands(lefts, (dqkv, da, du, df))
 
 
@@ -1614,25 +1770,18 @@
     _, _, frames, places, features = frames_in.shape
     tokens = frames * places
     low_cotangent = cotangent.reshape(frames, places, features).astype(LOW)
-    weights, (partials, conditions, g_two) = gather_weights(
-        shards, partial_mod.reshape(-1, LANES), conditioning.reshape(-1, LANES), low_cotangent, 0
-    )
-    modulation = jnp.sum(partials, 0).reshape(2, 6, features)
-    mod_one, mod_two = modulation[0], modulation[1]
-    weights_one, weights_two = weights[:4], weights[4:]
     x_one = frames_in.reshape(tokens, features)
-    x_two, kept_one, lefts_one = layer_forward(
-        x_one, mod_one, weights_one, True, frames, frames, (2, 4)
-    )
-    x_two = x_two.reshape(tokens, features)
-    y_two, kept_two, lefts_two = layer_forward(x_two, mod_two, weights_two, False, 2)
+    weights, (mods, conditions, g_two, other, x_two, y_two), (kept_one, kept_two) = forward(
+        shards, partial_mod.reshape(-1, LANES), conditioning.reshape(-1, LANES), low_cotangent,
+        x_one, 0,
+    )
     g_one, (block_out,), mod_grad_two, operands_two = layer_backward(
-        g_two.reshape(tokens, features), x_two, mod_two, weights_two, kept_two, lefts_two, False,
-        y_two.reshape(g_two.shape), frames, (5, None, 6),
+        g_two.reshape(tokens, features), x_two.reshape(tokens, features), mods[1], weights[4:],
+        kept_two, None, False, y_two.reshape(g_two.shape), frames, (5, None, 6),
     )
     input_grad, _, mod_grad_one, operands_one = layer_backward(
-        g_one.reshape(tokens, features), x_one, mod_one, weights_one, kept_one, lefts_one, True,
-        cids=(None, 3, None),
+        g_one.reshape(tokens, features), x_one, mods[0], weights[:4], kept_one,
+        other.reshape(frames, places, 2 * features), True, cids=(None, 3, None),
     )
     mod_grads = jnp.concatenate([mod_grad_one, mod_grad_two], 1).astype(LOW)
     (grads_two, grads_one), every_mod = reduce_grads(

time: 882 us -> 777 us (0.88)
  Pallas kernels: 820 us -> 727 us
  local copies, waits for them, and re-layouts: 33.3 us -> 22.3 us
    pallas_call x7 -> x1, Pallas kernels: 355 us -> 263 us  [forward(): pl.pallas_call(functools.partial(forward_kernel, shapes), out_shape=outs,...]
    unnamed x70 -> x54, local copies, waits for them, and re-layouts: 31.7 us -> 19.3 us
where the time goes in v4:
time: 777 us; the launch traced here: 767 us
  Pallas kernels  727 us (94%)
  local copies, waits for them, and re-layouts  22.3 us (3%)
  matrix products  9.98 us (1%)
    pallas_call x1, Pallas kernels, reduce_grads(): pl.pallas_call(functools.partial(reduce_kernel, len(layers), rows, width,...  310 us
    pallas_call x1, Pallas kernels, forward(): pl.pallas_call(functools.partial(forward_kernel, shapes), out_shape=outs,...  263 us
    pallas_call x2, Pallas kernels, mlp_backward(): pl.pallas_call(functools.partial(mlp_back_kernel, send), grid=(wide // bl...  60.3 us
    pallas_call x2, Pallas kernels, attention_backward(): pl.pallas_call(functools.partial(attend_back_kernel, spatial), grid=(grou...  52.7 us
    pallas_call x2, Pallas kernels, qkv_backward(): pl.pallas_call(functools.partial(qkv_back_kernel, send), grid=(steps,), i...  40 us
    unnamed x54, local copies, waits for them, and re-layouts  19.3 us

profile of v4, /device:TPU:0, one launch (start us, length us, event | category | flops | bytes accessed | tf_op | source)
XLA Modules:
  0.0 766.9 jit_solution(12634185548103444740)
XLA Ops:
  0.6 0.0 copy-start
  0.7 1.4 reduce.1
  2.1 2.2 fusion.11
  4.3 1.1 fusion.9
  5.4 0.8 maximum_reduce_fusion
  6.2 1.1 convert_bitcast_fusion.refs_10_
  7.3 263.5 %forward.1 = (bf16[8,144,3456]{2,1,0:T(8,128)(2,1)}, bf16[8,144,1152]{2,1,0:T(8,128)(2,1)}, bf16[8,144,4608]{2,1,0:T(8,128)(2,1)}, bf16[8,576,1152]{2,1,0:T(8,12...) custom-call(bf16[144,3456]{1,0:T(8,128)(2,1)} %refs_0_.1, ...), custom_call_target="tpu_custom_call" | custom-call | flops 32614907904 | bytes 254803968 | tf_op jit(solution)/shard_map/forward/pallas_call | solution.py:1168
  270.8 0.8 copy.33
  271.6 1.4 slice_bitcast_fusion
  273.0 31.3 %mlp_backward.2 = (bf16[512,4608]{1,0:T(8,128)(2,1)}, bf16[512,1152]{1,0:T(8,128)(2,1)}, f32[512,1152]{1,0:T(8,128)}, bf16[512,1152]{1,0:T(8,128)(2,1)}, f32[8,1...) custom-call(bf16[512,1152]{1,0:T(8,128)(2,1)} %bitcast.117, f32[512,1152]{1,0:T(8,128)} %get-tuple-element.72.refs_1_, ...), custom_call_target="tpu_custom_call" | custom-call | flops 10871635968 | bytes 21233664 | tf_op jit(solution)/shard_map/mlp_backward/pallas_call | solution.py:1313
  304.3 0.0 copy-start.3
  304.3 20.3 %attend_temporal_back.1 = bf16[4,2,64,3456]{3,2,1,0:T(8,128)(2,1)} custom-call(bf16[512,1152]{1,0:T(8,128)(2,1)} %get-tuple-element.81.refs_0_.refs_5_, bf16[4,2,64,3456]{3,2,1,0:T(8,128)(2,1)} %bitcast.84, bf16[2,16,256,256]{3,2,1,0:T(8,128)(2,1)} %get-tuple-element.83.refs_2_, bf16[1152,1152]{1,0:T(8,128)(2,1)} %bitcast.88), custom_call_target="tpu_custom_call" | custom-call | flops 2868903936 | bytes 7077888 | tf_op jit(solution)/shard_map/attend_temporal_back/pallas_call | solution.py:730
  324.6 0.0 copy-done.3
  324.7 27.4 %qkv_backward.2 = (bf16[4,128,1152]{2,1,0:T(8,128)(2,1)S(1)}, f32[8,1152]{1,0:T(8,128)S(1)}) custom-call(bf16[512,3456]{1,0:T(8,128)(2,1)} %bitcast.82, bf16[1152,3456]{1,0:T(8,128)(2,1)} %bitcast.110, bf16[512,1152]{1,0:T(8,128)(2,1)S(1)} %bitcast.80, f32[512,1152]{1,0:T(8,128)S(1)} %copy-done.10, f32[6,1152]{1,0:T(8,128)S(1)} %copy-done.3), custom_call_target="tpu_custom_call" | custom-call | flops 4076863488 | bytes 7962624 | tf_op jit(solution)/shard_map/qkv_backward/pallas_call | solution.py:1382
  352.1 0.0 copy-start.9
  352.1 1.0 copy-done.9
  353.1 29.0 %mlp_backward.3 = (bf16[512,4608]{1,0:T(8,128)(2,1)}, bf16[512,1152]{1,0:T(8,128)(2,1)}, f32[512,1152]{1,0:T(8,128)}, bf16[512,1152]{1,0:T(8,128)(2,1)}, f32[8,1152]{1,0:T(8,128)}) custom-call(bf16[512,1152]{1,0:T(8,128)(2,1)} %bitcast.81, f32[512,1152]{1,0:T(8,128)} %get-tuple-element.89.refs_1_, bf16[512,1152]{1,0:T(8,128)(2,1)} %get-tuple-element.90.refs_2_, ...), custom_call_target="tpu_custom_call" | custom-call | flops 10871635968 | bytes 21233664 | tf_op jit(solution)/shard_map/mlp_backward/pallas_call | solution.py:1313
  382.1 0.0 copy-start.2
  382.1 0.0 copy-start.4
  382.2 32.4 %attend_spatial_back.1 = bf16[4,128,3456]{2,1,0:T(8,128)(2,1)} custom-call(bf16[512,1152]{1,0:T(8,128)(2,1)} %get-tuple-element.95.refs_0_.refs_13_, bf16[4,128,3456]{2,1,0:T(8,128)(2,1)} %bitcast.85, bf16[4,16,128,256]{3,2,1,0:T(8,128)(2,1)} %get-tuple-element.97.refs_2_, bf16[1152,1152]{1,0:T(8,128)(2,1)} %bitcast.89, bf16[4,128,2304]{2,1,0:T(8,128)(2,1)} %bitcast.90), custom_call_target="tpu_custom_call" | custom-call | flops 2868903936 | bytes 7077888 | tf_op jit(solution)/shard_map/attend_spatial_back/pallas_call | solution.py:730
  414.6 0.0 copy-start.11
  414.6 1.7 copy-done.11
  416.3 12.6 %qkv_backward.3 = (f32[512,1152]{1,0:T(8,128)}, f32[8,1152]{1,0:T(8,128)S(1)}) custom-call(bf16[512,3456]{1,0:T(8,128)(2,1)} %bitcast.86, bf16[1152,3456]{1,0:T(8,128)(2,1)} %bitcast.109, bf16[512,1152]{1,0:T(8,128)(2,1)S(1)} %bitcast.76, f32[512,1152]{1,0:T(8,128)S(1)} %copy-done.11, f32[6,1152]{1,0:T(8,128)S(1)} %copy-done.2), custom_call_target="tpu_custom_call" | custom-call | flops 4076863488 | bytes 7962624 | tf_op jit(solution)/shard_map/qkv_backward/pallas_call | solution.py:1382
  428.8 0.8 slice.61
  429.6 0.8 slice.60
  430.5 0.2 maximum_reduce_fusion.1
  430.7 310.3 %reduce_grads.1 = (f32[144,3456]{1,0:T(8,128)}, f32[144,1152]{1,0:T(8,128)S(1)}, f32[144,4608]{1,0:T(8,128)}, f32[576,1152]{1,0:T(8,128)}, f32[144,3456]{1,0:T(8...) custom-call(bf16[4,2,144,512]{3,2,1,0:T(8,128)(2,1)S(1)} %bitcast.77, ...), custom_call_target="tpu_custom_call" | custom-call | flops 32614907904 | bytes 16146432 | tf_op jit(solution)/shard_map/reduce_grads/pallas_call | solution.py:1703
  741.0 0.0 copy-start.12
  741.1 0.6 fusion.4
  741.7 0.9 copy-done.12
  742.6 0.6 fusion.5
  743.2 1.4 fusion.8
  744.6 1.6 bitcast_convert_fusion
  746.1 2.7 fusion
  748.9 2.7 fusion.2
  751.6 1.3 copy.42
  752.9 0.8 copy.43
  753.8 0.6 copy-done.16
  754.4 1.5 copy.44
  755.9 1.2 copy-done.15
  757.1 1.5 copy.45
  758.6 1.0 copy-done.18
  759.6 1.3 copy.46
  760.9 0.8 copy.47
  761.7 0.6 copy-done.14
  762.3 1.5 copy.48
  763.8 1.2 copy-done.13
  765.0 1.5 copy.49
  (34 shorter events, 0.2 us)
Async XLA Ops:
  0.6 3.6 copy-start
  2.1 4.1 copy-start.17
  304.3 20.4 %copy-start.3 = (f32[6,1152]{1,0:T(8,128)S(1)}, f32[6,1152]{1,0:T(8,128)}, u32[]{:S(2)}) copy-start(f32[6,1152]{1,0:T(8,128)} %get-tuple-element.130.refs_4_) | copy-start | bytes 82948
  304.3 20.3 %copy-start.8 = (bf16[8,4,16,1152]{3,2,1,0:T(8,128)(2,1)S(1)}, bf16[8,4,16,1152]{3,2,1,0:T(8,128)(2,1)}, u32[]{:S(2)}) copy-start(bf16[8,4,16,1152]{3,2,1,0:T(8,128)(2,1)} %get-tuple-element.86) | copy-start | bytes 3538948
  304.3 20.3 %copy-start.10 = (f32[512,1152]{1,0:T(8,128)S(1)}, f32[512,1152]{1,0:T(8,128)}, u32[]{:S(2)}) copy-start(f32[512,1152]{1,0:T(8,128)} %get-tuple-element.87.refs_3_) | copy-start | bytes 7077892
  352.1 1.0 copy-start.9
  382.1 32.4 %copy-start.2 = (f32[6,1152]{1,0:T(8,128)S(1)}, f32[6,1152]{1,0:T(8,128)}, u32[]{:S(2)}) copy-start(f32[6,1152]{1,0:T(8,128)} %get-tuple-element.129.refs_4_) | copy-start | bytes 82948
  382.1 32.4 %copy-start.4 = (bf16[1,1,4,128,1152]{4,3,2,1,0:T(8,128)(2,1)S(1)}, bf16[1,1,4,128,1152]{4,3,2,1,0:T(8,128)(2,1)}, u32[]{:S(2)}) copy-start(bf16[1,1,4,128,1152]{4,3,2,1,0:T(8,128)(2,1)} %param.13) | copy-start | bytes 3538948
  414.6 1.7 copy-start.11
  416.2 14.4 %copy-start.1 = (bf16[512,1152]{1,0:T(8,128)(2,1)S(1)}, bf16[512,1152]{1,0:T(8,128)(2,1)}, u32[]{:S(2)}) copy-start(bf16[512,1152]{1,0:T(8,128)(2,1)} %get-tuple-element.81.refs_0_.refs_5_) | copy-start | bytes 3538948
  416.2 14.4 %copy-start.5 = (bf16[1152,512]{1,0:T(8,128)(2,1)S(1)}, bf16[1152,512]{1,0:T(8,128)(2,1)}, u32[]{:S(2)}) copy-start(bf16[1152,512]{1,0:T(8,128)(2,1)} %get-tuple-element.103) | copy-start | bytes 3538948
  416.2 14.4 %copy-start.6 = (bf16[1152,512]{1,0:T(8,128)(2,1)S(1)}, bf16[1152,512]{1,0:T(8,128)(2,1)}, u32[]{:S(2)}) copy-start(bf16[1152,512]{1,0:T(8,128)(2,1)} %get-tuple-element.104) | copy-start | bytes 3538948
  416.2 14.4 %copy-start.7 = (bf16[1152,512]{1,0:T(8,128)(2,1)S(1)}, bf16[1152,512]{1,0:T(8,128)(2,1)}, u32[]{:S(2)}) copy-start(bf16[1152,512]{1,0:T(8,128)(2,1)} %get-tuple-element.105) | copy-start | bytes 3538948
  741.0 1.6 copy-start.12
  741.1 3.5 copy-start.20
  748.9 2.8 copy-start.19
  751.6 2.7 copy-start.16
  754.3 2.7 copy-start.15
  757.1 2.5 copy-start.18
  759.6 2.7 copy-start.14
  762.3 2.7 copy-start.13

commit v5 on v4

--- a/solution.py
+++ b/solution.py
@@ -501,10 +501,6 @@
     pl.semaphore_wait(barrier, len(seq_masks) + len(rep_masks))
 
 
-def joined_rows(fulls):
-    return [full.reshape(-1, full.shape[2]) for full in fulls]
-
-
 LOW = jnp.bfloat16
 WIDE = jnp.float32
 LANES = 128
@@ -591,161 +587,10 @@
             total[:, lanes] = total[:, lanes] + piece
 
 
-def group_rows(ref, group, column, wide, spatial):
-    lanes = slice(column, column + wide)
-    if spatial:
-        return ref[group, :, lanes]
-    block = ref[:, group, :, lanes]
-    return block.reshape(-1, wide)
-
-
 def same_place():
     row = lax.broadcasted_iota(jnp.int32, (KEYS, KEYS), 0)
     column = lax.broadcasted_iota(jnp.int32, (KEYS, KEYS), 1)
     return (row & 15) == (column & 15)
-
-
-def put_rows(ref, group, block, spatial):
-    if spatial:
-        ref[group] = block
-    else:
-        ref[:, group] = block.reshape(ref.shape[0], ref.shape[2], ref.shape[3])
-
-
-def sibling_barrier(me):
-    barrier = pltpu.get_barrier_semaphore()
-    pl.semaphore_signal(barrier, inc=1, device_id={"seq": me ^ 1})
-    pl.semaphore_wait(barrier, 1)
-
-
-def attend_back_kernel(spatial, *refs):
-    if spatial:
-        (
-            da_ref, qkv_ref, prob_ref, w_ref, other_ref, dqkv_ref,
-            dout, total_q, total_k, total_v, other, give, take, load_sem, send_sem, arrive_sem,
-        ) = refs
-    else:
-        da_ref, qkv_ref, prob_ref, w_ref, dqkv_ref, dout, total_q, total_k, total_v = refs
-    group, groups = pl.program_id(0), pl.num_programs(0)
-    features = da_ref.shape[1]
-    root = HEAD_WIDTH ** (-0.5)
-    if spatial:
-        me = lax.axis_index("seq")
-
-        def exchange(j):
-            return pltpu.make_async_remote_copy(
-                give.at[j], take.at[j], send_sem.at[j], arrive_sem.at[j], device_id={"seq": me ^ 1},
-            )
-
-    @pl.when(group == 0)
-    def _():
-        if spatial:
-            load = pltpu.make_async_copy(other_ref, other, load_sem)
-            load.start()
-            sibling_barrier(me)
-        half = da_ref.shape[0] // 2
-        for j in range(2):
-            got = times_turned(da_ref[j * half : (j + 1) * half], w_ref[...]).astype(LOW)
-            if spatial:
-                dout[2 * j : 2 * j + 2] = got.reshape(2, half // 2, features)
-            else:
-                dout[2 * j : 2 * j + 2] = got.reshape(2, 2, half // 4, features)
-        if spatial:
-            load.wait()
-
-    for head in range(HEADS):
-        start, wide, _ = window(head)
-        mask = head_mask(head)
-        queries = group_rows(qkv_ref, group, start, wide, spatial) * mask
-        keys = group_rows(qkv_ref, group, features + start, wide, spatial)
-        values = group_rows(qkv_ref, group, 2 * features + start, wide, spatial)
-        grads = group_rows(dout, group, start, wide, spatial) * mask
-        if spatial:
-            keys = jnp.concatenate([keys, other[group, :, start : start + wide]], 0)
-            values = jnp.concatenate(
-                [values, other[group, :, features + start : features + start + wide]], 0
-            )
-        prob = prob_ref[0, head]
-        known = prob.astype(WIDE)
-        dprob = times_turned(grads, values)
-        level = jnp.sum(dprob * known, axis=-1, keepdims=True)
-        dscores = (known * (dprob - level)).astype(LOW)
-        add_window(total_q, head, times(dscores, keys * mask))
-        add_window(total_k, head, turned_times(dscores, queries))
-        add_window(total_v, head, turned_times(prob, grads))
-
-    own = total_q.shape[0]
-    pieces = (
-        (total_q[...] * root).astype(LOW),
-        (total_k[:own] * root).astype(LOW),
-        total_v[:own].astype(LOW),
-    )
-    for j, piece in enumerate(pieces):
-        lanes = slice(j * features, (j + 1) * features)
-        if spatial:
-            dqkv_ref[group, :, lanes] = piece
-        else:
-            dqkv_ref[:, group, :, lanes] = piece.reshape(4, -1, features)
-    if spatial:
-        give[group, :, :features] = (total_k[own:] * root).astype(LOW)
-        give[group, :, features:] = total_v[own:].astype(LOW)
-        exchange(group).start()
-
-        @pl.when(group == groups - 1)
-        def _():
-            for j in range(take.shape[0]):
-                exchange(j).wait()
-                lanes = slice(features, 3 * features)
-                dqkv_ref[j, :, lanes] = dqkv_ref[j, :, lanes] + take[j]
-
-
-def attention_backward(da, qkv, prob, weight, other, spatial, cid=None):
-    tokens, features = da.shape
-    groups = prob.shape[0]
-    span = tokens // groups
-    shape = (groups, span, 3 * features) if spatial else (4, groups, span // 4, 3 * features)
-    rest = shape[:-1]
-    in_specs = [
-        whole_block(da.shape),
-        whole_block(shape),
-        pl.BlockSpec((1, HEADS, span, KEYS), lambda g: (g, 0, 0, 0)),
-        whole_block(weight.shape),
-    ]
-    scratch = [
-        pltpu.VMEM(rest + (features,), LOW),
-        pltpu.VMEM((span, features), WIDE),
-        pltpu.VMEM((KEYS, features), WIDE),
-        pltpu.VMEM((KEYS, features), WIDE),
-    ]
-    args = [da, qkv.reshape(shape), prob, weight]
-    if spatial:
-        in_specs.append(pl.BlockSpec(memory_space=pl.ANY))
-        args.append(other)
-        scratch += [pltpu.VMEM(other.shape, LOW)] * 3
-        scratch += [
-            pltpu.SemaphoreType.DMA(()),
-            pltpu.SemaphoreType.DMA((groups,)),
-            pltpu.SemaphoreType.DMA((groups,)),
-        ]
-    got = pl.pallas_call(
-        functools.partial(attend_back_kernel, spatial),
-        grid=(groups,),
-        in_specs=in_specs,
-        out_specs=whole_block(shape),
-        out_shape=jax.ShapeDtypeStruct(shape, LOW),
-        scratch_shapes=scratch,
-        compiler_params=params(56, cid),
-        cost_estimate=cost(2 * tokens * (weight.size + 5 * features * KEYS), 4 * qkv.size),
-        name="attend_spatial_back" if spatial else "attend_temporal_back",
-    )(*args)
-    return got.reshape(tokens, 3 * features)
-
-
-def seq_barrier(me):
-    barrier = pltpu.get_barrier_semaphore()
-    for mask in range(1, 8):
-        pl.semaphore_signal(barrier, inc=1, device_id={"seq": me ^ mask})
-    pl.semaphore_wait(barrier, 7)
 
 
 def moves(source, target, sems, local_sem, me, to_places):
@@ -1203,284 +1048,435 @@
         cost_estimate=cost(flops, 4 * flops // tokens),
         name="forward",
     )(*shards, partial, condition, cotangent, x)
-    weights = joined_rows(got[:count])
+    weights = got[:count]
     named = [dict(zip(OUTS, got[count + 6 + 10 * at : count + 16 + 10 * at])) for at in range(2)]
     return weights, got[count : count + 6], named
 
 
-def mlp_back_kernel(send, *refs):
-    g_ref, x1_ref, branch_ref, mlp_ref, mod_ref, up_ref, down_ref, slope_ref = refs[:8]
-    refs = refs[8:]
-    if send:
-        done_ref, refs = refs[0], refs[1:]
-    du_ref, df_ref, dx1_ref, da_ref, sums_ref = refs[:5]
-    refs = refs[5:]
-    if send:
-        moved_ref, refs = refs[0], refs[1:]
-    df, total = refs[:2]
-    step, steps = pl.program_id(0), pl.num_programs(0)
-    if send:
-        me = lax.axis_index("seq")
-        copies = moves(done_ref, moved_ref, refs[2], refs[3], me, False)
-
-    @pl.when(step == 0)
-    def _():
-        if send:
-            seq_barrier(me)
-            for copy in copies:
-                copy.start()
-        gate = mod_ref[5:6]
-        sums_ref[...] = jnp.zeros_like(sums_ref)
-
-        def begin(at):
-            grad = g_ref[at].astype(WIDE)
-            low = (gate * grad).astype(LOW)
-            df[at] = low
-            df_ref[at] = low
-            sums_ref[3:4] += jnp.sum(grad * mlp_ref[at].astype(WIDE), axis=0, keepdims=True)
-
-        strips(df.shape[0], begin)
-
-    half = df.shape[0] // 2
-    for j in range(2):
-        rows = slice(j * half, (j + 1) * half)
-        du = times_turned(df[rows], down_ref[...]) * slope_ref[rows].astype(WIDE)
-        du = du.astype(LOW)
-        du_ref[rows] = du
-        part = times_turned(du, up_ref[...])
-
-        @pl.when(step == 0)
-        def _():
-            total[rows] = part
-
-        @pl.when(step > 0)
-        def _():
-            total[rows] = total[rows] + part
-
-    @pl.when(step == steps - 1)
-    def _():
-        gate, scaled = mod_ref[2:3], 1.0 + mod_ref[4:5]
-
-        def finish(at):
-            grad = total[at]
-            unit, spread = unit_rows(x1_ref[at])
-            middle = g_ref[at].astype(WIDE) + into_norm(grad, scaled, unit, spread)
-            dx1_ref[at] = middle
-            da_ref[at] = (gate * middle).astype(LOW)
-            sums_ref[0:1] += jnp.sum(
-                middle * branch_ref[at].astype(WIDE), axis=0, keepdims=True
-            )
-            sums_ref[1:2] += jnp.sum(grad, axis=0, keepdims=True)
-            sums_ref[2:3] += jnp.sum(grad * unit, axis=0, keepdims=True)
-
-        strips(df.shape[0], finish)
-        if send:
-            for copy in copies:
-                copy.wait()
-
-
-def mlp_backward(g, x1, branch, mlp, mod, up, down, slope, done=None, cid=None):
-    tokens, features = x1.shape
-    wide = up.shape[1]
-    block = 768
-    send = done is not None
-    in_specs = [
-        whole_block(g.shape), whole_block(x1.shape), whole_block(branch.shape),
-        whole_block(mlp.shape), whole_block(mod.shape),
-        pl.BlockSpec((features, block), lambda j: (0, j)),
-        pl.BlockSpec((block, features), lambda j: (j, 0)),
-        pl.BlockSpec((tokens, block), lambda j: (0, j)),
-    ]
-    args = [g, x1, branch, mlp, mod, up, down, slope]
-    out_shape = [
-        jax.ShapeDtypeStruct((tokens, wide), LOW),
-        jax.ShapeDtypeStruct((tokens, features), LOW),
-        jax.ShapeDtypeStruct((tokens, features), WIDE),
-        jax.ShapeDtypeStruct((tokens, features), LOW),
-        jax.ShapeDtypeStruct((8, features), WIDE),
-    ]
-    out_specs = [pl.BlockSpec((tokens, block), lambda j: (0, j))]
-    out_specs += [whole_block(o.shape) for o in out_shape[1:]]
-    scratch = [pltpu.VMEM((tokens, features), LOW), pltpu.VMEM((tokens, features), WIDE)]
-    if send:
-        in_specs.append(pl.BlockSpec(memory_space=pl.ANY))
-        args.append(done)
-        out_shape.append(
-            jax.ShapeDtypeStruct((done.shape[1], 8 * done.shape[2], features), LOW)
-        )
-        out_specs.append(pl.BlockSpec(memory_space=pl.ANY))
-        scratch += move_scratch()
-    return pl.pallas_call(
-        functools.partial(mlp_back_kernel, send),
-        grid=(wide // block,),
-        in_specs=in_specs,
-        out_specs=out_specs,
-        out_shape=out_shape,
-        scratch_shapes=scratch,
-        compiler_params=params(56, cid),
-        cost_estimate=cost(4 * tokens * up.size, 4 * up.size),
-        name="mlp_backward",
-    )(*args)
-
-
-def qkv_back_kernel(send, *refs):
-    dqkv_ref, w_ref, x_ref, dx1_ref, mod_ref, dx_ref, sums_ref, total = refs[:8]
-    step, steps = pl.program_id(0), pl.num_programs(0)
-    part = times_turned(dqkv_ref[...], w_ref[...])
-
-    @pl.when(step == 0)
-    def _():
-        total[...] = part
-
-    @pl.when(step > 0)
-    def _():
-        total[...] = total[...] + part
-
-    @pl.when(step == steps - 1)
-    def _():
-        scaled = 1.0 + mod_ref[1:2]
-        sums_ref[...] = jnp.zeros_like(sums_ref)
-        if send:
-            ready, sems, local_sem = refs[8:]
-            me = lax.axis_index("seq")
-            seq_barrier(me)
-
-        def finish(at):
-            grad = total[at]
-            unit, spread = unit_rows(x_ref[at].astype(WIDE))
-            sums_ref[0:1] += jnp.sum(grad, axis=0, keepdims=True)
-            sums_ref[1:2] += jnp.sum(grad * unit, axis=0, keepdims=True)
-            got = dx1_ref[at] + into_norm(grad, scaled, unit, spread)
-            if send:
-                total[at] = got
-            else:
-                dx_ref[at] = got
-
-        strips(total.shape[0], finish)
-        if send:
-            ready[...] = total[...].astype(LOW).reshape(ready.shape)
-            copies = moves(ready, dx_ref, sems, local_sem, me, False)
-            for copy in copies:
-                copy.start()
-            for copy in copies:
-                copy.wait()
-
-
-def qkv_backward(dqkv, weight, x, dx1, mod, frames=None, cid=None):
-    tokens, features = x.shape
-    steps = weight.shape[1] // features
-    send = frames is not None
-    out_shape = [
-        jax.ShapeDtypeStruct((tokens, features), WIDE),
-        jax.ShapeDtypeStruct((8, features), WIDE),
-    ]
-    scratch = [pltpu.VMEM((tokens, features), WIDE)]
-    if send:
-        places = tokens // frames
-        out_shape[0] = jax.ShapeDtypeStruct((frames, places, features), LOW)
-        scratch += [pltpu.VMEM((8, frames, places // 8, features), LOW)] + move_scratch()
-    return pl.pallas_call(
-        functools.partial(qkv_back_kernel, send),
-        grid=(steps,),
-        in_specs=[
-            pl.BlockSpec((tokens, features), lambda j: (0, j)),
-            pl.BlockSpec((features, features), lambda j: (0, j)),
-            whole_block(x.shape), whole_block(dx1.shape), whole_block(mod.shape),
-        ],
-        out_specs=[
-            pl.BlockSpec(memory_space=pl.ANY) if send else whole_block((tokens, features)),
-            whole_block((8, features)),
-        ],
-        out_shape=out_shape,
-        scratch_shapes=scratch,
-        compiler_params=params(48, cid),
-        cost_estimate=cost(2 * tokens * weight.size, 2 * weight.size),
-        name="qkv_backward",
-    )(dqkv, weight, x, dx1, mod)
-
-
 SLOTS = 3
 BACK = 4
 
 
-def reduce_kernel(layers, rows, width, edge, *refs):
-    ins, mods = refs[: 8 * layers], refs[8 * layers]
-    outs, every_mod = refs[8 * layers + 1 : 12 * layers + 1], refs[12 * layers + 1]
+KEPT = ("h", "o", "h2", "z", "qkv", "prob", "slope", "x1", "branch", "mlp")
+RIGHTS = ("qkv", "da", "du", "df")
+ORDER = (3, 2, 1, 0)
+
+
+def backward_kernel(dims, *refs):
+    rows, width, edge, tokens, total, spans = dims
+    weights, refs = (refs[:4], refs[4:8]), refs[8:]
+    kept = [dict(zip(KEPT, refs[10 * at : 10 * at + 10])) for at in range(2)]
+    g_in, other_in, y_in, x_ins, mod_ref = refs[20], refs[21], refs[22], refs[23:25], refs[25]
+    refs = refs[26:]
+    grads, refs = (refs[:4], refs[4:8]), refs[8:]
+    rights = [dict(zip(RIGHTS, refs[4 * at : 4 * at + 4])) for at in range(2)]
+    every_mod, moved, input_grad, g_out = refs[8:12]
     (
-        left, right, away, pair_in, part,
-        first_in_a, first_in_b, mid_a, mid_b, second_in_a, second_in_b,
+        left, right, away, pair_in, part, first_in_a, first_in_b, mid_a, mid_b, second_in_a, second_in_b,
         clip, rep_in, joined, inner_in, final, back_in, wide,
-        mod_in, load_sem, pair_sem, link_sem, rep_sem, back_sem, store_sem, mod_sem,
-    ) = refs[12 * layers + 2 :]
+        tall, short, acc, middle, grad_in, low, aux, slope, du, qkv, other, take, prob, dout,
+        total_q, total_k, total_v, ready, sums, mod_low, mod_in,
+        load_sem, pair_sem, link_sem, rep_sem, back_sem, store_sem, mod_sem, tall_sem, short_sem, slope_sem,
+        in_sem, prob_sem, out_sem, swap_sem, move_sem, stay_sem, last_move_sem, last_stay_sem,
+    ) = refs[12:]
     me, z = lax.axis_index("seq"), lax.axis_index("rep")
     core, x, y = me & 1, (me >> 1) & 1, (me >> 2) & 1
     inner = (z == 1) | (z == 2)
     outer = (z == 0) | (z == 3)
-
-    barrier = pltpu.get_barrier_semaphore()
-    for mask in range(1, 8):
-        pl.semaphore_signal(barrier, inc=1, device_id={"seq": me ^ mask})
-    for mask in range(1, 4):
-        pl.semaphore_signal(barrier, inc=1, device_id={"rep": z ^ mask})
-    pl.semaphore_wait(barrier, 10)
-
-    mod_copies = [
-        pltpu.make_async_remote_copy(
-            mods, mod_in.at[me], mod_sem.at[0, mask], mod_sem.at[1, mask],
-            device_id={"seq": me ^ mask},
-        )
-        for mask in range(1, 8)
-    ]
-    clip_copies = [
-        pltpu.make_async_remote_copy(
-            every_mod.at[z], every_mod.at[z], mod_sem.at[0, 7 + mask], mod_sem.at[1, 7 + mask],
-            device_id={"rep": z ^ mask},
-        )
-        for mask in range(1, 4)
-    ]
-    for copy in mod_copies:
+    features = width
+    steps = weights[0][2].shape[2] // CHUNK
+    root = HEAD_WIDTH ** (-0.5)
+
+
+    def wait_out(source, target):
+        copy = pltpu.make_async_copy(source, target, out_sem)
         copy.start()
-    mod_in[me] = mods[...]
-
-    spans, start = [], 0
-    for layer in range(layers):
-        for kind in range(4):
-            shape = outs[4 * layer + kind].shape
-            count = shape[0] // rows * (shape[1] // width)
-            spans.append((layer, kind, start, count))
-            start += count
-    total = start
+        copy.wait()
+
+    def flat_in(ref):
+        return ref if len(ref.shape) == 2 else ref.reshape(tokens, features)
+
+    def load_in(name, at):
+        source, target = {
+            "grad": (flat_in((g_out, g_in)[at]), grad_in),
+            "mlp": (kept[at]["mlp"], aux),
+            "branch": (kept[at]["branch"], aux),
+            "x": (flat_in(x_ins[at]), aux),
+            "x1": (kept[at]["x1"], middle),
+            "qkv": (kept[at]["qkv"], qkv),
+            "other": (other_in, other),
+        }[name]
+        order = ("grad", "mlp", "branch", "x", "x1", "qkv", "other")
+        return pltpu.make_async_copy(source, target, in_sem.at[order.index(name)])
+
+    def chunk_loads(at, step, slot):
+        column = pl.multiple_of(step * CHUNK, CHUNK)
+        down = weights[at][3].reshape(*split_rows(weights[at][3].shape))
+        return (
+            pltpu.make_async_copy(
+                weights[at][2].at[:, :, pl.ds(column, CHUNK)],
+                tall.at[slot, :, :, pl.ds(0, CHUNK)], tall_sem.at[slot],
+            ),
+            pltpu.make_async_copy(
+                down.at[pl.ds(pl.multiple_of(step * 4, 4), 4)], short.at[slot], short_sem.at[slot]
+            ),
+            pltpu.make_async_copy(
+                kept[at]["slope"].at[:, pl.ds(column, CHUNK)], slope.at[slot], slope_sem.at[slot]
+            ),
+        )
+
+    def tall_load(source, slot):
+        return pltpu.make_async_copy(source, tall.at[slot], tall_sem.at[slot])
+
+    def qkv_block(at, j):
+        return weights[at][0].at[:, :, pl.ds(j * features, features)]
+
+    def mlp_begin(at):
+        load_in("grad", at).start()
+        load_in("mlp", at).start()
+        load_in("x1", at).start()
+        for slot in range(2):
+            for copy in chunk_loads(at, slot, slot):
+                copy.start()
+        load_in("grad", at).wait()
+        load_in("mlp", at).wait()
+        gate = mod_ref[at, 5:6]
+        sums[at] = jnp.zeros_like(sums[at])
+
+        def begin(strip):
+            grad = grad_in[strip].astype(WIDE)
+            low[strip] = (gate * grad).astype(LOW)
+            sums[at, 5:6] += jnp.sum(grad * aux[strip].astype(WIDE), axis=0, keepdims=True)
+
+        strips(tokens, begin)
+        load_in("branch", at).start()
+        wait_out(low, rights[at]["df"])
+
+    def mlp_chunk(at, step):
+        slot = lax.rem(step, 2)
+        for copy in chunk_loads(at, step, slot):
+            copy.wait()
+        half = tokens // 2
+        up = tall[slot, :, :, :CHUNK].reshape(features, CHUNK)
+        for j in range(2):
+            strip = slice(j * half, (j + 1) * half)
+            got = times_turned(low[strip], short[slot].reshape(CHUNK, features))
+            got = (got * slope[slot, strip].astype(WIDE)).astype(LOW)
+            du[strip] = got
+            got = times_turned(got, up)
+
+            @pl.when(step == 0)
+            def _():
+                acc[strip] = got
+
+            @pl.when(step > 0)
+            def _():
+                acc[strip] = acc[strip] + got
+
+        @pl.when(step + 2 < steps)
+        def _():
+            for copy in chunk_loads(at, step + 2, slot):
+                copy.start()
+
+        column = pl.multiple_of(step * CHUNK, CHUNK)
+        wait_out(du, rights[at]["du"].at[:, pl.ds(column, CHUNK)])
+
+    def prob_load(at, group):
+        span = tokens // kept[at]["prob"].shape[0]
+        return pltpu.make_async_copy(
+            kept[at]["prob"].at[group], prob.at[:, pl.ds(0, span)], prob_sem
+        )
+
+    def mlp_finish(at):
+        tall_load(weights[at][1], 0).start()
+        tall_load(qkv_block(at, 0), 1).start()
+        load_in("qkv", at).start()
+        prob_load(at, 0).start()
+        if at == 0:
+            load_in("other", at).start()
+        load_in("branch", at).wait()
+        load_in("x1", at).wait()
+        gate, scaled = mod_ref[at, 2:3], 1.0 + mod_ref[at, 4:5]
+
+        def finish(strip):
+            grad = acc[strip]
+            unit, spread = unit_rows(middle[strip])
+            got = grad_in[strip].astype(WIDE) + into_norm(grad, scaled, unit, spread)
+            middle[strip] = got
+            low[strip] = (gate * got).astype(LOW)
+            sums[at, 2:3] += jnp.sum(got * aux[strip].astype(WIDE), axis=0, keepdims=True)
+            sums[at, 3:4] += jnp.sum(grad, axis=0, keepdims=True)
+            sums[at, 4:5] += jnp.sum(grad * unit, axis=0, keepdims=True)
+
+        strips(tokens, finish)
+        load_in("x", at).start()
+        wait_out(low, rights[at]["da"])
+
+    def project(at):
+        tall_load(weights[at][1], 0).wait()
+        half = tokens // 2
+        for j in range(2):
+            got = times_turned(
+                low[j * half : (j + 1) * half], tall[0].reshape(features, features)
+            ).astype(LOW)
+            dout[4 * j : 4 * j + 4] = got.reshape(4, -1, features)
+        tall_load(qkv_block(at, 1), 0).start()
+        load_in("qkv", at).wait()
+        if at == 0:
+            load_in("other", at).wait()
+
+    def rows_of(ref, group, column, lanes, spatial):
+        lanes = slice(column, column + lanes)
+        if spatial:
+            block = ref[pl.ds(2 * group, 2), :, lanes]
+            return block.reshape(-1, block.shape[2])
+        return jnp.concatenate([ref[2 * block + group, :, lanes] for block in range(4)], 0)
+
+    def swap_copy(j):
+        return pltpu.make_async_remote_copy(
+            other.at[pl.ds(2 * j, 2)], take.at[pl.ds(2 * j, 2)],
+            swap_sem.at[0, j], swap_sem.at[1, j], device_id={"seq": me ^ 1},
+        )
+
+    def attend_group(at, group):
+        spatial = at == 0
+        groups = kept[at]["prob"].shape[0]
+        span = tokens // groups
+        prob_load(at, group).wait()
+        for head in range(HEADS):
+            start, lanes, _ = window(head)
+            mask = head_mask(head)
+            queries = rows_of(qkv, group, start, lanes, spatial) * mask
+            keys = rows_of(qkv, group, features + start, lanes, spatial)
+            values = rows_of(qkv, group, 2 * features + start, lanes, spatial)
+            coming = rows_of(dout, group, start, lanes, spatial) * mask
+            if spatial:
+                keys = jnp.concatenate([keys, rows_of(other, group, start, lanes, True)], 0)
+                values = jnp.concatenate(
+                    [values, rows_of(other, group, features + start, lanes, True)], 0
+                )
+            chance = prob[head, :span]
+            known = chance.astype(WIDE)
+            dprob = times_turned(coming, values)
+            level = jnp.sum(dprob * known, axis=-1, keepdims=True)
+            dscores = (known * (dprob - level)).astype(LOW)
+            add_window(total_q.at[pl.ds(0, span)], head, times(dscores, keys * mask))
+            add_window(total_k, head, turned_times(dscores, queries))
+            add_window(total_v, head, turned_times(chance, coming))
+
+        @pl.when(group + 1 < groups)
+        def _():
+            prob_load(at, group + 1).start()
+
+        pieces = (
+            (total_q[:span] * root).astype(LOW),
+            (total_k[:span] * root).astype(LOW),
+            total_v[:span].astype(LOW),
+        )
+        for j, piece in enumerate(pieces):
+            lanes = slice(j * features, (j + 1) * features)
+            if spatial:
+                qkv[pl.ds(2 * group, 2), :, lanes] = piece.reshape(2, -1, features)
+            else:
+                for block in range(4):
+                    qkv[2 * block + group, :, lanes] = piece[block * 64 : (block + 1) * 64]
+        if spatial:
+            other[pl.ds(2 * group, 2), :, :features] = (
+                (total_k[span:] * root).astype(LOW).reshape(2, -1, features)
+            )
+            other[pl.ds(2 * group, 2), :, features:] = (
+                total_v[span:].astype(LOW).reshape(2, -1, features)
+            )
+            swap_copy(group).start()
+
+    def attend_finish(at):
+        if at == 0:
+            for j in range(4):
+                swap_copy(j).wait()
+                pair = slice(2 * j, 2 * j + 2)
+                lanes = slice(features, 3 * features)
+                qkv[pair, :, lanes] = qkv[pair, :, lanes] + take[pair]
+        wait_out(qkv, rights[at]["qkv"].reshape(*qkv.shape))
+
+    def qkv_chunks(at):
+        for j in range(3):
+            slot = 1 - j % 2
+            tall_load(qkv_block(at, j), slot).wait()
+            got = times_turned(
+                qkv[:, :, j * features : (j + 1) * features].reshape(tokens, features),
+                tall[slot].reshape(features, features),
+            )
+            if j == 0:
+                acc[...] = got
+                tall_load(qkv_block(at, 2), slot).start()
+            else:
+                acc[...] = acc[...] + got
+
+    def last_moves():
+        return moves(y_in, moved, last_move_sem, last_stay_sem, me, False)
+
+    def grad_moves():
+        return moves(ready, g_out, move_sem, stay_sem, me, False)
+
+    def qkv_finish(at):
+        load_in("x", at).wait()
+        scaled = 1.0 + mod_ref[at, 1:2]
+
+        def finish(strip):
+            grad = acc[strip]
+            unit, spread = unit_rows(aux[strip].astype(WIDE))
+            sums[at, 0:1] += jnp.sum(grad, axis=0, keepdims=True)
+            sums[at, 1:2] += jnp.sum(grad * unit, axis=0, keepdims=True)
+            acc[strip] = middle[strip] + into_norm(grad, scaled, unit, spread)
+
+        strips(tokens, finish)
+        if at == 0:
+            wait_out(acc, input_grad)
+        else:
+            ready[...] = acc[...].astype(LOW).reshape(ready.shape)
+            for copy in grad_moves():
+                copy.start()
+
+    def backward_step(t):
+        def at_turn(turn):
+            return pl.when(t == turn)
+
+        @pl.when(t < steps - 1)
+        def _():
+            mlp_chunk(1, t + 1)
+
+        @at_turn(4)
+        def _():
+            mlp_finish(1)
+            project(1)
+
+        @pl.when((t >= 5) & (t < 7))
+        def _():
+            attend_group(1, t - 5)
+
+        @at_turn(6)
+        def _():
+            attend_finish(1)
+
+        @at_turn(7)
+        def _():
+            qkv_chunks(1)
+
+        @at_turn(8)
+        def _():
+            qkv_finish(1)
+
+        @at_turn(10)
+        def _():
+            for copy in grad_moves():
+                copy.wait()
+            mlp_begin(0)
+
+        @pl.when((t >= 10) & (t < 10 + steps))
+        def _():
+            mlp_chunk(0, t - 10)
+
+        @at_turn(15)
+        def _():
+            mlp_finish(0)
+            project(0)
+
+        @pl.when((t >= 16) & (t < 20))
+        def _():
+            attend_group(0, t - 16)
+
+        @at_turn(19)
+        def _():
+            attend_finish(0)
+
+        @at_turn(20)
+        def _():
+            qkv_chunks(0)
+
+        @at_turn(21)
+        def _():
+            qkv_finish(0)
+            mod_low[...] = jnp.zeros_like(mod_low)
+            for at in range(2):
+                mod_low[8 * at : 8 * at + 8] = sums[at].astype(LOW)
+            mod_in[me] = mod_low[...]
+            for copy in mod_copies():
+                copy.start()
+
+        @at_turn(23)
+        def _():
+            for copy in mod_copies():
+                copy.wait()
+            summed = mod_in[0].astype(WIDE)
+            for device in range(1, 8):
+                summed += mod_in[device].astype(WIDE)
+            every_mod[z] = summed.astype(LOW)
+            for copy in clip_copies():
+                copy.start()
+
+        @at_turn(25)
+        def _():
+            for copy in last_moves():
+                copy.start()
+
+        @at_turn(total + 5)
+        def _():
+            for copy in clip_copies():
+                copy.wait()
+            for copy in last_moves():
+                copy.wait()
+
+    def mod_copies():
+        return [
+            pltpu.make_async_remote_copy(
+                mod_low, mod_in.at[me], mod_sem.at[0, mask], mod_sem.at[1, mask],
+                device_id={"seq": me ^ mask},
+            )
+            for mask in range(1, 8)
+        ]
+
+    def clip_copies():
+        return [
+            pltpu.make_async_remote_copy(
+                every_mod.at[z], every_mod.at[z], mod_sem.at[0, 7 + mask], mod_sem.at[1, 7 + mask],
+                device_id={"rep": z ^ mask},
+            )
+            for mask in range(1, 4)
+        ]
+
+
+    names = ("h", "o", "h2", "z")
 
     def loads(block, slot):
         for layer, kind, first, count in spans:
             @pl.when((block >= first) & (block < first + count))
             def _():
-                source = ins[8 * layer + kind]
+                source = kept[layer][names[kind]]
                 if kind == 3:
                     source = source.at[:, :, block - first]
                 pltpu.make_async_copy(source, left.at[slot], load_sem.at[0, slot]).start()
-                source = ins[8 * layer + 4 + kind]
+                source = rights[layer][RIGHTS[kind]]
                 if kind in (0, 2):
                     column = pl.multiple_of((block - first) * width, width)
                     source = source.at[:, pl.ds(column, width)]
                 pltpu.make_async_copy(source, right.at[slot], load_sem.at[1, slot]).start()
 
     def wait_loads(slot):
-        pltpu.make_async_copy(ins[0], left.at[slot], load_sem.at[0, slot]).wait()
-        pltpu.make_async_copy(ins[5], right.at[slot], load_sem.at[1, slot]).wait()
-
-    def store(block, slot):
+        pltpu.make_async_copy(kept[0]["h"], left.at[slot], load_sem.at[0, slot]).wait()
+        pltpu.make_async_copy(rights[0]["da"], right.at[slot], load_sem.at[1, slot]).wait()
+
+    def store(block):
         for layer, kind, first, count in spans:
             @pl.when((block >= first) & (block < first + count))
             def _():
-                target = outs[4 * layer + kind]
+                target = grads[layer][kind]
                 if kind == 3:
                     row = pl.multiple_of((block - first) * rows, rows)
                     target = target.at[pl.ds(row, rows)]
                 elif kind in (0, 2):
                     column = pl.multiple_of((block - first) * width, width)
                     target = target.at[:, pl.ds(column, width)]
-                pltpu.make_async_copy(wide.at[slot], target, store_sem.at[slot]).start()
+                pltpu.make_async_copy(wide, target, store_sem).start()
 
     def to_seq(source, target, which, slot, mask):
         return pltpu.make_async_remote_copy(
@@ -1534,8 +1530,6 @@
             device_id={"rep": z ^ 1},
         )
 
-    loads(0, 0)
-
     def turn(t, carry):
         def stage(back):
             return (t >= back) & (t < total + back)
@@ -1584,33 +1578,29 @@
         def _():
             @pl.when(inner)
             def _():
-                wide[now2] = final[was2].astype(jnp.float32)
+                wide[...] = final[was2].astype(WIDE)
 
             @pl.when(outer)
             def _():
-                wide[now2] = back_in[lax.rem(t + 3, BACK)].astype(jnp.float32)
-
-            store(t - 6, now2)
+                wide[...] = back_in[lax.rem(t + 3, BACK)].astype(WIDE)
+
+            store(t - 6)
 
         @pl.when(t < total)
         def _():
             wait_loads(now2)
             slot3 = lax.rem(t, SLOTS)
-
-            def product(which):
-                def columns(j, carry):
-                    at = pl.ds(pl.multiple_of(j * (width // 3), width // 3), width // 3)
-                    block = left[now2, :, which]
-                    four, _, depth = block.shape
-                    got = jnp.dot(
-                        block.reshape(four * rows, depth), right[now2, :, at],
-                        preferred_element_type=jnp.float32,
-                    ).astype(jnp.bfloat16)
-                    return at, got.reshape(four, rows, width // 3)
-                return columns
+            third = width // 3
+
+            def product(which, j):
+                at = pl.ds(pl.multiple_of(j * third, third), third)
+                block = left[now2, :, which]
+                four, _, depth = block.shape
+                got = times(block.reshape(four * rows, depth), right[now2, :, at]).astype(LOW)
+                return at, got.reshape(four, rows, third)
 
             def away_columns(j, carry):
-                at, got = product(1 - core)(j, carry)
+                at, got = product(1 - core, j)
                 away[:, :, at] = got
                 return carry
 
@@ -1618,7 +1608,7 @@
             pair_copy(t).start()
 
             def kept_columns(j, carry):
-                at, got = product(core)(j, carry)
+                at, got = product(core, j)
                 part[slot3, 0, :, :, at] = got[:2]
                 part[slot3, 1, :, :, at] = got[2:]
                 return carry
@@ -1632,6 +1622,8 @@
 
             lax.fori_loop(0, 4, add, 0)
 
+        backward_step(t)
+
         @pl.when(stage(1))
         def _():
             for copy in first_copies(t):
@@ -1668,102 +1660,124 @@
 
         @pl.when(stage(6))
         def _():
-            pltpu.make_async_copy(wide.at[now2], outs[1], store_sem.at[now2]).wait()
+            pltpu.make_async_copy(wide, grads[0][1], store_sem).wait()
 
         return carry
 
-    lax.fori_loop(0, 2, turn, 0)
-    for copy in mod_copies:
-        copy.wait()
-    mod_total = mod_in[0].astype(jnp.float32)
-    for device in range(1, 8):
-        mod_total += mod_in[device].astype(jnp.float32)
-    every_mod[z] = mod_total.astype(every_mod.dtype)
-    for copy in clip_copies:
-        copy.start()
-    lax.fori_loop(2, total + 6, turn, 0)
-    for copy in clip_copies:
-        copy.wait()
-
-
-def reduce_grads(layers, mods, cid):
-    tokens = layers[0][4].shape[0]
-    rows, width = layers[0][0].shape[2], layers[0][5].shape[1]
-    edge = width * 5 // 9 // 128 * 128
-    low = jnp.bfloat16
-    outs = []
-    for ops in layers:
-        for kind in range(4):
-            tall = ops[kind].shape[2] if kind == 3 else 1
-            outs.append(jax.ShapeDtypeStruct((tall * rows, ops[4 + kind].shape[1]), jnp.float32))
-    outs.append(jax.ShapeDtypeStruct((4,) + mods.shape, mods.dtype))
-    vm = pltpu.VMEM
-    dma = pltpu.SemaphoreType.DMA
-    flops = sum(2 * tokens * 8 * o.size for o in outs[:-1])
+    enter(range(1, 8), range(1, 4))
+    mlp_begin(1)
+    mlp_chunk(1, jnp.int32(0))
+    loads(0, 0)
+    lax.fori_loop(0, total + 6, turn, 0)
+
+
+def backward(weights, kept, g, other, y, xs, mods, cid):
+    struct = jax.ShapeDtypeStruct
+    tokens, features = xs[0].shape
+    rows = features // 8
+    wide = weights[0][2].shape[2]
+    edge = features * 5 // 9 // 128 * 128
+    frames, places = g.shape[1], 8 * g.shape[2]
+    out_shapes = [(rows, 3 * features), (rows, features), (rows, wide), (wide // 8, features)]
+    spans, total = [], 0
+    for layer in (1, 0):
+        for kind in ORDER:
+            count = out_shapes[kind][0] * out_shapes[kind][1] // (rows * features)
+            spans.append((layer, kind, total, count))
+            total += count
+    dims = (rows, features, edge, tokens, total, spans)
+    any_ = pl.BlockSpec(memory_space=pl.ANY)
+    outs = [struct(shape, WIDE) for shape in out_shapes] * 2
+    outs += [
+        struct((tokens, 3 * features), LOW), struct((tokens, features), LOW),
+        struct((tokens, wide), LOW), struct((tokens, features), LOW),
+    ] * 2
+    outs += [
+        struct((4, 16, features), LOW),
+        struct((frames, places, features), LOW),
+        struct((tokens, features), WIDE),
+        struct((frames, places, features), LOW),
+    ]
+    vm, dma = pltpu.VMEM, pltpu.SemaphoreType.DMA
+    rest = features - edge
+    scratch = [
+        vm((2, 4, 2, rows, tokens), LOW),
+        vm((2, tokens, features), LOW),
+        vm((4, rows, features), LOW),
+        vm((2, 4, rows, features), LOW),
+        vm((SLOTS, 2, 2, rows, features), LOW),
+        vm((SLOTS, 2, rows, edge), LOW),
+        vm((SLOTS, 2, rows, rest), LOW),
+        vm((2, 2, rows, edge), LOW),
+        vm((2, 2, rows, rest), LOW),
+        vm((SLOTS, rows, edge), LOW),
+        vm((SLOTS, rows, rest), LOW),
+        vm((2, rows, features), LOW),
+        vm((SLOTS, rows, features), LOW),
+        vm((2, rows, features), LOW),
+        vm((SLOTS, rows, features), LOW),
+        vm((2, rows, features), LOW),
+        vm((BACK, rows, features), LOW),
+        vm((rows, features), WIDE),
+        vm((2, 8, rows, features), LOW),
+        vm((2, 4, CHUNK // 4, features), LOW),
+        vm((tokens, features), WIDE),
+        vm((tokens, features), WIDE),
+        vm((tokens, features), LOW),
+        vm((tokens, features), LOW),
+        vm((tokens, features), LOW),
+        vm((2, tokens, CHUNK), LOW),
+        vm((tokens, CHUNK), LOW),
+        vm((8, tokens // 8, 3 * features), LOW),
+        vm((8, tokens // 8, 2 * features), LOW),
+        vm((8, tokens // 8, 2 * features), LOW),
+        vm((HEADS, KEYS, KEYS), LOW),
+        vm((8, tokens // 8, features), LOW),
+        vm((KEYS, features), WIDE),
+        vm((KEYS, features), WIDE),
+        vm((KEYS, features), WIDE),
+        vm((8, frames, places // 8, features), LOW),
+        vm((2, 8, features), WIDE),
+        vm((16, features), LOW),
+        vm((8, 16, features), LOW),
+        dma((2, 2)),
+        dma((2, 2)),
+        dma((2, 4, SLOTS)),
+        dma((2, 2, SLOTS)),
+        dma((2, BACK)),
+        dma(()),
+        dma((2, 11)),
+        dma((2,)),
+        dma((2,)),
+        dma((2,)),
+        dma((7,)),
+        dma(()),
+        dma(()),
+        dma((2, 4)),
+        *move_scratch(),
+        *move_scratch(),
+    ]
+    flops = 4 * tokens * 8 * sum(a * b for a, b in out_shapes) * 2
     got = pl.pallas_call(
-        functools.partial(reduce_kernel, len(layers), rows, width, edge),
+        functools.partial(backward_kernel, dims),
         out_shape=outs,
-        in_specs=[pl.BlockSpec(memory_space=pl.ANY)] * (8 * len(layers))
-        + [pl.BlockSpec(memory_space=vm)],
-        out_specs=[pl.BlockSpec(memory_space=pl.ANY)] * (4 * len(layers))
-        + [pl.BlockSpec(memory_space=vm)],
-        scratch_shapes=[
-            vm((2, 4, 2, rows, tokens), low),
-            vm((2, tokens, width), low),
-            vm((4, rows, width), low),
-            vm((2, 4, rows, width), low),
-            vm((SLOTS, 2, 2, rows, width), low),
-            vm((SLOTS, 2, rows, edge), low),
-            vm((SLOTS, 2, rows, width - edge), low),
-            vm((2, 2, rows, edge), low),
-            vm((2, 2, rows, width - edge), low),
-            vm((SLOTS, rows, edge), low),
-            vm((SLOTS, rows, width - edge), low),
-            vm((2, rows, width), low),
-            vm((SLOTS, rows, width), low),
-            vm((2, rows, width), low),
-            vm((SLOTS, rows, width), low),
-            vm((2, rows, width), low),
-            vm((BACK, rows, width), low),
-            vm((2, rows, width), jnp.float32),
-            vm((8,) + mods.shape, mods.dtype),
-            dma((2, 2)),
-            dma((2, 2)),
-            dma((2, 4, SLOTS)),
-            dma((2, 2, SLOTS)),
-            dma((2, BACK)),
-            dma((2,)),
-            dma((2, 11)),
-        ],
-        compiler_params=pltpu.CompilerParams(
-            collective_id=cid, has_side_effects=True, vmem_limit_bytes=48 << 20
-        ),
-        cost_estimate=pl.CostEstimate(flops=flops, bytes_accessed=4 * sum(o.size for o in outs), transcendentals=0),
-        name="reduce_grads",
-    )(*[op for ops in layers for op in ops], mods)
-    return [tuple(got[4 * at : 4 * at + 4]) for at in range(len(layers))], got[-1]
-
-
-def reduce_operands(lefts, rights):
-    features = rights[1].shape[1]
-    shaped = []
-    for left in lefts:
-        tall, tokens = left.shape[0] // features, left.shape[1]
-        shape = (4, 2, features // 8, tokens) if tall == 1 else (4, 2, tall, features // 8, tokens)
-        shaped.append(left.reshape(shape))
-    return (*shaped, *rights)
-
-
-def layer_backward(g, x, mod, weights, kept, other, spatial, done=None, frames=None, cids=(None,) * 3):
-    qkv_w, out_w, up_w, down_w = weights
-    du, df, dx1, da, sums, *moved = mlp_backward(
-        g, kept["x1"], kept["branch"], kept["mlp"], mod, up_w, down_w, kept["slope"], done, cids[0]
-    )
-    dqkv = attention_backward(da, kept["qkv"], kept["prob"], out_w, other, spatial, cids[1])
-    dx, last_sums = qkv_backward(dqkv, qkv_w, x, dx1, mod, frames, cids[2])
-    mod_grad = jnp.concatenate([last_sums[:2], sums[:4]], 0).reshape(1, -1)
-    lefts = [kept[name] for name in ("h", "o", "h2", "z")]
-    return dx, moved, mod_grad, reduce_operands(lefts, (dqkv, da, du, df))
+        in_specs=[any_] * (8 + 20 + 5) + [pl.BlockSpec(memory_space=vm)],
+        out_specs=[any_] * 16 + [pl.BlockSpec(memory_space=vm)] + [any_] * 3,
+        scratch_shapes=scratch,
+        compiler_params=params(63, cid),
+        cost_estimate=cost(flops, flops // tokens),
+        name="backward",
+    )(
+        *weights[0], *weights[1], *[each[name] for each in kept for name in KEPT],
+        g, other, y, *xs, mods,
+    )
+    return got[:4], got[4:8], got[16], got[17], got[18]
+
+
+def by_device(left, features):
+    tall, tokens = left.shape[0] // features, left.shape[1]
+    rows = features // 8
+    return left.reshape((4, 2, rows, tokens) if tall == 1 else (4, 2, tall, rows, tokens))
 
 
 def fused_device(frames_in, conditioning, shards, partial_mod, cotangent):
@@ -1771,23 +1785,18 @@
     tokens = frames * places
     low_cotangent = cotangent.reshape(frames, places, features).astype(LOW)
     x_one = frames_in.reshape(tokens, features)
-    weights, (mods, conditions, g_two, other, x_two, y_two), (kept_one, kept_two) = forward(
+    weights, (mods, conditions, g_two, other, x_two, y_two), kept = forward(
         shards, partial_mod.reshape(-1, LANES), conditioning.reshape(-1, LANES), low_cotangent,
         x_one, 0,
     )
-    g_one, (block_out,), mod_grad_two, operands_two = layer_backward(
-        g_two.reshape(tokens, features), x_two.reshape(tokens, features), mods[1], weights[4:],
-        kept_two, None, False, y_two.reshape(g_two.shape), frames, (5, None, 6),
-    )
-    input_grad, _, mod_grad_one, operands_one = layer_backward(
-        g_one.reshape(tokens, features), x_one, mods[0], weights[:4], kept_one,
-        other.reshape(frames, places, 2 * features), True, cids=(None, 3, None),
-    )
-    mod_grads = jnp.concatenate([mod_grad_one, mod_grad_two], 1).astype(LOW)
-    (grads_two, grads_one), every_mod = reduce_grads(
-        [operands_two, operands_one], mod_grads.reshape(-1, LANES), 1
-    )
-    every_mod = every_mod.reshape(-1, mod_grads.shape[1])
+    for each in kept:
+        for name in ("h", "o", "h2", "z"):
+            each[name] = by_device(each[name], features)
+    grads_one, grads_two, every_mod, block_out, input_grad = backward(
+        (weights[:4], weights[4:]), kept, g_two, other, y_two.reshape(g_two.shape),
+        (x_one, x_two.reshape(tokens, features)), mods, 1,
+    )
+    every_mod = every_mod.reshape(-1, 2, 8, features)[:, :, :6].reshape(-1, 12 * features)
     return (
         block_out.astype(WIDE), input_grad, grads_one, grads_two, every_mod,
         conditions.reshape(-1, features),

time: 777 us -> 683 us (0.88)
  Pallas kernels: 727 us -> 636 us
    pallas_call x7 -> x1, Pallas kernels: 463 us -> 373 us  [backward(): pl.pallas_call(functools.partial(backward_kernel, dims), out_shape=outs,...]
    unnamed x54 -> x40, local copies, waits for them, and re-layouts: 19.3 us -> 18.6 us
where the time goes in v5:
time: 683 us; the launch traced here: 673 us
  Pallas kernels  636 us (93%)
  local copies, waits for them, and re-layouts  19.6 us (3%)
  matrix products  9.31 us (1%)
    pallas_call x1, Pallas kernels, backward(): pl.pallas_call(functools.partial(backward_kernel, dims), out_shape=outs,...  373 us
    pallas_call x1, Pallas kernels, forward(): pl.pallas_call(functools.partial(forward_kernel, shapes), out_shape=outs,...  263 us
    unnamed x40, local copies, waits for them, and re-layouts  18.6 us

profile of v5, /device:TPU:0, one launch (start us, length us, event | category | flops | bytes accessed | tf_op | source)
XLA Modules:
  0.0 672.9 jit_solution(5032793953565989507)
XLA Ops:
  0.6 0.0 copy-start.14
  0.7 0.0 copy-start
  0.7 2.2 fusion.11
  2.8 0.0 copy-done.14
  2.8 0.0 copy-done
  2.8 0.5 fusion.9
  3.3 0.8 maximum_reduce_fusion
  4.1 2.8 convert_bitcast_fusion.refs_10_
  6.9 0.6 reduce.1
  7.5 263.1 %forward.1 = (bf16[8,144,3456]{2,1,0:T(8,128)(2,1)}, bf16[8,144,1152]{2,1,0:T(8,128)(2,1)}, bf16[8,144,4608]{2,1,0:T(8,128)(2,1)}, bf16[8,576,1152]{2,1,0:T(8,12...) custom-call(bf16[144,3456]{1,0:T(8,128)(2,1)} %refs_0_.1, ...), custom_call_target="tpu_custom_call" | custom-call | flops 32614907904 | bytes 254803968 | tf_op jit(solution)/shard_map/forward/pallas_call | solution.py:1013
  270.6 0.0 copy-start.13
  270.6 373.2 %backward.1 = (f32[144,3456]{1,0:T(8,128)}, f32[144,1152]{1,0:T(8,128)}, f32[144,4608]{1,0:T(8,128)}, f32[576,1152]{1,0:T(8,128)}, f32[144,3456]{1,0:T(8,128)}, ...) custom-call(bf16[8,144,3456]{2,1,0:T(8,128)(2,1)} %get-tuple-element, ...), custom_call_target="tpu_custom_call" | custom-call | flops 65229815808 | bytes 127401984 | tf_op jit(solution)/shard_map/backward/pallas_call | solution.py:1761
  643.9 1.0 reshape.118
  644.8 0.0 copy-done.13
  644.9 2.8 fusion
  647.6 0.0 copy-start.1
  647.6 2.7 fusion.2
  650.4 0.0 copy-done.1
  650.4 0.0 copy-start.2
  650.4 0.0 copy-start.10
  650.4 0.6 fusion.4
  651.0 0.9 copy-done.2
  651.9 0.6 fusion.5
  652.5 0.0 copy-start.7
  652.5 0.7 fusion.8
  653.2 0.0 copy-done.10
  653.2 1.6 bitcast_convert_fusion
  654.8 0.0 copy-done.7
  654.8 1.4 copy.38
  656.2 1.0 copy-done.9
  657.2 0.0 copy-start.12
  657.2 0.0 copy-start.6
  657.2 1.3 copy.39
  658.5 0.3 copy-done.12
  658.8 0.8 copy.40
  659.6 0.5 copy-done.6
  660.2 0.0 copy-start.5
  660.2 1.5 copy.41
  661.7 1.2 copy-done.5
  662.9 1.5 copy.42
  664.4 1.0 copy-done.8
  665.4 1.3 copy.43
  666.7 0.3 copy-done.11
  666.9 0.8 copy.44
  667.8 0.5 copy-done.4
  668.3 1.5 copy.45
  669.8 1.2 copy-done.3
  671.0 1.5 copy.46
  (7 shorter events, 0.0 us)
Async XLA Ops:
  0.6 2.2 copy-start.14
  0.7 2.2 copy-start
  270.6 374.2 %copy-start.13 = (f32[4,9,128]{2,1,0:T(8,128)S(1)}, f32[4,9,128]{2,1,0:T(8,128)}, u32[]{:S(2)}) copy-start(f32[4,9,128]{2,1,0:T(8,128)} %get-tuple-element.94) | copy-start | bytes 55300
  647.6 2.8 copy-start.1
  650.4 1.6 copy-start.2
  650.4 2.9 copy-start.10
  652.5 2.3 copy-start.7
  654.8 2.4 copy-start.9
  657.2 1.5 copy-start.12
  657.2 2.9 copy-start.6
  660.2 2.7 copy-start.5
  662.9 2.5 copy-start.8
  665.4 1.5 copy-start.11
  665.4 2.9 copy-start.4
  668.3 2.7 copy-start.3

commit v6 on v5

--- a/solution.py
+++ b/solution.py
@@ -520,6 +520,10 @@
     lax.fori_loop(0, total // STRIP, step, 0)
 
 
+def clear(ref, at):
+    ref[at] = jnp.zeros_like(ref[at])
+
+
 def turn_into(target, source):
     for j in range(source.shape[1] // LANES):
         target[j * LANES : (j + 1) * LANES, :] = source[:, j * LANES : (j + 1) * LANES].T
@@ -662,10 +666,6 @@
     for copy in small:
         copy.start()
     gather.start()
-    gather.advance(0)
-    later = moves(tokens, moved, move_sem, stay_sem, me, True)
-    for copy in later:
-        copy.start()
     for copy in small:
         copy.wait()
     modulation = partials[0]
@@ -725,11 +725,13 @@
                 values = jnp.concatenate(
                     [values, rows_of(other, group, features + start, wide, True)], 0
                 )
-            scores = times_turned(queries, keys) * HEAD_WIDTH ** (-0.5)
+            scores = times_turned(queries, keys)
             if not spatial:
                 scores = jnp.where(allowed, scores, -3e38)
-            grown = jnp.exp(scores - jnp.max(scores, axis=-1, keepdims=True))
-            chance = (grown / jnp.sum(grown, axis=-1, keepdims=True)).astype(LOW)
+            grown = jnp.exp2(
+                (scores - jnp.max(scores, axis=-1, keepdims=True)) * (HEAD_WIDTH ** (-0.5) * 1.4426950408889634)
+            )
+            chance = (grown * (1.0 / jnp.sum(grown, axis=-1, keepdims=True))).astype(LOW)
             prob[head, :span] = chance
             add_window(part.at[pl.ds(0, span)], head, times(chance, values * mask))
         got = part[:span].astype(LOW)
@@ -760,6 +762,9 @@
             for at in plan.get(place, ()):
                 if at is None:
                     gather.share(len(gather.pieces) - 1)
+                elif isinstance(at, list):
+                    for copy in at:
+                        copy.start()
                 else:
                     gather.advance(at)
 
@@ -892,6 +897,7 @@
 
         start_loads(0, 0)
         half = x.shape[0] // 2
+        strips(x.shape[0], lambda at: clear(total, at))
 
         def chunk(step, carry):
             slot = lax.rem(step, 2)
@@ -914,15 +920,7 @@
                 slope[slot, rows] = bend.astype(LOW)
                 value = value.astype(LOW)
                 hidden[slot, :, rows] = value.T
-                got = times(value, short[slot].reshape(CHUNK, features))
-
-                @pl.when(step == 0)
-                def _():
-                    total[rows] = got
-
-                @pl.when(step > 0)
-                def _():
-                    total[rows] = total[rows] + got
+                total[rows] += times(value, short[slot].reshape(CHUNK, features))
 
             for copy in chunk_outs(step, slot):
                 copy.start()
@@ -945,13 +943,11 @@
         ready[...] = total[...].astype(LOW).reshape(ready.shape)
 
     layer(0, True, x_ref, {
-        "norm": (1, 2, 3), "qkv1": (4,), ("group", 0): (5,), ("group", 1): (6,), ("group", 2): (7,),
+        "norm": (0, 1, 2, 3), "qkv1": (4,), ("group", 0): (5,), ("group", 1): (6,), ("group", 2): (7,),
         ("group", 3): (8,), "attended": (9,), "middle": (10, 11, 12), ("chunk", 1): (13,),
         ("chunk", 3): (14,), ("chunk", 4): (15,),
     })
     copies = moves(ready, x2_ref, next_move_sem, next_stay_sem, me, True)
-    for copy in later:
-        copy.wait()
     for copy in copies:
         copy.start()
     gather.local(4)
@@ -963,13 +959,16 @@
     fetch.start()
     fetch.wait()
     x2_rows = x2.reshape(x_ref.shape)
+    later = moves(tokens, moved, move_sem, stay_sem, me, True)
     layer(1, False, x2_rows, {
         "norm": (18,), "qkv0": (19,), "qkv2": (20,), ("group", 1): (21,), "attended": (22,),
-        "middle": (23, None),
+        "middle": (23, None, later),
     })
     begin("ready", ready, y_ref)
     for name in names:
         settle(name)
+    for copy in later:
+        copy.wait()
     gather.finish()
 
 
@@ -1077,7 +1076,7 @@
         tall, short, acc, middle, grad_in, low, aux, slope, du, qkv, other, take, prob, dout,
         total_q, total_k, total_v, ready, sums, mod_low, mod_in,
         load_sem, pair_sem, link_sem, rep_sem, back_sem, store_sem, mod_sem, tall_sem, short_sem, slope_sem,
-        in_sem, prob_sem, out_sem, swap_sem, move_sem, stay_sem, last_move_sem, last_stay_sem,
+        in_sem, prob_sem, out_sem, du_sem, swap_sem, move_sem, stay_sem, last_move_sem, last_stay_sem,
     ) = refs[12:]
     me, z = lax.axis_index("seq"), lax.axis_index("rep")
     core, x, y = me & 1, (me >> 1) & 1, (me >> 2) & 1
@@ -1146,14 +1145,24 @@
         def begin(strip):
             grad = grad_in[strip].astype(WIDE)
             low[strip] = (gate * grad).astype(LOW)
+            clear(acc, strip)
             sums[at, 5:6] += jnp.sum(grad * aux[strip].astype(WIDE), axis=0, keepdims=True)
 
         strips(tokens, begin)
         load_in("branch", at).start()
         wait_out(low, rights[at]["df"])
 
+    def du_copy(at, step):
+        column = pl.multiple_of(step * CHUNK, CHUNK)
+        return pltpu.make_async_copy(du, rights[at]["du"].at[:, pl.ds(column, CHUNK)], du_sem)
+
     def mlp_chunk(at, step):
         slot = lax.rem(step, 2)
+
+        @pl.when(step > 0)
+        def _():
+            du_copy(at, step).wait()
+
         for copy in chunk_loads(at, step, slot):
             copy.wait()
         half = tokens // 2
@@ -1163,23 +1172,14 @@
             got = times_turned(low[strip], short[slot].reshape(CHUNK, features))
             got = (got * slope[slot, strip].astype(WIDE)).astype(LOW)
             du[strip] = got
-            got = times_turned(got, up)
-
-            @pl.when(step == 0)
-            def _():
-                acc[strip] = got
-
-            @pl.when(step > 0)
-            def _():
-                acc[strip] = acc[strip] + got
+            acc[strip] += times_turned(got, up)
 
         @pl.when(step + 2 < steps)
         def _():
             for copy in chunk_loads(at, step + 2, slot):
                 copy.start()
 
-        column = pl.multiple_of(step * CHUNK, CHUNK)
-        wait_out(du, rights[at]["du"].at[:, pl.ds(column, CHUNK)])
+        du_copy(at, step).start()
 
     def prob_load(at, group):
         span = tokens // kept[at]["prob"].shape[0]
@@ -1194,6 +1194,7 @@
         prob_load(at, 0).start()
         if at == 0:
             load_in("other", at).start()
+        du_copy(at, 0).wait()
         load_in("branch", at).wait()
         load_in("x1", at).wait()
         gate, scaled = mod_ref[at, 2:3], 1.0 + mod_ref[at, 4:5]
@@ -1578,11 +1579,11 @@
         def _():
             @pl.when(inner)
             def _():
-                wide[...] = final[was2].astype(WIDE)
+                wide[...] = final[was2]
 
             @pl.when(outer)
             def _():
-                wide[...] = back_in[lax.rem(t + 3, BACK)].astype(WIDE)
+                wide[...] = back_in[lax.rem(t + 3, BACK)]
 
             store(t - 6)
 
@@ -1590,39 +1591,34 @@
         def _():
             wait_loads(now2)
             slot3 = lax.rem(t, SLOTS)
-            third = width // 3
-
-            def product(which, j):
-                at = pl.ds(pl.multiple_of(j * third, third), third)
+            parts = (slice(0, 512), slice(512, width))
+
+            def product(which, at):
                 block = left[now2, :, which]
                 four, _, depth = block.shape
                 got = times(block.reshape(four * rows, depth), right[now2, :, at]).astype(LOW)
-                return at, got.reshape(four, rows, third)
-
-            def away_columns(j, carry):
-                at, got = product(1 - core, j)
-                away[:, :, at] = got
-                return carry
-
-            lax.fori_loop(0, 3, away_columns, 0)
+                return got.reshape(four, rows, -1)
+
+            for at in parts:
+                away[:, :, at] = product(1 - core, at)
             pair_copy(t).start()
-
-            def kept_columns(j, carry):
-                at, got = product(core, j)
+            for at in parts:
+                got = product(core, at)
                 part[slot3, 0, :, :, at] = got[:2]
                 part[slot3, 1, :, :, at] = got[2:]
-                return carry
-
-            lax.fori_loop(0, 3, kept_columns, 0)
+
+        backward_step(t)
+
+        @pl.when(t < total)
+        def _():
             pair_copy(t).wait()
+            slot3 = lax.rem(t, SLOTS)
 
             def add(j, carry):
                 part[slot3, j // 2, j % 2] = part[slot3, j // 2, j % 2] + pair_in[now2, j]
                 return carry
 
             lax.fori_loop(0, 4, add, 0)
-
-        backward_step(t)
 
         @pl.when(stage(1))
         def _():
@@ -1687,7 +1683,7 @@
             total += count
     dims = (rows, features, edge, tokens, total, spans)
     any_ = pl.BlockSpec(memory_space=pl.ANY)
-    outs = [struct(shape, WIDE) for shape in out_shapes] * 2
+    outs = [struct(shape, LOW) for shape in out_shapes] * 2
     outs += [
         struct((tokens, 3 * features), LOW), struct((tokens, features), LOW),
         struct((tokens, wide), LOW), struct((tokens, features), LOW),
@@ -1718,7 +1714,7 @@
         vm((SLOTS, rows, features), LOW),
         vm((2, rows, features), LOW),
         vm((BACK, rows, features), LOW),
-        vm((rows, features), WIDE),
+        vm((rows, features), LOW),
         vm((2, 8, rows, features), LOW),
         vm((2, 4, CHUNK // 4, features), LOW),
         vm((tokens, features), WIDE),
@@ -1753,6 +1749,7 @@
         dma((7,)),
         dma(()),
         dma(()),
+        dma(()),
         dma((2, 4)),
         *move_scratch(),
         *move_scratch(),
@@ -1771,7 +1768,8 @@
         *weights[0], *weights[1], *[each[name] for each in kept for name in KEPT],
         g, other, y, *xs, mods,
     )
-    return got[:4], got[4:8], got[16], got[17], got[18]
+    grads = [grad.astype(WIDE) for grad in got[:8]]
+    return grads[:4], grads[4:], got[16], got[17], got[18]
 
 
 def by_device(left, features):

time: 683 us -> 637 us (0.933)
  Pallas kernels: 636 us -> 595 us
  local copies, waits for them, and re-layouts: 19.6 us -> 3.64 us
  other arithmetic: 6.51 us -> 18 us
    pallas_call x1, Pallas kernels: 373 us -> 349 us  [backward(): pl.pallas_call(functools.partial(backward_kernel, dims), out_shape=outs,...]
    pallas_call x1, Pallas kernels: 263 us -> 246 us  [forward(): pl.pallas_call(functools.partial(forward_kernel, shapes), out_shape=outs,...]
    unnamed x40 -> x32, local copies, waits for them, and re-layouts: 18.6 us -> 2.67 us
    convert_element_type x0 -> x8, other arithmetic: none -> 11.5 us  [backward(): grads = [grad.astype(WIDE) for grad in got[:8]]]
where the time goes in v6:
time: 637 us; the launch traced here: 627 us
  Pallas kernels  595 us (93%)
  other arithmetic  18 us (3%)
  matrix products  9.31 us (1%)
    pallas_call x1, Pallas kernels, backward(): pl.pallas_call(functools.partial(backward_kernel, dims), out_shape=outs,...  349 us
    pallas_call x1, Pallas kernels, forward(): pl.pallas_call(functools.partial(forward_kernel, shapes), out_shape=outs,...  246 us

profile of v6, /device:TPU:0, one launch (start us, length us, event | category | flops | bytes accessed | tf_op | source)
XLA Modules:
  0.0 626.8 jit_solution(6324513091019133691)
XLA Ops:
  0.6 0.0 copy-start.14
  0.7 0.0 copy-start
  0.7 2.2 fusion.11
  2.8 0.0 copy-done.14
  2.8 0.0 copy-done
  2.8 0.5 fusion.9
  3.3 0.8 maximum_reduce_fusion
  4.1 2.8 convert_bitcast_fusion.refs_10_
  6.9 0.6 reduce.1
  7.5 245.5 %forward.1 = (bf16[8,144,3456]{2,1,0:T(8,128)(2,1)}, bf16[8,144,1152]{2,1,0:T(8,128)(2,1)}, bf16[8,144,4608]{2,1,0:T(8,128)(2,1)}, bf16[8,576,1152]{2,1,0:T(8,12...) custom-call(bf16[144,3456]{1,0:T(8,128)(2,1)} %refs_0_.1, ...), custom_call_target="tpu_custom_call" | custom-call | flops 32614907904 | bytes 254803968 | tf_op jit(solution)/shard_map/forward/pallas_call | solution.py:1012
  253.0 0.0 copy-start.13
  253.0 349.1 %backward.1 = (bf16[144,3456]{1,0:T(8,128)(2,1)}, bf16[144,1152]{1,0:T(8,128)(2,1)}, bf16[144,4608]{1,0:T(8,128)(2,1)}, bf16[576,1152]{1,0:T(8,128)(2,1)}, bf16[...) custom-call(bf16[8,144,3456]{2,1,0:T(8,128)(2,1)} %get-tuple-element, ...), custom_call_target="tpu_custom_call" | custom-call | flops 65229815808 | bytes 127401984 | tf_op jit(solution)/shard_map/backward/pallas_call | solution.py:1758
  602.2 1.0 reshape.118
  603.2 0.0 copy-done.13
  603.2 2.8 fusion
  606.0 0.0 copy-start.1
  606.0 2.7 fusion.2
  608.7 0.0 copy-done.1
  608.7 0.0 copy-start.2
  608.7 0.0 copy-start.7
  608.7 0.6 fusion.4
  609.3 0.9 copy-done.2
  610.3 0.6 fusion.5
  610.9 0.7 fusion.8
  611.6 0.0 copy-done.7
  611.6 0.0 copy-start.6
  611.6 1.8 convert_element_type.42
  613.4 0.0 copy-done.6
  613.4 0.0 copy-start.5
  613.4 1.7 convert_element_type.43
  615.1 0.1 copy-done.5
  615.2 0.0 copy-start.4
  615.2 1.8 convert_element_type.46
  616.9 0.0 copy-done.4
  616.9 1.7 convert_element_type.47
  618.6 0.0 copy-start.10
  618.6 0.0 copy-done.8
  618.6 1.6 bitcast_convert_fusion
  620.2 0.0 copy-done.10
  620.2 1.4 convert_element_type.40
  621.6 0.2 copy-done.9
  621.8 1.4 convert_element_type.44
  623.2 0.0 copy-done.12
  623.2 0.9 convert_element_type.41
  624.1 0.0 copy-done.11
  624.1 0.9 convert_element_type.45
  625.0 0.0 copy-done.3
  625.0 1.4 copy.30
  (7 shorter events, 0.0 us)
Async XLA Ops:
  0.6 2.2 copy-start.14
  0.7 2.2 copy-start
  253.0 350.2 %copy-start.13 = (f32[4,9,128]{2,1,0:T(8,128)S(1)}, f32[4,9,128]{2,1,0:T(8,128)}, u32[]{:S(2)}) copy-start(f32[4,9,128]{2,1,0:T(8,128)} %get-tuple-element.94) | copy-start | bytes 55300
  606.0 2.8 copy-start.1
  608.7 1.6 copy-start.2
  608.7 2.9 copy-start.7
  611.6 1.8 copy-start.6
  613.4 1.8 copy-start.5
  615.2 1.8 copy-start.4
  616.9 1.7 copy-start.8
  618.6 1.6 copy-start.10
  620.2 1.6 copy-start.9
  621.6 1.6 copy-start.12
  621.8 2.3 copy-start.11
  621.8 3.2 copy-start.3

commit v7 on v6

--- a/solution.py
+++ b/solution.py
@@ -1493,7 +1493,7 @@
         )
 
     def first_copies(t):
-        slot, block = lax.rem(t, SLOTS), lax.rem(t - 1, SLOTS)
+        slot, block = lax.rem(t, BACK), lax.rem(t - 1, SLOTS)
         return (
             to_seq(part.at[block, :, 1 - x, :, pl.ds(0, edge)], first_in_a.at[slot], 0, slot, 2),
             to_seq(
@@ -1537,22 +1537,18 @@
 
         now2, was2 = lax.rem(t, 2), lax.rem(t + 1, 2)
         was3 = lax.rem(t + 2, SLOTS)
+        was4 = lax.rem(t + 3, BACK)
 
         @pl.when(t + 1 < total)
         def _():
             loads(t + 1, was2)
-
-        @pl.when(stage(1))
-        def _():
-            for copy in first_copies(t):
-                copy.start()
 
         @pl.when(stage(2))
         def _():
             block = lax.rem(t + 1, SLOTS)
             for at in range(2):
-                mid_a[now2, at] = part[block, at, x, :, :edge] + first_in_a[was3, at]
-                mid_b[now2, at] = part[block, y, at, :, edge:] + first_in_b[was3, at]
+                mid_a[now2, at] = part[block, at, x, :, :edge] + first_in_a[was4, at]
+                mid_b[now2, at] = part[block, y, at, :, edge:] + first_in_b[was4, at]
             for copy in second_copies(t):
                 copy.start()
 
@@ -1619,6 +1615,8 @@
                 return carry
 
             lax.fori_loop(0, 4, add, 0)
+            for copy in first_copies(t + 1):
+                copy.start()
 
         @pl.when(stage(1))
         def _():
@@ -1702,8 +1700,8 @@
         vm((4, rows, features), LOW),
         vm((2, 4, rows, features), LOW),
         vm((SLOTS, 2, 2, rows, features), LOW),
-        vm((SLOTS, 2, rows, edge), LOW),
-        vm((SLOTS, 2, rows, rest), LOW),
+        vm((BACK, 2, rows, edge), LOW),
+        vm((BACK, 2, rows, rest), LOW),
         vm((2, 2, rows, edge), LOW),
         vm((2, 2, rows, rest), LOW),
         vm((SLOTS, rows, edge), LOW),
@@ -1738,7 +1736,7 @@
         vm((8, 16, features), LOW),
         dma((2, 2)),
         dma((2, 2)),
-        dma((2, 4, SLOTS)),
+        dma((2, 4, BACK)),
         dma((2, 2, SLOTS)),
         dma((2, BACK)),
         dma(()),
@@ -1801,6 +1799,13 @@
     )
 
 
+def outer_sum(left, right):
+    total = 0.0
+    for row in range(left.shape[0]):
+        total = total + left[row, :, None].astype(jnp.float32) * right[row].astype(jnp.float32)
+    return total
+
+
 def per_device(
     frames_in,
     conditioning,
@@ -1868,12 +1873,8 @@
         mod_total = lax.psum(mod_grads, "seq").astype(jnp.bfloat16)
         every_mod = lax.all_gather(mod_total, "rep", axis=0, tiled=True)
     low_one, low_two = mod_total[:, :mod_width], mod_total[:, mod_width:]
-    mod_weight_one = jnp.einsum(
-        "cd,ce->de", every_silu, every_mod[:, :mod_width], preferred_element_type=jnp.float32
-    )
-    mod_weight_two = jnp.einsum(
-        "cd,ce->de", every_silu, every_mod[:, mod_width:], preferred_element_type=jnp.float32
-    )
+    mod_weight_one = outer_sum(every_silu, every_mod[:, :mod_width])
+    mod_weight_two = outer_sum(every_silu, every_mod[:, mod_width:])
     silu_grad = jnp.einsum("ce,de->cd", low_one, mod_first, preferred_element_type=jnp.float32)
     silu_grad = silu_grad + jnp.einsum(
         "ce,de->cd", low_two, mod_second, preferred_element_type=jnp.float32

time: 637 us -> 634 us (level)
  no operation moved by 1% of the time
where the time goes in v7:
time: 634 us; the launch traced here: 625 us
  Pallas kernels  591 us (93%)
  other arithmetic  22.3 us (4%)
  matrix products  7.02 us (1%)
    pallas_call x1, Pallas kernels, backward(): pl.pallas_call(functools.partial(backward_kernel, dims), out_shape=outs,...  346 us
    pallas_call x1, Pallas kernels, forward(): pl.pallas_call(functools.partial(forward_kernel, shapes), out_shape=outs,...  246 us

profile of v7, /device:TPU:0, one launch (start us, length us, event | category | flops | bytes accessed | tf_op | source)
XLA Modules:
  0.0 624.6 jit_solution(3030520885362535118)
XLA Ops:
  0.6 0.0 copy-start.1
  0.7 2.2 fusion.13
  2.8 0.0 copy-start.13
  2.8 2.0 fusion.15
  4.9 0.8 maximum_reduce_fusion
  5.6 0.0 copy-done.1
  5.6 1.1 convert_bitcast_fusion.refs_10_
  6.8 0.0 copy-done.13
  6.8 0.6 reduce.1
  7.4 245.5 %forward.1 = (bf16[8,144,3456]{2,1,0:T(8,128)(2,1)}, bf16[8,144,1152]{2,1,0:T(8,128)(2,1)}, bf16[8,144,4608]{2,1,0:T(8,128)(2,1)}, bf16[8,576,1152]{2,1,0:T(8,12...) custom-call(bf16[144,3456]{1,0:T(8,128)(2,1)} %refs_0_.1, ...), custom_call_target="tpu_custom_call" | custom-call | flops 32614907904 | bytes 254803968 | tf_op jit(solution)/shard_map/forward/pallas_call | solution.py:1012
  252.9 0.0 copy-start.12
  252.9 345.8 %backward.1 = (bf16[144,3456]{1,0:T(8,128)(2,1)}, bf16[144,1152]{1,0:T(8,128)(2,1)}, bf16[144,4608]{1,0:T(8,128)(2,1)}, bf16[576,1152]{1,0:T(8,128)(2,1)}, bf16[...) custom-call(bf16[8,144,3456]{2,1,0:T(8,128)(2,1)} %get-tuple-element, ...), custom_call_target="tpu_custom_call" | custom-call | flops 65229815808 | bytes 127401984 | tf_op jit(solution)/shard_map/backward/pallas_call | solution.py:1756
  598.8 1.0 reshape.154
  599.8 0.6 fusion.3
  600.4 0.0 copy-done.12
  600.4 0.1 fusion.10
  600.5 0.0 copy-start
  600.5 5.3 multiply_add_fusion
  605.8 0.0 copy-start.6
  605.9 0.0 copy-done
  605.9 0.6 fusion.8
  606.5 2.2 fusion.9
  608.7 0.0 copy-start.5
  608.7 0.7 fusion.12
  609.4 0.0 copy-done.6
  609.4 1.8 convert_element_type.114
  611.2 0.0 copy-start.4
  611.2 0.0 copy-done.5
  611.2 1.7 convert_element_type.115
  612.9 0.0 copy-start.3
  612.9 0.1 copy-done.4
  613.0 1.8 convert_element_type.118
  614.8 0.0 copy-start.7
  614.8 0.0 copy-done.3
  614.8 1.7 convert_element_type.119
  616.5 0.0 copy-start.9
  616.5 0.0 copy-done.7
  616.5 1.6 bitcast_convert_fusion
  618.0 0.0 copy-done.9
  618.0 1.4 convert_element_type.112
  619.4 0.1 copy-done.8
  619.6 1.4 convert_element_type.116
  621.0 0.0 copy-done.11
  621.0 0.9 convert_element_type.113
  621.9 0.0 copy-done.10
  621.9 0.9 convert_element_type.117
  622.8 0.0 copy-done.2
  622.8 1.4 copy.30
  (7 shorter events, 0.0 us)
Async XLA Ops:
  0.6 5.0 copy-start.1
  2.8 4.0 copy-start.13
  252.9 347.4 %copy-start.12 = (f32[4,9,128]{2,1,0:T(8,128)S(1)}, f32[4,9,128]{2,1,0:T(8,128)}, u32[]{:S(2)}) copy-start(f32[4,9,128]{2,1,0:T(8,128)} %get-tuple-element.94) | copy-start | bytes 55300
  600.5 5.4 copy-start
  605.8 3.6 copy-start.6
  608.7 2.5 copy-start.5
  611.2 1.8 copy-start.4
  612.9 1.9 copy-start.3
  614.8 1.7 copy-start.7
  616.5 1.6 copy-start.9
  618.0 1.6 copy-start.8
  618.0 3.0 copy-start.11
  619.4 2.4 copy-start.10
  619.6 3.2 copy-start.2

commit v8 on v7

--- a/solution.py
+++ b/solution.py
@@ -1299,8 +1299,8 @@
                 qkv[pair, :, lanes] = qkv[pair, :, lanes] + take[pair]
         wait_out(qkv, rights[at]["qkv"].reshape(*qkv.shape))
 
-    def qkv_chunks(at):
-        for j in range(3):
+    def qkv_chunks(at, blocks):
+        for j in blocks:
             slot = 1 - j % 2
             tall_load(qkv_block(at, j), slot).wait()
             got = times_turned(
@@ -1355,16 +1355,14 @@
         def _():
             attend_group(1, t - 5)
 
-        @at_turn(6)
+        @at_turn(7)
         def _():
             attend_finish(1)
-
-        @at_turn(7)
-        def _():
-            qkv_chunks(1)
+            qkv_chunks(1, (0, 1))
 
         @at_turn(8)
         def _():
+            qkv_chunks(1, (2,))
             qkv_finish(1)
 
         @at_turn(10)
@@ -1392,10 +1390,11 @@
 
         @at_turn(20)
         def _():
-            qkv_chunks(0)
+            qkv_chunks(0, (0, 1))
 
         @at_turn(21)
         def _():
+            qkv_chunks(0, (2,))
             qkv_finish(0)
             mod_low[...] = jnp.zeros_like(mod_low)
             for at in range(2):

time: 634 us -> 634 us (level)
  no operation moved by 1% of the time
where the time goes in v8:
time: 634 us; the launch traced here: 624 us
  Pallas kernels  591 us (93%)
  other arithmetic  22.3 us (4%)
  matrix products  7.02 us (1%)
    pallas_call x1, Pallas kernels, backward(): pl.pallas_call(functools.partial(backward_kernel, dims), out_shape=outs,...  345 us
    pallas_call x1, Pallas kernels, forward(): pl.pallas_call(functools.partial(forward_kernel, shapes), out_shape=outs,...  246 us

profile of v8, /device:TPU:0, one launch (start us, length us, event | category | flops | bytes accessed | tf_op | source)
XLA Modules:
  0.0 624.0 jit_solution(15676173359834949060)
XLA Ops:
  0.6 0.0 copy-start.1
  0.7 2.2 fusion.13
  2.8 0.0 copy-start.13
  2.8 2.0 fusion.15
  4.9 0.8 maximum_reduce_fusion
  5.6 0.0 copy-done.1
  5.6 1.1 convert_bitcast_fusion.refs_10_
  6.8 0.0 copy-done.13
  6.8 0.6 reduce.1
  7.4 245.5 %forward.1 = (bf16[8,144,3456]{2,1,0:T(8,128)(2,1)}, bf16[8,144,1152]{2,1,0:T(8,128)(2,1)}, bf16[8,144,4608]{2,1,0:T(8,128)(2,1)}, bf16[8,576,1152]{2,1,0:T(8,12...) custom-call(bf16[144,3456]{1,0:T(8,128)(2,1)} %refs_0_.1, ...), custom_call_target="tpu_custom_call" | custom-call | flops 32614907904 | bytes 254803968 | tf_op jit(solution)/shard_map/forward/pallas_call | solution.py:1012
  252.9 0.0 copy-start.12
  252.9 345.3 %backward.1 = (bf16[144,3456]{1,0:T(8,128)(2,1)}, bf16[144,1152]{1,0:T(8,128)(2,1)}, bf16[144,4608]{1,0:T(8,128)(2,1)}, bf16[576,1152]{1,0:T(8,128)(2,1)}, bf16[...) custom-call(bf16[8,144,3456]{2,1,0:T(8,128)(2,1)} %get-tuple-element, ...), custom_call_target="tpu_custom_call" | custom-call | flops 65229815808 | bytes 127401984 | tf_op jit(solution)/shard_map/backward/pallas_call | solution.py:1755
  598.2 1.0 reshape.154
  599.2 0.6 fusion.3
  599.8 0.0 copy-done.12
  599.8 0.1 fusion.10
  599.9 0.0 copy-start
  600.0 5.3 multiply_add_fusion
  605.3 0.0 copy-start.6
  605.3 0.0 copy-done
  605.3 0.6 fusion.8
  605.9 2.2 fusion.9
  608.1 0.0 copy-start.5
  608.2 0.7 fusion.12
  608.9 0.0 copy-done.6
  608.9 1.8 convert_element_type.114
  610.6 0.0 copy-start.4
  610.6 0.0 copy-done.5
  610.6 1.7 convert_element_type.115
  612.3 0.0 copy-start.3
  612.3 0.1 copy-done.4
  612.4 1.8 convert_element_type.118
  614.2 0.0 copy-start.7
  614.2 0.0 copy-done.3
  614.2 1.7 convert_element_type.119
  615.9 0.0 copy-start.9
  615.9 0.0 copy-done.7
  615.9 1.6 bitcast_convert_fusion
  617.5 0.0 copy-done.9
  617.5 1.4 convert_element_type.112
  618.9 0.1 copy-done.8
  619.0 1.4 convert_element_type.116
  620.4 0.0 copy-done.11
  620.4 0.9 convert_element_type.113
  621.3 0.0 copy-done.10
  621.3 0.9 convert_element_type.117
  622.2 0.0 copy-done.2
  622.2 1.4 copy.30
  (7 shorter events, 0.0 us)
Async XLA Ops:
  0.6 5.0 copy-start.1
  2.8 4.0 copy-start.13
  252.9 346.9 %copy-start.12 = (f32[4,9,128]{2,1,0:T(8,128)S(1)}, f32[4,9,128]{2,1,0:T(8,128)}, u32[]{:S(2)}) copy-start(f32[4,9,128]{2,1,0:T(8,128)} %get-tuple-element.94) | copy-start | bytes 55300
  599.9 5.4 copy-start
  605.3 3.6 copy-start.6
  608.1 2.5 copy-start.5
  610.6 1.8 copy-start.4
  612.3 1.9 copy-start.3
  614.2 1.7 copy-start.7
  615.9 1.6 copy-start.9
  617.5 1.6 copy-start.8
  617.5 3.0 copy-start.11
  618.9 2.4 copy-start.10
  619.0 3.2 copy-start.2
